TPU v7x, 32 devices: a whole 2x2x4 slice. The times are simulated.
32 devices in a mesh: fsdp: 4 (over y, x), ctx: 4 (over z), tp: 2 (over core).
Axes of the slice: x: 2, y: 2, z: 4, core: 2. Of those that a mesh axis runs over, the one named last changes fastest.
Arguments:
- hidden_in: bfloat16 [4, 512, 1024], P('fsdp', 'ctx'), may hold values from -6 to 6
- out_grad: bfloat16 [4, 512, 1024], P('fsdp', 'ctx'), may hold values from -6 to 6
- attention_gain: bfloat16 [1024], P(('fsdp', 'ctx')), may hold values from 0.5 to 1.5
- query_weight: bfloat16 [1024, 1024], P(('fsdp', 'ctx'), 'tp'), may hold values from -1 to 1
- key_weight: bfloat16 [1024, 512], P(('fsdp', 'ctx'), 'tp'), may hold values from -1 to 1
- value_weight: bfloat16 [1024, 512], P(('fsdp', 'ctx'), 'tp'), may hold values from -0.1875 to 0.1875
- output_weight: bfloat16 [1024, 1024], P(('fsdp', 'ctx'), 'tp'), may hold values from -0.75 to 0.75
- expert_gain: bfloat16 [1024], P(('fsdp', 'ctx')), may hold values from 0.5 to 1.5
- router_weight: bfloat16 [1024, 16], P(('fsdp', 'ctx')), may hold values from -1 to 1
- gate_weight: bfloat16 [16, 1024, 512], P(None, ('fsdp', 'ctx'), 'tp'), may hold values from -0.1875 to 0.1875
- up_weight: bfloat16 [16, 1024, 512], P(None, ('fsdp', 'ctx'), 'tp'), may hold values from -0.1875 to 0.1875
- down_weight: bfloat16 [16, 1024, 512], P(None, ('fsdp', 'ctx'), 'tp'), may hold values from -0.25 to 0.25
- doc_lengths: int32 [4, 8], P('fsdp'), may hold values from 1 to 256, 512 in all within a row
- expert_choice: int32 [4, 512, 8], P('fsdp', 'ctx'), may hold values from 0 to 15, all different within a row; in each aligned block of 128 rows (0 to 127, 128 to 255, ..., all dimensions but the last counted through in order) at most 96 rows name the same one
Outputs:
- block_out: bfloat16 [4, 512, 1024], P('fsdp', 'ctx')
- input_grad: float32 [4, 512, 1024], P('fsdp', 'ctx')
- attention_gain_grad: float32 [1024], P(('fsdp', 'ctx'))
- query_weight_grad: float32 [1024, 1024], P(('fsdp', 'ctx'), 'tp')
- key_weight_grad: float32 [1024, 512], P(('fsdp', 'ctx'), 'tp')
- value_weight_grad: float32 [1024, 512], P(('fsdp', 'ctx'), 'tp')
- output_weight_grad: float32 [1024, 1024], P(('fsdp', 'ctx'), 'tp')
- expert_gain_grad: float32 [1024], P(('fsdp', 'ctx'))
- router_weight_grad: float32 [1024, 16], P(('fsdp', 'ctx'))
- gate_weight_grad: float32 [16, 1024, 512], P(None, ('fsdp', 'ctx'), 'tp')
- up_weight_grad: float32 [16, 1024, 512], P(None, ('fsdp', 'ctx'), 'tp')
- down_weight_grad: float32 [16, 1024, 512], P(None, ('fsdp', 'ctx'), 'tp')
Inputs may be any that keep to these rules, and one draw needn't show every extreme that they name: `doc_lengths`: each row's lengths sum to 512; in every row the longest document has exactly 256 positions. `expert_choice`: A token names 8 different experts. Among the tokens of one block of 128 positions (one device's tokens) no expert is named more than 96 times, and in every draw some expert is named exactly 96 times in some block.
All inputs are finite; a program needn't handle non-finite values.
Results may differ from a plain program's by a relative error of at most 0.04.
Values may be sent and summed in bfloat16 or wider, within the bound.
A program may use at most 192 MiB of HBM per device.

v0:
```python
import jax
import jax.numpy as jnp
from jax import lax
from jax.sharding import PartitionSpec as P

HD = 64


epsilon = 1e-05
rope_base = 10000.0
masked_score = -1e30
highest = lax.Precision.HIGHEST


def doc_layout(lengths, positions):
    ends = jnp.cumsum(lengths)
    after = (positions[:, None] >= ends[None, :]).astype(jnp.int32)
    segment = jnp.sum(after, axis=1)
    offset = positions - jnp.sum(after * lengths[None, :], axis=1)
    return (segment, offset)


def rope_tables(offset):
    halfway = HD // 2
    frequency = rope_base ** (-jnp.arange(halfway, dtype=jnp.float32) / halfway)
    angle = offset.astype(jnp.float32)[:, None] * frequency[None, :]
    return (jnp.cos(angle), jnp.sin(angle))


def rotate(vectors, cosine, sine):
    halfway = vectors.shape[-1] // 2
    former = vectors[..., :halfway]
    latter = vectors[..., halfway:]
    cosine = cosine[:, None, :]
    sine = sine[:, None, :]
    return jnp.concatenate(
        [former * cosine - latter * sine, latter * cosine + former * sine], axis=-1
    )


def rotate_back(grads, cosine, sine):
    halfway = grads.shape[-1] // 2
    former = grads[..., :halfway]
    latter = grads[..., halfway:]
    cosine = cosine[:, None, :]
    sine = sine[:, None, :]
    return jnp.concatenate(
        [former * cosine + latter * sine, latter * cosine - former * sine], axis=-1
    )


def norm_forward(values, gain):
    inverse = lax.rsqrt(jnp.mean(values * values, axis=-1, keepdims=True) + epsilon)
    return (values * inverse * gain.astype(jnp.float32), inverse)


def norm_backward(values, inverse, gain, grad_normed):
    scaled = grad_normed * gain.astype(jnp.float32)
    grad_values = inverse * scaled - values * inverse**3 * jnp.mean(
        scaled * values, axis=-1, keepdims=True
    )
    grad_gain = jnp.sum(grad_normed * values * inverse, axis=0)
    return (grad_values, grad_gain)


def dispatch(route, experts, capacity):
    flat = route.reshape(-1)
    onehot = (flat[:, None] == jnp.arange(experts, dtype=jnp.int32)[None, :]).astype(jnp.int32)
    rank = jnp.sum((jnp.cumsum(onehot, axis=0) - onehot) * onehot, axis=1)
    slot = flat * capacity + rank
    pairs = flat.shape[0]
    owner = (
        jnp.zeros((experts * capacity,), jnp.int32).at[slot].set(jnp.arange(pairs, dtype=jnp.int32))
    )
    filled = jnp.zeros((experts * capacity,), jnp.int32).at[slot].set(1) > 0
    return (slot, owner, filled)


def expert_math(slot_inputs, slot_grads, gate_full, up_full, down_full):
    gate_pre = jnp.einsum(
        "gsd,gdf->gsf", slot_inputs, gate_full, preferred_element_type=jnp.float32
    )
    up_pre = jnp.einsum("gsd,gdf->gsf", slot_inputs, up_full, preferred_element_type=jnp.float32)
    sigmoid = jax.nn.sigmoid(gate_pre)
    activated = (gate_pre * sigmoid * up_pre).astype(jnp.bfloat16)
    expert_out = jnp.einsum(
        "gsf,gdf->gsd", activated, down_full, preferred_element_type=jnp.float32
    )
    act_grad = jnp.einsum("gsd,gdf->gsf", slot_grads, down_full, preferred_element_type=jnp.float32)
    gate_pre_grad = (act_grad * up_pre * sigmoid * (1.0 + gate_pre * (1.0 - sigmoid))).astype(
        jnp.bfloat16
    )
    up_pre_grad = (act_grad * gate_pre * sigmoid).astype(jnp.bfloat16)
    down_term = jnp.einsum(
        "gsd,gsf->gdf", slot_grads, activated, preferred_element_type=jnp.float32
    )
    gate_term = jnp.einsum(
        "gsd,gsf->gdf", slot_inputs, gate_pre_grad, preferred_element_type=jnp.float32
    )
    up_term = jnp.einsum(
        "gsd,gsf->gdf", slot_inputs, up_pre_grad, preferred_element_type=jnp.float32
    )
    slot_back = jnp.einsum(
        "gsf,gdf->gsd", gate_pre_grad, gate_full, preferred_element_type=jnp.float32
    ) + jnp.einsum("gsf,gdf->gsd", up_pre_grad, up_full, preferred_element_type=jnp.float32)
    return (expert_out, slot_back, gate_term, up_term, down_term)


def local(
    hidden_in,
    out_grad,
    attention_gain,
    query_weight,
    key_weight,
    value_weight,
    output_weight,
    expert_gain,
    router_weight,
    gate_weight,
    up_weight,
    down_weight,
    doc_lengths,
    expert_choice,
):
    block = hidden_in.shape[1]
    experts = gate_weight.shape[0]
    capacity = block * 3 // 4
    chosen_count = expert_choice.shape[2]
    context_count = lax.axis_size("ctx")
    scale = HD ** (-0.5)
    position = lax.axis_index("ctx") * block + jnp.arange(block, dtype=jnp.int32)
    lengths = doc_lengths[0]
    segment, offset = doc_layout(lengths, position)
    cosine, sine = rope_tables(offset)
    gain_one, query_full, key_full, value_full, output_full, gain_two, router_full = (
        lax.all_gather(attention_gain, ("fsdp", "ctx"), axis=0, tiled=True),
        lax.all_gather(query_weight, ("fsdp", "ctx"), axis=0, tiled=True),
        lax.all_gather(key_weight, ("fsdp", "ctx"), axis=0, tiled=True),
        lax.all_gather(value_weight, ("fsdp", "ctx"), axis=0, tiled=True),
        lax.all_gather(output_weight, ("fsdp", "ctx"), axis=0, tiled=True),
        lax.all_gather(expert_gain, ("fsdp", "ctx"), axis=0, tiled=True),
        lax.all_gather(router_weight, ("fsdp", "ctx"), axis=0, tiled=True),
    )
    inputs = hidden_in[0].astype(jnp.float32)
    normed_one, inverse_one = norm_forward(inputs, gain_one)
    normed_one = normed_one.astype(jnp.bfloat16)
    heads_local = query_full.shape[1] // HD
    groups_local = key_full.shape[1] // HD
    ratio = heads_local // groups_local
    query = rotate(
        jnp.dot(normed_one, query_full, preferred_element_type=jnp.float32).reshape(
            block, heads_local, HD
        ),
        cosine,
        sine,
    ).astype(jnp.bfloat16)
    keys = rotate(
        jnp.dot(normed_one, key_full, preferred_element_type=jnp.float32).reshape(
            block, groups_local, HD
        ),
        cosine,
        sine,
    ).astype(jnp.bfloat16)
    values = jnp.dot(normed_one, value_full, preferred_element_type=jnp.float32).astype(
        jnp.bfloat16
    )
    query_grouped = query.reshape(block, groups_local, ratio, HD)

    def allowed_mask(key_start, count):
        key_position = key_start + jnp.arange(count, dtype=jnp.int32)
        key_segment, unused = doc_layout(lengths, key_position)
        return (segment[:, None] == key_segment[None, :]) & (
            key_position[None, :] <= position[:, None]
        )

    def forward_update(state, key_block, value_block, allowed):
        peak, total, accum = state
        mask = allowed[:, None, None, :]
        scores = (
            jnp.einsum(
                "qgrd,kgd->qgrk", query_grouped, key_block, preferred_element_type=jnp.float32
            )
            * scale
        )
        scores = jnp.where(mask, scores, masked_score)
        new_peak = jnp.maximum(peak, jnp.max(scores, axis=3))
        weights = jnp.where(mask, jnp.exp(scores - new_peak[..., None]), 0.0)
        rescale = jnp.exp(peak - new_peak)
        total = total * rescale + jnp.sum(weights, axis=3)
        accum = accum * rescale[..., None] + jnp.einsum(
            "qgrk,kgd->qgrd", weights, value_block.astype(jnp.float32), precision=highest
        )
        return (new_peak, total, accum)

    travel = (keys.reshape(block, groups_local * HD), values)
    initial = (
        jnp.full((block, groups_local, ratio), masked_score, jnp.float32),
        jnp.zeros((block, groups_local, ratio), jnp.float32),
        jnp.zeros((block, groups_local, ratio, HD), jnp.float32),
    )
    state = initial
    key_piece = lax.all_gather(travel[0], "ctx", axis=0, tiled=True)
    value_piece = lax.all_gather(travel[1], "ctx", axis=0, tiled=True)
    pieces = key_piece.shape[0] // block
    key_blocks = key_piece.reshape(pieces, block, groups_local, HD)
    value_blocks = value_piece.reshape(pieces, block, groups_local, HD)
    starts = block * jnp.arange(pieces, dtype=jnp.int32)

    def visit(carry, item):
        key_block, value_block, key_start = item
        allowed = allowed_mask(key_start, block)
        return (forward_update(carry, key_block, value_block, allowed), None)

    state, unused = lax.scan(visit, state, (key_blocks, value_blocks, starts))
    peak, total, accum = state
    attended = (accum / total[..., None]).reshape(block, heads_local * HD).astype(jnp.bfloat16)
    log_total = peak + jnp.log(total)
    projected = lax.psum(jnp.dot(attended, output_full.T, preferred_element_type=jnp.float32), "tp")
    residual = inputs + projected
    normed_two, inverse_two = norm_forward(residual, gain_two)
    normed_two = normed_two.astype(jnp.bfloat16)
    route = expert_choice[0]
    logits = jnp.dot(normed_two, router_full, preferred_element_type=jnp.float32)
    gates = jax.nn.softmax(jnp.take_along_axis(logits, route, axis=1), axis=1)
    slot, owner, filled = dispatch(route, experts, capacity)
    token_of = owner // chosen_count
    grad_out = out_grad[0].astype(jnp.float32)
    slot_inputs = jnp.where(filled[:, None], normed_two[token_of], 0).reshape(experts, capacity, -1)
    slot_gate = jnp.where(filled, gates.reshape(-1)[owner], 0.0)
    slot_grads = (
        (grad_out[token_of] * slot_gate[:, None])
        .astype(jnp.bfloat16)
        .reshape(experts, capacity, -1)
    )
    gate_full, up_full, down_full = (
        lax.all_gather(gate_weight, ("fsdp", "ctx"), axis=1, tiled=True),
        lax.all_gather(up_weight, ("fsdp", "ctx"), axis=1, tiled=True),
        lax.all_gather(down_weight, ("fsdp", "ctx"), axis=1, tiled=True),
    )
    expert_out, slot_back, gate_term, up_term, down_term = expert_math(
        slot_inputs, slot_grads, gate_full, up_full, down_full
    )
    gate_share, up_share, down_share = (
        lax.psum_scatter(gate_term, ("fsdp", "ctx"), scatter_dimension=1, tiled=True),
        lax.psum_scatter(up_term, ("fsdp", "ctx"), scatter_dimension=1, tiled=True),
        lax.psum_scatter(down_term, ("fsdp", "ctx"), scatter_dimension=1, tiled=True),
    )
    pair_out = expert_out.reshape(experts * capacity, -1)[slot].reshape(block, chosen_count, -1)
    pair_back = slot_back.reshape(experts * capacity, -1)[slot].reshape(block, chosen_count, -1)
    mixed_part = jnp.sum(gates[..., None] * pair_out, axis=1)
    gate_dot_part = jnp.sum(pair_out * grad_out[:, None, :], axis=2)
    moe_part = jnp.sum(pair_back, axis=1)
    mixed, gate_dot, moe_input = (
        lax.psum(mixed_part.astype(jnp.bfloat16), "tp").astype(jnp.float32),
        lax.psum(gate_dot_part.astype(jnp.bfloat16), "tp").astype(jnp.float32),
        lax.psum(moe_part.astype(jnp.bfloat16), "tp").astype(jnp.float32),
    )
    block_out = (residual + mixed).astype(jnp.bfloat16)[None]
    chosen_grad = gates * (gate_dot - jnp.sum(gates * gate_dot, axis=1, keepdims=True))
    picked = (route[..., None] == jnp.arange(experts, dtype=jnp.int32)[None, None, :]).astype(
        jnp.float32
    )
    logit_grad = jnp.sum(picked * chosen_grad[..., None], axis=1)
    router_term = jnp.dot(normed_two.astype(jnp.float32).T, logit_grad, precision=highest)
    router_input = jnp.dot(logit_grad, router_full.astype(jnp.float32).T, precision=highest)
    grad_residual_norm, gain_two_term = norm_backward(
        residual, inverse_two, gain_two, moe_input + router_input
    )
    grad_residual = grad_out + grad_residual_norm
    residual_low = grad_residual.astype(jnp.bfloat16)
    attended_grad = jnp.dot(residual_low, output_full, preferred_element_type=jnp.float32).astype(
        jnp.bfloat16
    )
    output_term = jnp.dot(residual_low.T, attended, preferred_element_type=jnp.float32)
    delta = jnp.sum(
        (attended_grad.astype(jnp.float32) * attended.astype(jnp.float32)).reshape(
            block, groups_local, ratio, HD
        ),
        axis=3,
    )
    grad_grouped = attended_grad.reshape(block, groups_local, ratio, HD)
    back_keys, back_values = (
        lax.all_gather(travel[0], "ctx", axis=0, tiled=True),
        lax.all_gather(travel[1], "ctx", axis=0, tiled=True),
    )
    key_blocks = back_keys.reshape(context_count, block, groups_local, HD)
    value_blocks = back_values.reshape(context_count, block, groups_local, HD)
    starts = block * jnp.arange(context_count, dtype=jnp.int32)

    def backward_update(grad_query, key_block, value_block, allowed):
        mask = allowed[:, None, None, :]
        scores = (
            jnp.einsum(
                "qgrd,kgd->qgrk", query_grouped, key_block, preferred_element_type=jnp.float32
            )
            * scale
        )
        probs = jnp.where(mask, jnp.exp(scores - log_total[..., None]), 0.0)
        value_grad = jnp.einsum(
            "qgrk,qgrd->kgd",
            probs.astype(jnp.bfloat16),
            grad_grouped,
            preferred_element_type=jnp.float32,
        )
        prob_grad = jnp.einsum(
            "qgrd,kgd->qgrk", grad_grouped, value_block, preferred_element_type=jnp.float32
        )
        score_grad = (probs * (prob_grad - delta[..., None]) * scale).astype(jnp.bfloat16)
        grad_query = grad_query + jnp.einsum(
            "qgrk,kgd->qgrd", score_grad, key_block, preferred_element_type=jnp.float32
        )
        key_grad = jnp.einsum(
            "qgrk,qgrd->kgd", score_grad, query_grouped, preferred_element_type=jnp.float32
        )
        return (grad_query, key_grad.reshape(block, -1), value_grad.reshape(block, -1))

    def backward_visit(grad_query, item):
        key_block, value_block, key_start = item
        allowed = allowed_mask(key_start, block)
        grad_query, key_grad, value_grad = backward_update(
            grad_query, key_block, value_block, allowed
        )
        return (grad_query, (key_grad, value_grad))

    grad_query, (key_grads, value_grads) = lax.scan(
        backward_visit,
        jnp.zeros((block, groups_local, ratio, HD), jnp.float32),
        (key_blocks, value_blocks, starts),
    )
    own_key_grad, own_value_grad = (
        lax.psum_scatter(
            key_grads.reshape(context_count * block, -1).astype(jnp.bfloat16),
            "ctx",
            scatter_dimension=0,
            tiled=True,
        ).astype(jnp.float32),
        lax.psum_scatter(
            value_grads.reshape(context_count * block, -1).astype(jnp.bfloat16),
            "ctx",
            scatter_dimension=0,
            tiled=True,
        ).astype(jnp.float32),
    )
    query_grad = (
        rotate_back(grad_query.reshape(block, heads_local, HD), cosine, sine)
        .reshape(block, -1)
        .astype(jnp.bfloat16)
    )
    key_grad = (
        rotate_back(own_key_grad.reshape(block, groups_local, HD), cosine, sine)
        .reshape(block, -1)
        .astype(jnp.bfloat16)
    )
    value_grad = own_value_grad.astype(jnp.bfloat16)
    input_part = jnp.dot(query_grad, query_full.T, preferred_element_type=jnp.float32)
    input_part = input_part + jnp.dot(key_grad, key_full.T, preferred_element_type=jnp.float32)
    input_part = input_part + jnp.dot(value_grad, value_full.T, preferred_element_type=jnp.float32)
    normed_one_grad = lax.psum(input_part.astype(jnp.bfloat16), "tp").astype(jnp.float32)
    grad_input_norm, gain_one_term = norm_backward(inputs, inverse_one, gain_one, normed_one_grad)
    input_grad = (grad_residual + grad_input_norm)[None]
    query_term = jnp.dot(normed_one.T, query_grad, preferred_element_type=jnp.float32)
    key_term = jnp.dot(normed_one.T, key_grad, preferred_element_type=jnp.float32)
    value_term = jnp.dot(normed_one.T, value_grad, preferred_element_type=jnp.float32)
    (
        gain_one_share,
        query_share,
        key_share,
        value_share,
        output_share,
        gain_two_share,
        router_share,
    ) = (
        lax.psum_scatter(gain_one_term, ("fsdp", "ctx"), scatter_dimension=0, tiled=True),
        lax.psum_scatter(query_term, ("fsdp", "ctx"), scatter_dimension=0, tiled=True),
        lax.psum_scatter(key_term, ("fsdp", "ctx"), scatter_dimension=0, tiled=True),
        lax.psum_scatter(value_term, ("fsdp", "ctx"), scatter_dimension=0, tiled=True),
        lax.psum_scatter(output_term, ("fsdp", "ctx"), scatter_dimension=0, tiled=True),
        lax.psum_scatter(gain_two_term, ("fsdp", "ctx"), scatter_dimension=0, tiled=True),
        lax.psum_scatter(router_term, ("fsdp", "ctx"), scatter_dimension=0, tiled=True),
    )
    return (
        block_out,
        input_grad,
        gain_one_share,
        query_share,
        key_share,
        value_share,
        output_share,
        gain_two_share,
        router_share,
        gate_share,
        up_share,
        down_share,
    )


def solution(mesh):
    in_specs = (
        P("fsdp", "ctx", None),
        P("fsdp", "ctx", None),
        P(("fsdp", "ctx")),
        P(("fsdp", "ctx"), "tp"),
        P(("fsdp", "ctx"), "tp"),
        P(("fsdp", "ctx"), "tp"),
        P(("fsdp", "ctx"), "tp"),
        P(("fsdp", "ctx")),
        P(("fsdp", "ctx"), None),
        P(None, ("fsdp", "ctx"), "tp"),
        P(None, ("fsdp", "ctx"), "tp"),
        P(None, ("fsdp", "ctx"), "tp"),
        P("fsdp", None),
        P("fsdp", "ctx", None),
    )
    out_specs = (
        P("fsdp", "ctx", None),
        P("fsdp", "ctx", None),
        P(("fsdp", "ctx")),
        P(("fsdp", "ctx"), "tp"),
        P(("fsdp", "ctx"), "tp"),
        P(("fsdp", "ctx"), "tp"),
        P(("fsdp", "ctx"), "tp"),
        P(("fsdp", "ctx")),
        P(("fsdp", "ctx"), None),
        P(None, ("fsdp", "ctx"), "tp"),
        P(None, ("fsdp", "ctx"), "tp"),
        P(None, ("fsdp", "ctx"), "tp"),
    )
    return jax.shard_map(local, mesh=mesh, in_specs=in_specs, out_specs=out_specs, check_vma=False)
```

profile of v0, /device:TPU:0, one launch (start us, length us, event | category | flops | bytes accessed | tf_op | source)
XLA Modules:
  0.0 2184.1 jit_solution(6278636484595905535)
XLA Ops:
  10.5 48.0 %all_gather.39 = bf16[1024,256]{1,0:T(8,128)(2,1)S(1)} all-gather(bf16[64,256]{1,0:T(8,128)(2,1)} %param.22), channel_id=1, replica_groups=mesh['fsdp'=4,'ctx'=4,'tp'=2] {'fsdp','ctx'}, dimensions={0}, use_global_device_ids=true | all-gather | bytes 557056 | tf_op jit(solution)/shard_map/all_gather | solution.py:138
  62.4 37.0 %all-reduce.5 = (bf16[1024]{0:T(1024)(128)(2,1)S(1)}, bf16[1024]{0:T(1024)(128)(2,1)S(1)}) all-reduce(bf16[1024]{0:T(1024)(128)(2,1)S(1)} %dynamic-update-slice, bf16[1024]{0:T(1024)(128)(2,1)S(1)} %dynamic-update-slice.1), channel_id=1, replica_groups=mesh['fsdp'=4,'ctx'=4,'tp'=2] {'fsdp','ctx'}, use_global_device_ids=true, to_apply=%add | all-reduce | flops 2048 | bytes 8192
  103.3 13.5 all_gather.40
  116.9 42.5 %all_gather.42 = bf16[1024,256]{1,0:T(8,128)(2,1)S(1)} all-gather(bf16[64,256]{1,0:T(8,128)(2,1)S(1)} %copy-done.36), channel_id=1, replica_groups=mesh['fsdp'=4,'ctx'=4,'tp'=2] {'fsdp','ctx'}, dimensions={0}, use_global_device_ids=true | all-gather | bytes 557056 | tf_op jit(solution)/shard_map/all_gather | solution.py:139
  159.7 13.9 all_gather.43
  195.5 36.8 %all-gather = bf16[16,64,16]{1,2,0:T(8,128)(2,1)S(1)} all-gather(bf16[1,64,16]{1,2,0:T(8,128)(2,1)S(1)} %bitcast.325), channel_id=1, replica_groups=mesh['fsdp'=4,'ctx'=4,'tp'=2] {'fsdp','ctx'}, dimensions={0}, use_global_device_ids=true | all-gather | bytes 34816 | tf_op jit(solution)/shard_map/all_gather | solution.py:142
  270.7 49.7 %all-gather.11.cloned.1.call-done = bf16[16,1024,256]{2,1,0:T(8,128)(2,1)} async-done(((bf16[16,64,256]{2,1,0:T(8,128)(2,1)}), bf16[16,1024,256]{2,1,0:T(8,128)(2,1)}) %all-gather.11.cloned.1.call-update) | async-done | bytes 8388624 | tf_op jit(solution)/shard_map/all_gather | solution.py:236
  327.4 106.5 %all-gather.13.cloned.1.call-done = bf16[16,1024,256]{2,1,0:T(8,128)(2,1)} async-done(((bf16[16,64,256]{2,1,0:T(8,128)(2,1)}), bf16[16,1024,256]{2,1,0:T(8,128)(2,1)}) %all-gather.13.cloned.1.call-update) | async-done | bytes 8388624 | tf_op jit(solution)/shard_map/all_gather | solution.py:237
  441.0 106.6 %all-gather.15.cloned.1.call-done = bf16[16,1024,256]{2,1,0:T(8,128)(2,1)} async-done(((bf16[16,64,256]{2,1,0:T(8,128)(2,1)}), bf16[16,1024,256]{2,1,0:T(8,128)(2,1)}) %all-gather.15.cloned.1.call-update) | async-done | bytes 8388624 | tf_op jit(solution)/shard_map/all_gather | solution.py:238
  607.8 16.9 all-reduce.13.cloned.1.call-done
  629.8 24.2 %while.35 = (s32[]{:T(128)}, f32[128,4,2,64]{0,3,2,1:T(8,128)S(1)}, bf16[4,128,256]{2,1,0:T(8,128)(2,1)}, bf16[4,128,256]{2,1,0:T(8,128)(2,1)}, bf16[4,128,4,64]...) while((s32[]{:T(128)}, f32[128,4,2,64]{0,3,2,1:T(8,128)S(1)}, ...), condition=%wide.region_31.32_spmd.clone, body=%wide.region_29.31_spmd.clone.sunk | while | flops 85118080 | bytes 4305131 | solution.py:325
  656.3 19.1 reduce-scatter.13.cloned.1.call-done
  676.8 19.2 reduce-scatter.15.cloned.1.call-done
  728.2 11.0 fusion.52
  740.0 34.4 %reduce-scatter.31.cloned.1.call-done = f32[64,16]{1,0:T(8,128)} async-done(((f32[1024,16]{1,0:T(8,128)}), f32[64,16]{1,0:T(8,128)}) %reduce-scatter.31.cloned.1.call-update) | async-done | bytes 4112
  775.8 16.6 all-reduce.15.cloned.1.call-done
  793.5 43.6 %all-reduce.4 = (f32[1024]{0:T(1024)S(1)}, f32[1024]{0:T(1024)S(1)}) all-reduce(f32[1024]{0:T(1024)S(1)} %get-tuple-element.550, f32[1024]{0:T(1024)S(1)} %copy-done.44), channel_id=4, replica_groups=mesh['fsdp'=4,'ctx'=4,'tp'=2] {'fsdp','ctx'}, use_global_device_ids=true, to_apply=%region_37.38.clone | all-reduce | flops 2048 | bytes 16384
  842.0 34.5 %reduce-scatter.19.cloned.1.call-done = f32[64,256]{1,0:T(8,128)} async-done(((f32[1024,256]{1,0:T(8,128)}), f32[64,256]{1,0:T(8,128)}) %reduce-scatter.19.cloned.1.call-update) | async-done | bytes 65552 | tf_op jit(solution)/shard_map/reduce_scatter | solution.py:375
  876.5 78.9 %reduce-scatter.21.cloned.1.call-done = f32[64,256]{1,0:T(8,128)} async-done(((f32[1024,256]{1,0:T(8,128)}), f32[64,256]{1,0:T(8,128)}) %reduce-scatter.21.cloned.1.call-update) | async-done | bytes 65552 | tf_op jit(solution)/shard_map/reduce_scatter | solution.py:376
  955.4 84.0 %reduce-scatter.17.cloned.1.call-done = f32[64,512]{1,0:T(8,128)} async-done(((f32[1024,512]{1,0:T(8,128)}), f32[64,512]{1,0:T(8,128)}) %reduce-scatter.17.cloned.1.call-update) | async-done | bytes 131088 | tf_op jit(solution)/shard_map/reduce_scatter | solution.py:374
  1039.4 84.5 %reduce-scatter.23.cloned.1.call-done = f32[64,512]{1,0:T(8,128)} async-done(((f32[1024,512]{1,0:T(8,128)}), f32[64,512]{1,0:T(8,128)}) %reduce-scatter.23.cloned.1.call-update) | async-done | bytes 131088 | tf_op jit(solution)/shard_map/reduce_scatter | solution.py:377
  1123.9 349.4 %reduce-scatter.25.cloned.1.call-done = f32[16,64,256]{2,1,0:T(8,128)} async-done(((f32[16,1024,256]{2,1,0:T(8,128)}), f32[16,64,256]{2,1,0:T(8,128)}) %reduce-scatter.25.cloned.1.call-update) | async-done | bytes 1048592 | tf_op jit(solution)/shard_map/reduce_scatter | solution.py:244
  1473.3 351.8 %reduce-scatter.27.cloned.1.call-done = f32[16,64,256]{2,1,0:T(8,128)} async-done(((f32[16,1024,256]{2,1,0:T(8,128)}), f32[16,64,256]{2,1,0:T(8,128)}) %reduce-scatter.27.cloned.1.call-update) | async-done | bytes 1048592 | tf_op jit(solution)/shard_map/reduce_scatter | solution.py:245
  1825.1 351.8 %reduce-scatter.29.cloned.1.call-done = f32[16,64,256]{2,1,0:T(8,128)} async-done(((f32[16,1024,256]{2,1,0:T(8,128)}), f32[16,64,256]{2,1,0:T(8,128)}) %reduce-scatter.29.cloned.1.call-update) | async-done | bytes 1048592 | tf_op jit(solution)/shard_map/reduce_scatter | solution.py:246
  (371 shorter events, 225.6 us)
Async XLA Ops:
  7.2 152.3 %copy-start.1 = (bf16[1,128,1024]{2,1,0:T(8,128)(2,1)S(1)}, bf16[1,128,1024]{2,1,0:T(8,128)(2,1)}, u32[]{:S(2)}) copy-start(bf16[1,128,1024]{2,1,0:T(8,128)(2,1)} %param.18) | copy-start | bytes 786436
  7.2 109.7 %copy-start.36 = (bf16[64,256]{1,0:T(8,128)(2,1)S(1)}, bf16[64,256]{1,0:T(8,128)(2,1)}, u32[]{:S(2)}) copy-start(bf16[64,256]{1,0:T(8,128)(2,1)} %param.23) | copy-start | bytes 98308
  7.2 166.9 %all-gather.7.cloned.1.call-start = ((), (), s32[]{:S(2)}) async-start(), calls=%async_computation.10 | async-start | bytes 1114112 | tf_op jit(solution)/shard_map/all_gather | solution.py:137
  7.9 177.8 %all-gather.9.cloned.1.call-start = ((), (), s32[]{:S(2)}) async-start(), calls=%async_computation.11 | async-start | bytes 1114112 | tf_op jit(solution)/shard_map/all_gather | solution.py:140
  8.7 240.3 %all-reduce.11.cloned.1.call-start = ((), (), s32[]{:S(2)}) async-start(), calls=%async_computation.12 | async-start | bytes 1048576 | tf_op jit(solution)/shard_map/psum | solution.py:218
  188.3 132.1 %all-gather.11.cloned.1.call-start = ((), (), s32[]{:S(2)}) async-start(), calls=%async_computation.13 | async-start | bytes 8912896 | tf_op jit(solution)/shard_map/all_gather | solution.py:236
  188.9 245.1 %all-gather.13.cloned.1.call-start = ((), (), s32[]{:S(2)}) async-start(), calls=%async_computation.14 | async-start | bytes 8912896 | tf_op jit(solution)/shard_map/all_gather | solution.py:237
  189.5 358.1 %all-gather.15.cloned.1.call-start = ((), (), s32[]{:S(2)}) async-start(), calls=%async_computation.15 | async-start | bytes 8912896 | tf_op jit(solution)/shard_map/all_gather | solution.py:238
  190.1 434.6 %all-reduce.13.cloned.1.call-start = ((), (), s32[]{:S(2)}) async-start(), calls=%async_computation.16 | async-start | bytes 524288 | tf_op jit(solution)/shard_map/psum | solution.py:256
  250.1 376.7 %copy-start.2 = (f32[128,1024]{1,0:T(8,128)}, f32[128,1024]{1,0:T(8,128)S(1)}, u32[]{:S(2)}) copy-start(f32[128,1024]{1,0:T(8,128)S(1)} %get-tuple-element.615) | copy-start | bytes 1572868
  270.5 163.5 %copy-start.42 = (pred[16,96]{1,0:T(8,128)(4,1)}, pred[16,96]{1,0:T(8,128)(4,1)S(1)}, u32[]{:S(2)}) copy-start(pred[16,96]{1,0:T(8,128)(4,1)S(1)} %broadcast_in_dim.157) | copy-start | bytes 4612
  270.5 277.1 %copy-start.34 = (f32[16,96]{1,0:T(8,128)}, f32[16,96]{1,0:T(8,128)S(1)}, u32[]{:S(2)}) copy-start(f32[16,96]{1,0:T(8,128)S(1)} %mul.453) | copy-start | bytes 18436
  270.5 308.2 %copy-start.31 = (f32[128,8]{0,1:T(8,128)}, f32[128,8]{0,1:T(8,128)S(1)}, u32[]{:S(2)}) copy-start(f32[128,8]{0,1:T(8,128)S(1)} %fusion.105) | copy-start | bytes 12292
  607.7 67.8 %reduce-scatter.13.cloned.1.call-start = ((), (), s32[]{:S(2)}) async-start(), calls=%async_computation.17 | async-start | bytes 327680 | tf_op jit(solution)/shard_map/reduce_scatter | solution.py:331
  654.1 41.9 %reduce-scatter.15.cloned.1.call-start = ((), (), s32[]{:S(2)}) async-start(), calls=%async_computation.18 | async-start | bytes 327680 | tf_op jit(solution)/shard_map/reduce_scatter | solution.py:337
  654.8 119.6 %reduce-scatter.31.cloned.1.call-start = ((), (), s32[]{:S(2)}) async-start(), calls=%async_computation.26 | async-start | bytes 557056
  656.2 136.2 %all-reduce.15.cloned.1.call-start = ((), (), s32[]{:S(2)}) async-start(), calls=%async_computation.27 | async-start | bytes 1048576 | tf_op jit(solution)/shard_map/psum | solution.py:254
  698.4 178.1 %reduce-scatter.19.cloned.1.call-start = ((), (), s32[]{:S(2)}) async-start(), calls=%async_computation.20 | async-start | bytes 1114112 | tf_op jit(solution)/shard_map/reduce_scatter | solution.py:375
  700.5 254.9 %reduce-scatter.21.cloned.1.call-start = ((), (), s32[]{:S(2)}) async-start(), calls=%async_computation.21 | async-start | bytes 1114112 | tf_op jit(solution)/shard_map/reduce_scatter | solution.py:376
  702.0 337.3 %reduce-scatter.17.cloned.1.call-start = ((), (), s32[]{:S(2)}) async-start(), calls=%async_computation.19 | async-start | bytes 2228224 | tf_op jit(solution)/shard_map/reduce_scatter | solution.py:374
  705.1 418.8 %reduce-scatter.23.cloned.1.call-start = ((), (), s32[]{:S(2)}) async-start(), calls=%async_computation.22 | async-start | bytes 2228224 | tf_op jit(solution)/shard_map/reduce_scatter | solution.py:377
  708.0 765.3 %reduce-scatter.25.cloned.1.call-start = ((), (), s32[]{:S(2)}) async-start(), calls=%async_computation.23 | async-start | bytes 17825792 | tf_op jit(solution)/shard_map/reduce_scatter | solution.py:244
  717.7 1107.4 %reduce-scatter.27.cloned.1.call-start = ((), (), s32[]{:S(2)}) async-start(), calls=%async_computation.24 | async-start | bytes 17825792 | tf_op jit(solution)/shard_map/reduce_scatter | solution.py:245
  727.1 1449.7 %reduce-scatter.29.cloned.1.call-start = ((), (), s32[]{:S(2)}) async-start(), calls=%async_computation.25 | async-start | bytes 17825792 | tf_op jit(solution)/shard_map/reduce_scatter | solution.py:246
  (46 other events, 1288.6 us)
Sparse Core Ops, SparseCore 0:
  10.8 58.8 all-gather.6
  72.4 54.6 all-gather.8
  188.4 15.5 all-reduce.10
  206.8 113.5 all-gather.10
  323.1 110.8 all-gather.12
  436.7 110.8 all-gather.14
  607.8 16.8 all-reduce.12
  654.2 21.2 reduce-scatter.12
  677.7 18.2 reduce-scatter.14
  698.1 76.2 reduce-scatter.30
  777.3 15.0 all-reduce.14
  795.1 81.3 reduce-scatter.18
  879.3 76.0 reduce-scatter.20
  958.1 81.2 reduce-scatter.16
  1042.1 81.7 reduce-scatter.22
  1126.6 346.6 reduce-scatter.24
  1476.0 348.9 reduce-scatter.26
  1827.8 348.9 reduce-scatter.28
where the time goes:
time: 2190 us; the launch traced here: 2180 us
  waiting for transfers between devices  1710 us (78%)
  blocking collectives  238 us (11%)
  matrix products  106 us (5%)
  local copies, waits for them, and re-layouts  75.4 us (3%)
  other arithmetic  38.6 us (2%)
    reduce_scatter x1, waiting for transfers between devices, local(): lax.psum_scatter(down_term, ('fsdp', 'ctx'), scatter_dimension=1, tiled=T...  352 us
    reduce_scatter x1, waiting for transfers between devices, local(): lax.psum_scatter(up_term, ('fsdp', 'ctx'), scatter_dimension=1, tiled=True)  352 us
    reduce_scatter x1, waiting for transfers between devices, local(): lax.psum_scatter(gate_term, ('fsdp', 'ctx'), scatter_dimension=1, tiled=T...  349 us
    all_gather x1, waiting for transfers between devices, local(): lax.all_gather(down_weight, ('fsdp', 'ctx'), axis=1, tiled=True)  107 us
    all_gather x1, waiting for transfers between devices, local(): lax.all_gather(up_weight, ('fsdp', 'ctx'), axis=1, tiled=True)  107 us
    reduce_scatter x1, waiting for transfers between devices, local(): lax.psum_scatter(output_term, ('fsdp', 'ctx'), scatter_dimension=0, tiled...  84.5 us
    reduce_scatter x1, waiting for transfers between devices, local(): lax.psum_scatter(query_term, ('fsdp', 'ctx'), scatter_dimension=0, tiled=...  84 us
    unnamed x2, blocking collectives  80.5 us
  transfers between devices with their start and end apart: 18, of which 15 were waited for; matrix products, arithmetic and copies ran while one was open for 6% of the time, Pallas kernels for 0%

commit v1 on v0

--- a/solution.py
+++ b/solution.py
@@ -1,6 +1,10 @@
+import functools
+
 import jax
 import jax.numpy as jnp
 from jax import lax
+from jax.experimental import pallas as pl
+from jax.experimental.pallas import tpu as pltpu
 from jax.sharding import PartitionSpec as P
 
 HD = 64
@@ -394,6 +398,683 @@
     )
 
 
+MESH = pl.DeviceIdType.MESH
+f32 = jnp.float32
+bf16 = jnp.bfloat16
+
+
+def dot_nn(a, b, precision=None):
+    return lax.dot_general(a, b, (((1,), (0,)), ((), ())), precision=precision, preferred_element_type=f32)
+
+
+def dot_nt(a, b, precision=None):
+    return lax.dot_general(a, b, (((1,), (1,)), ((), ())), precision=precision, preferred_element_type=f32)
+
+
+def dot_tn(a, b, precision=None):
+    return lax.dot_general(a, b, (((0,), (0,)), ((), ())), precision=precision, preferred_element_type=f32)
+
+
+class Net:
+    def __init__(self, send_sems, recv_sems):
+        self.send_sems, self.recv_sems, self.copies = send_sems, recv_sems, []
+
+    def send(self, source, target, device):
+        at = len(self.copies)
+        copy = pltpu.make_async_remote_copy(
+            src_ref=source,
+            dst_ref=target,
+            send_sem=self.send_sems.at[at],
+            recv_sem=self.recv_sems.at[at],
+            device_id=device,
+            device_id_type=MESH,
+        )
+        copy.start()
+        self.copies.append(copy)
+        return copy
+
+    def drain(self):
+        for copy in self.copies:
+            copy.wait_send()
+
+
+def layer_kernel(
+    dims,
+    x_ref, g_ref, wp_ref, sm_ref, wo_ref, wg_ref, wu_ref, wd_ref, dl_ref, ec_ref, fr_ref,
+    block_out, input_grad, small_out, gain_out, dqkv_out, dwo_out, dgu_out, dd_out,
+    X, WQ, WO, SMB, SMW, N1, CT, ST, SEGC, POSC, Q, K, V, PSC, ATT, AT, PP, PR, RES,
+    N2, GTB, GA, WGU, WD, AA, PSX, GC, H, UG, PRD, MP, MR, BP, BR, DGU, DDT, GDS, GD,
+    RB, RM, TB, RB2, TM, RM2, BOWN, MOWN, DGB, GUL, DDB, DDL, SG, RSG, GRES, RL,
+    AGS, AGR, DWO, RWO, ZWO, LWO, DS, DQ, DQKV, NG, NR, NZ, DWQ, RWQ, ZWQ, LWQ,
+    SG1, RSG1, EXB, EXG,
+    send_sems, recv_sems, local_sems,
+):
+    nf, nz, hb, width, experts, half_ff, ndoc, chosen = dims
+    rows = 2 * nz * hb
+    half = nz * hb
+    block = 2 * hb
+    f, z, c = lax.axis_index("fsdp"), lax.axis_index("ctx"), lax.axis_index("tp")
+    other = 1 - c
+    own = f * nz + z
+    net = Net(send_sems, recv_sems)
+    device = lambda df, dz, core: {"fsdp": df, "ctx": dz, "tp": core}
+    partner = device(f, z, other)
+    zs = [lax.rem(z + k, nz) for k in range(nz)]
+    zback = [lax.rem(z + nz - k, nz) for k in range(nz)]
+    fs = [lax.rem(f + k, nf) for k in range(nf)]
+    fback = [lax.rem(f + nf - k, nf) for k in range(nf)]
+    everyone = [(i, j, k) for k in range(2) for i in range(nf) for j in range(nz) if (i, j, k) != (0, 0, 0)]
+    others = [device(fs[i], zs[j], lax.rem(c + k, 2)) for i, j, k in everyone]
+    mine = pl.ds(pl.multiple_of(c * hb, hb), hb)
+    yours = pl.ds(pl.multiple_of(other * hb, hb), hb)
+
+    barrier = pltpu.get_barrier_semaphore()
+    for peer in others:
+        pl.semaphore_signal(barrier, inc=1, device_id=peer, device_id_type=MESH)
+    pl.semaphore_wait(barrier, len(others))
+
+    sends_x = [net.send(x_ref.at[mine], X.at[c, z], device(f, zs[k], c)) for k in range(1, nz)]
+    sends_q = [net.send(wp_ref.at[zs[k]], WQ.at[f, z], device(f, zs[k], c)) for k in range(1, nz)]
+    sends_s = [
+        net.send(sm_ref, SMB.at[f, z], device(fs[i], zs[j], c))
+        for i in range(nf) for j in range(nz) if (i, j) != (0, 0)
+    ]
+    X[0, z] = x_ref[0:hb]
+    X[1, z] = x_ref[hb:block]
+    WQ[f, z] = wp_ref[z]
+    SMB[f, z] = sm_ref[...]
+    sends_o = [net.send(wo_ref, WO.at[f, z], device(f, zs[k], c)) for k in range(1, nz)]
+    WO[f, z] = wo_ref[...]
+    sends_g = [net.send(g_ref.at[mine], GA.at[f, c, z], device(f, zs[k], c)) for k in range(1, nz)]
+    GA[f, 0, z] = g_ref[0:hb]
+    GA[f, 1, z] = g_ref[hb:block]
+
+    def places(shape, dim):
+        at = lax.broadcasted_iota(jnp.int32, shape, dim)
+        core_at, rest = lax.div(at, half), lax.rem(at, half)
+        return lax.div(rest, hb) * block + core_at * hb + lax.rem(rest, hb)
+
+    def layout(position):
+        segment = jnp.zeros_like(position)
+        start = jnp.zeros_like(position)
+        end = jnp.int32(0)
+        for i in range(ndoc):
+            length = dl_ref[0, i]
+            end = end + length
+            after = jnp.where(position >= end, 1, 0)
+            segment = segment + after
+            start = start + after * length
+        return segment, position - start
+
+    pos_col = places((rows, 1), 0)
+    seg_col, offset = layout(pos_col)
+    POSC[...] = pos_col
+    SEGC[...] = seg_col
+    angle = offset.astype(f32) * fr_ref[0:1, :]
+    lane = lax.broadcasted_iota(jnp.int32, (1, 2 * HD), 1)
+    former = lax.rem(lane, HD) < HD // 2
+    CT[...] = jnp.cos(angle)
+    ST[...] = jnp.where(former, -1.0, 1.0) * jnp.sin(angle)
+    pos_row = places((1, rows), 1)
+    seg_row, unused = layout(pos_row)
+    is_key = lane < HD
+
+    def swapped(v):
+        return jnp.where(former, pltpu.roll(v, 2 * HD - HD // 2, 1), pltpu.roll(v, HD // 2, 1))
+
+    for k in range(1, nz):
+        sends_q[k - 1].wait_recv()
+    sends_q2 = [net.send(WQ.at[f], WQ.at[f], device(fs[k], z, c)) for k in range(1, nf)]
+    forwards_x = []
+    for k in range(1, nz):
+        sends_x[k - 1].wait_recv()
+        forwards_x.append(net.send(X.at[c, zback[k]], X.at[c, zback[k]], partner))
+
+    sends_e = []
+    for i in range(nf):
+        for j in range(nz):
+            if (i, j) != (0, 0):
+                e = fs[i] * nz + zs[j]
+                to = device(fs[i], zs[j], c)
+                sends_e.append(net.send(wg_ref.at[e], WGU.at[own, :, pl.ds(0, half_ff)], to))
+                sends_e.append(net.send(wu_ref.at[e], WGU.at[own, :, pl.ds(half_ff, half_ff)], to))
+                sends_e.append(net.send(wd_ref.at[e], WD.at[own], to))
+    locals_e = [
+        pltpu.make_async_copy(wg_ref.at[own], WGU.at[own, :, pl.ds(0, half_ff)], local_sems.at[0]),
+        pltpu.make_async_copy(wu_ref.at[own], WGU.at[own, :, pl.ds(half_ff, half_ff)], local_sems.at[1]),
+        pltpu.make_async_copy(wd_ref.at[own], WD.at[own], local_sems.at[2]),
+    ]
+    for copy in locals_e:
+        copy.start()
+
+    for copy in sends_s:
+        copy.wait_recv()
+    for pair in range(nf * nz // 2):
+        at_f, at_z = pair // (nz // 2), 2 * (pair % (nz // 2))
+        SMW[:, 128 * pair : 128 * pair + 128] = SMB[at_f, at_z] + SMB[at_f, at_z + 1]
+    gain_one = SMW[0:1, :].astype(f32)
+    gain_two = SMW[1:2, :].astype(f32)
+
+    for copy in sends_o:
+        copy.wait_recv()
+    sends_o2 = [net.send(WO.at[f], WO.at[f], device(fs[k], z, c)) for k in range(1, nf)]
+
+    for copy in forwards_x:
+        copy.wait_recv()
+
+    def norm_chunk(i, carry):
+        at_c, at_z = lax.div(i, nz), lax.rem(i, nz)
+        v = X[at_c, at_z].astype(f32)
+        inverse = lax.rsqrt(jnp.mean(v * v, axis=1, keepdims=True) + epsilon)
+        N1[pl.ds(pl.multiple_of(i * hb, hb), hb), :] = (v * inverse * SMW[0:1, :].astype(f32)).astype(bf16)
+        return carry
+
+    lax.fori_loop(0, 2 * nz, norm_chunk, 0)
+    for copy in sends_q2:
+        copy.wait_recv()
+    wq_full = WQ[...].reshape(width, 4 * HD)
+    projected = dot_nn(N1[...], wq_full)
+    cosine, sine = CT[...], ST[...]
+    q_part, kv_part = projected[:, : 2 * HD], projected[:, 2 * HD :]
+    Q[...] = (q_part * cosine + swapped(q_part) * sine).astype(bf16)
+    kv = jnp.where(is_key, kv_part * cosine + swapped(kv_part) * sine, kv_part).astype(bf16)
+    K[...] = kv[:, :HD]
+    V[...] = kv[:, HD:]
+
+    scale = HD ** (-0.5)
+    step = 2 * hb
+
+    def attend(i, carry):
+        at = pl.ds(pl.multiple_of(i * step, step), step)
+        mask = (SEGC[at, :] == seg_row) & (pos_row <= POSC[at, :])
+        q = Q[at, :]
+        pieces = []
+        for r in range(2):
+            scores = dot_nt(q[:, r * HD : (r + 1) * HD], K[...]) * scale
+            scores = jnp.where(mask, scores, masked_score)
+            peak = jnp.max(scores, axis=1, keepdims=True)
+            weights = jnp.where(mask, jnp.exp(scores - peak), 0.0)
+            total = jnp.sum(weights, axis=1, keepdims=True)
+            pieces.append(dot_nn(weights.astype(bf16), V[...]) / total)
+            PSC[r, at, :] = weights / total
+        out = jnp.concatenate(pieces, axis=1).astype(bf16)
+        at_c, at_z = lax.div(2 * i, nz), lax.rem(2 * i, nz)
+        ATT[at_c, pl.ds(at_z, 2)] = out.reshape(2, hb, 2 * HD)
+        return carry
+
+    lax.fori_loop(0, rows // step, attend, 0)
+    columns = pl.ds(pl.multiple_of(z * 2 * HD, 2 * HD), 2 * HD)
+    sends_a = [
+        net.send(ATT.at[:, zs[k]], AT.at[:, :, columns], device(f, zs[k], c)) for k in range(1, nz)
+    ]
+    AT[:, :, columns] = ATT[:, z]
+
+    for copy in sends_g:
+        copy.wait_recv()
+    sends_g2 = [net.send(GA.at[f, c], GA.at[f, c], device(fs[k], z, c)) for k in range(1, nf)]
+    forwards_g = [net.send(GA.at[f, c, zback[k]], GA.at[f, c, zback[k]], partner) for k in range(1, nz)]
+
+    for copy in sends_o2:
+        copy.wait_recv()
+    for copy in sends_a:
+        copy.wait_recv()
+    part = dot_nt(AT[...].reshape(block, nz * 2 * HD), WO[...].reshape(width, nz * 2 * HD))
+    PP[...] = part.reshape(2, hb, width)
+    send_p = net.send(PP.at[other], PR, partner)
+    x_own = x_ref[mine, :].astype(f32)
+    send_p.wait_recv()
+    residual = x_own + PP[c] + PR[...]
+    RES[...] = residual
+    inverse_two = lax.rsqrt(jnp.mean(residual * residual, axis=1, keepdims=True) + epsilon)
+    N2[f, c, z] = (residual * inverse_two * gain_two).astype(bf16)
+    sends_n = [net.send(N2.at[f, c, z], N2.at[f, c, z], device(f, zs[k], c)) for k in range(1, nz)]
+    normed_two = N2[f, c, z]
+    logits = dot_nt(SMW[16 : 16 + experts, :], normed_two)
+    expert_at = lax.broadcasted_iota(jnp.int32, (experts, hb), 0)
+    picked = jnp.zeros((experts, hb), jnp.bool_)
+    for j in range(chosen):
+        picked = picked | (ec_ref[j : j + 1, 0:hb] == expert_at)
+    peak = jnp.max(jnp.where(picked, logits, masked_score), axis=0, keepdims=True)
+    weight = jnp.where(picked, jnp.exp(logits - peak), 0.0)
+    gates = weight / jnp.sum(weight, axis=0, keepdims=True)
+    GTB[f, c, z] = jnp.concatenate([gates, jnp.zeros((experts, 128 - hb), f32)], axis=1)
+    sends_t = [
+        net.send(GTB.at[f, c, z], GTB.at[f, c, z], device(fs[i], zs[j], lax.rem(c + k, 2)))
+        for i, j, k in everyone
+    ]
+
+    for copy in locals_e:
+        copy.wait()
+    for copy in sends_e:
+        copy.wait_recv()
+    for copy in forwards_g:
+        copy.wait_recv()
+    wd_full = lambda: WD[...].reshape(width, half_ff)
+    wgu_full = lambda: WGU[...].reshape(width, 2 * half_ff)
+    AA[f] = dot_nn(GA[f].reshape(rows, width), wd_full())
+
+    for copy in sends_n:
+        copy.wait_recv()
+    sends_n2 = [net.send(N2.at[f, c], N2.at[f, c], device(fs[k], z, c)) for k in range(1, nf)]
+    forwards_n = [net.send(N2.at[f, c], N2.at[f, c], partner)]
+    forwards_g2 = []
+    for k in range(1, nf):
+        sends_g2[k - 1].wait_recv()
+        forwards_g2.append(net.send(GA.at[fback[k], c], GA.at[fback[k], c], partner))
+    for copy in sends_t:
+        copy.wait_recv()
+
+    chosen_row = jnp.where(
+        lax.broadcasted_iota(jnp.int32, (experts, 128), 0) == own, 1.0, 0.0
+    ).astype(f32)
+    DGU[...] = jnp.zeros_like(DGU)
+    DDT[...] = jnp.zeros_like(DDT)
+    sends_d, sends_b, sends_m = [], [], []
+    exchange_b, exchange_m = [], []
+
+    for k in range(nf):
+        at_f = fback[k]
+        if k > 0:
+            forwards_g2[k - 1].wait_recv()
+            AA[at_f] = dot_nn(GA[at_f].reshape(rows, width), wd_full())
+            sends_n2[k - 1].wait_recv()
+            forwards_n.append(net.send(N2.at[at_f, c], N2.at[at_f, c], partner))
+        forwards_n[k].wait_recv()
+        tokens = N2[at_f].reshape(rows, width)
+        PSX[...] = dot_nn(tokens, wgu_full())
+        for piece in range(2 * nz):
+            tile = GTB[at_f, piece // nz, piece % nz][:, 0:hb]
+            GC[piece * hb : (piece + 1) * hb, :] = dot_tn(tile, chosen_row, lax.Precision.HIGHEST)
+
+        def expert_chunk(i, carry):
+            at = pl.ds(pl.multiple_of(i * 32, 32), 32)
+            gate_pre = PSX[at, 0:half_ff]
+            up_pre = PSX[at, half_ff : 2 * half_ff]
+            raw = AA[at_f, at, :]
+            gate = GC[at, 0:1]
+            sigmoid = jax.nn.sigmoid(gate_pre)
+            silu = gate_pre * sigmoid
+            act = silu * up_pre
+            PRD[at, :] = (act * raw).astype(bf16)
+            H[at, :] = (act * gate).astype(bf16)
+            grad = raw * gate
+            UG[at, 0:half_ff] = (
+                grad * up_pre * sigmoid * (1.0 + gate_pre * (1.0 - sigmoid))
+            ).astype(bf16)
+            UG[at, half_ff : 2 * half_ff] = (grad * silu).astype(bf16)
+            return carry
+
+        lax.fori_loop(0, rows // 32, expert_chunk, 0)
+        BP[at_f] = dot_nt(UG[...], wgu_full()).astype(bf16).reshape(2, nz, hb, width)
+        exchange_b.append(net.send(BP.at[at_f, other], BR.at[at_f], partner))
+        GDS[k] = dot_nt(jnp.ones((8, half_ff), bf16), PRD[...])
+        for j in range(nz):
+            for t in range(2):
+                if (k, j, t) != (0, 0, 0):
+                    to_z, to_c = zs[j], lax.rem(c + t, 2)
+                    lanes = pl.ds(pl.multiple_of((to_c * (nz // 2) + lax.div(to_z, 2)) * 128, 128), 128)
+                    sends_d.append(
+                        net.send(GDS.at[k, :, lanes], GD.at[f, z, c], device(at_f, to_z, to_c))
+                    )
+                else:
+                    lanes = pl.ds(pl.multiple_of((c * (nz // 2) + lax.div(z, 2)) * 128, 128), 128)
+                    GD[f, z, c] = GDS[0, :, lanes]
+        MP[at_f] = dot_nt(H[...], wd_full()).astype(bf16).reshape(2, nz, hb, width)
+        exchange_m.append(net.send(MP.at[at_f, other], MR.at[at_f], partner))
+        exchange_b[k].wait_recv()
+        if k == 0:
+            BOWN[...] = BP[at_f, c].astype(f32) + BR[at_f].astype(f32)
+        else:
+            BP[at_f, c] = (BP[at_f, c].astype(f32) + BR[at_f].astype(f32)).astype(bf16)
+            sends_b.append(net.send(BP.at[at_f, c], RB.at[f], device(at_f, z, c)))
+        DGU[...] += dot_tn(UG[...], tokens)
+        DDT[...] += dot_tn(H[...], GA[at_f].reshape(rows, width))
+        exchange_m[k].wait_recv()
+        if k == 0:
+            MOWN[...] = MP[at_f, c].astype(f32) + MR[at_f].astype(f32)
+        else:
+            MP[at_f, c] = (MP[at_f, c].astype(f32) + MR[at_f].astype(f32)).astype(bf16)
+            sends_m.append(net.send(MP.at[at_f, c], RM.at[f], device(at_f, z, c)))
+
+    for k in range(1, nf):
+        sends_b[k - 1].wait_recv()
+        source = lax.rem(f + k, nf)
+        BOWN[...] += RB[source].astype(f32)
+    TB[...] = BOWN[...].astype(bf16)
+    sends_b2 = [net.send(TB.at[zs[k]], RB2.at[z], device(f, zs[k], c)) for k in range(1, nz)]
+
+    DGB[...] = jnp.transpose(DGU[...]).astype(bf16).reshape(nf, nz, width // (nf * nz), 2 * half_ff)
+    DDB[...] = jnp.transpose(DDT[...]).astype(bf16).reshape(nf, nz, width // (nf * nz), half_ff)
+    sends_w = []
+    for i in range(nf):
+        for j in range(nz):
+            if (i, j) != (0, 0):
+                to = device(fs[i], zs[j], c)
+                sends_w.append(net.send(DGB.at[fs[i], zs[j]], GUL.at[own], to))
+                sends_w.append(net.send(DDB.at[fs[i], zs[j]], DDL.at[own], to))
+    GUL[own] = DGB[f, z]
+    DDL[own] = DDB[f, z]
+
+    for copy in sends_d:
+        copy.wait_recv()
+    dots = jnp.concatenate(
+        [
+            GD[e // nz, e % nz, 0][0:1, :] + GD[e // nz, e % nz, 1][0:1, :]
+            for e in range(experts)
+        ],
+        axis=0,
+    )
+    dots = jnp.where(lax.rem(z, 2) == 0, dots, pltpu.roll(dots, 64, 1))[:, 0:hb]
+    gates = GTB[f, c, z][:, 0:hb]
+    logit_grad = gates * (dots - jnp.sum(gates * dots, axis=0, keepdims=True))
+    router_t = SMW[16 : 16 + experts, :].astype(f32)
+    router_term = dot_nn(logit_grad, N2[f, c, z].astype(f32), lax.Precision.HIGHEST)
+    router_input = dot_tn(logit_grad, router_t, lax.Precision.HIGHEST)
+    moe = BOWN[z]
+    for k in range(1, nz):
+        sends_b2[k - 1].wait_recv()
+        moe = moe + RB2[zback[k]].astype(f32)
+    grad_two = moe + router_input
+    residual = RES[...]
+    inverse_two = lax.rsqrt(jnp.mean(residual * residual, axis=1, keepdims=True) + epsilon)
+    scaled = grad_two * gain_two
+    grad_res = (
+        g_ref[mine, :].astype(f32)
+        + inverse_two * scaled
+        - residual * (inverse_two * inverse_two * inverse_two) * jnp.mean(scaled * residual, axis=1, keepdims=True)
+    )
+    GRES[...] = grad_res
+    RL[c] = grad_res.astype(bf16)
+    send_r = net.send(RL.at[c], RL.at[c], partner)
+    gain_term = jnp.sum(grad_two * residual * inverse_two, axis=0, keepdims=True)
+    SG[0:experts, :] = router_term
+    SG[experts : experts + 8, :] = jnp.broadcast_to(gain_term, (8, width))
+    sends_sg = []
+    for (i, j, k), to in zip(everyone, others):
+        lanes = pl.ds(pl.multiple_of((fs[i] * (nz // 2) + lax.div(zs[j], 2)) * 128, 128), 128)
+        sends_sg.append(net.send(SG.at[:, lanes], RSG.at[f, z, c], to))
+    own_lanes = pl.ds(pl.multiple_of((f * (nz // 2) + lax.div(z, 2)) * 128, 128), 128)
+    RSG[f, z, c] = SG[:, own_lanes]
+    send_r.wait_recv()
+    low = RL[...].reshape(block, width)
+    AGS[...] = dot_nn(low, WO[...].reshape(width, nz * 2 * HD)).astype(bf16).reshape(2, hb, nz * 2 * HD)
+    sends_ag = [
+        net.send(
+            AGS.at[:, :, pl.ds(pl.multiple_of(zs[k] * 2 * HD, 2 * HD), 2 * HD)],
+            AGR.at[:, z],
+            device(f, zs[k], c),
+        )
+        for k in range(1, nz)
+    ]
+    AGR[:, z] = AGS[:, :, columns]
+    shard = width // (nf * nz)
+    DWO[...] = (
+        dot_tn(low, AT[...].reshape(block, nz * 2 * HD))
+        .astype(bf16)
+        .reshape(nf, nz, shard, nz * 2 * HD)
+    )
+    sends_wo = [net.send(DWO.at[fs[k]], RWO.at[f], device(fs[k], z, c)) for k in range(1, nf)]
+
+    for copy in sends_ag:
+        copy.wait_recv()
+
+    def backward(i, carry):
+        at = pl.ds(pl.multiple_of(i * step, step), step)
+        at_c, at_z = lax.div(2 * i, nz), lax.rem(2 * i, nz)
+        grad = AGR[at_c, pl.ds(at_z, 2)].reshape(step, 2 * HD)
+        out = ATT[at_c, pl.ds(at_z, 2)].reshape(step, 2 * HD)
+        both = grad.astype(f32) * out.astype(f32)
+        pieces = []
+        for r in range(2):
+            delta = jnp.sum(both[:, r * HD : (r + 1) * HD], axis=1, keepdims=True)
+            prob_grad = dot_nt(grad[:, r * HD : (r + 1) * HD], V[...])
+            probs = PSC[r, at, :]
+            score_grad = (probs * (prob_grad - delta) * scale).astype(bf16)
+            DS[r, at, :] = score_grad
+            pieces.append(dot_nn(score_grad, K[...]))
+        DQ[at, :] = jnp.concatenate(pieces, axis=1)
+        return carry
+
+    lax.fori_loop(0, rows // step, backward, 0)
+    grads = AGR[...].reshape(rows, 2 * HD)
+    key_t = dot_tn(Q[:, 0:HD], DS[0]) + dot_tn(Q[:, HD : 2 * HD], DS[1])
+    value_t = dot_tn(grads[:, 0:HD], PSC[0].astype(bf16)) + dot_tn(
+        grads[:, HD : 2 * HD], PSC[1].astype(bf16)
+    )
+    kv_grad = jnp.transpose(jnp.concatenate([key_t, value_t], axis=0))
+    cosine, sine = CT[...], ST[...]
+    q_grad = DQ[...]
+    DQKV[:, 0 : 2 * HD] = (q_grad * cosine - swapped(q_grad) * sine).astype(bf16)
+    DQKV[:, 2 * HD : 4 * HD] = jnp.where(
+        is_key, kv_grad * cosine - swapped(kv_grad) * sine, kv_grad
+    ).astype(bf16)
+    NG[...] = dot_nt(DQKV[...], WQ[...].reshape(width, 4 * HD)).astype(bf16).reshape(2, nz, hb, width)
+    send_ng = net.send(NG.at[other], NR, partner)
+    DWQ[...] = (
+        jnp.transpose(dot_tn(DQKV[...], N1[...])).astype(bf16).reshape(nf, nz, shard, 4 * HD)
+    )
+    send_ng.wait_recv()
+    NG[c] = (NG[c].astype(f32) + NR[...].astype(f32)).astype(bf16)
+    sends_nz = [net.send(NG.at[c, zs[k]], NZ.at[z], device(f, zs[k], c)) for k in range(1, nz)]
+    sends_wq = [net.send(DWQ.at[fs[k]], RWQ.at[f], device(fs[k], z, c)) for k in range(1, nf)]
+
+    for k in range(1, nf):
+        sends_m[k - 1].wait_recv()
+        MOWN[...] += RM[lax.rem(f + k, nf)].astype(f32)
+    TM[...] = MOWN[...].astype(bf16)
+    sends_m2 = [net.send(TM.at[zs[k]], RM2.at[z], device(f, zs[k], c)) for k in range(1, nz)]
+
+    total = DWO[f].astype(f32)
+    for k in range(1, nf):
+        sends_wo[k - 1].wait_recv()
+        total = total + RWO[fback[k]].astype(f32)
+    ZWO[...] = total.astype(bf16)
+    sends_wo2 = [net.send(ZWO.at[zs[k]], LWO.at[z], device(f, zs[k], c)) for k in range(1, nz)]
+    LWO[z] = ZWO[z]
+    total = DWQ[f].astype(f32)
+    for k in range(1, nf):
+        sends_wq[k - 1].wait_recv()
+        total = total + RWQ[fback[k]].astype(f32)
+    ZWQ[...] = total.astype(bf16)
+    sends_wq2 = [net.send(ZWQ.at[zs[k]], LWQ.at[z], device(f, zs[k], c)) for k in range(1, nz)]
+    LWQ[z] = ZWQ[z]
+
+    grad_one = NG[c, z].astype(f32)
+    for k in range(1, nz):
+        sends_nz[k - 1].wait_recv()
+        grad_one = grad_one + NZ[zback[k]].astype(f32)
+    x_own = x_ref[mine, :].astype(f32)
+    inverse = lax.rsqrt(jnp.mean(x_own * x_own, axis=1, keepdims=True) + epsilon)
+    gain_term = jnp.sum(grad_one * x_own * inverse, axis=0, keepdims=True)
+    SG1[...] = jnp.broadcast_to(gain_term, (8, width))
+    sends_g1 = []
+    for (i, j, k), to in zip(everyone, others):
+        lanes = pl.ds(pl.multiple_of((fs[i] * (nz // 2) + lax.div(zs[j], 2)) * 128, 128), 128)
+        sends_g1.append(net.send(SG1.at[:, lanes], RSG1.at[f, z, c], to))
+    RSG1[f, z, c] = SG1[:, own_lanes]
+    scaled = grad_one * gain_one
+    EXG[c] = (
+        GRES[...]
+        + inverse * scaled
+        - x_own * (inverse * inverse * inverse) * jnp.mean(scaled * x_own, axis=1, keepdims=True)
+    )
+    send_ig = net.send(EXG.at[c], EXG.at[c], partner)
+
+    mixed = MOWN[z]
+    for k in range(1, nz):
+        sends_m2[k - 1].wait_recv()
+        mixed = mixed + RM2[zback[k]].astype(f32)
+    EXB[c] = (RES[...] + mixed).astype(bf16)
+    send_bo = net.send(EXB.at[c], EXB.at[c], partner)
+
+    for copy in sends_sg:
+        copy.wait_recv()
+    small = jnp.zeros((experts + 8, 128), f32)
+    for i in range(nf):
+        for j in range(nz):
+            small = small + RSG[i, j, 0] + RSG[i, j, 1]
+    small_out[...] = small
+    for copy in sends_wo2:
+        copy.wait_recv()
+    total = LWO[0].astype(f32)
+    for j in range(1, nz):
+        total = total + LWO[j].astype(f32)
+    dwo_out[...] = total
+    for copy in sends_wq2:
+        copy.wait_recv()
+    dqkv_out[...] = LWQ[...]
+    for copy in sends_w:
+        copy.wait_recv()
+    outs = [
+        pltpu.make_async_copy(GUL, dgu_out, local_sems.at[3]),
+        pltpu.make_async_copy(DDL, dd_out, local_sems.at[4]),
+    ]
+    for copy in outs:
+        copy.start()
+    for copy in sends_g1:
+        copy.wait_recv()
+    small = jnp.zeros((8, 128), f32)
+    for i in range(nf):
+        for j in range(nz):
+            small = small + RSG1[i, j, 0] + RSG1[i, j, 1]
+    gain_out[...] = small
+    send_bo.wait_recv()
+    block_out[...] = EXB[...].reshape(block, width)
+    send_ig.wait_recv()
+    input_grad[...] = EXG[...].reshape(block, width)
+    for copy in outs:
+        copy.wait()
+    net.drain()
+
+
+def fast_local(
+    nf, nz,
+    hidden_in, out_grad, attention_gain, query_weight, key_weight, value_weight, output_weight,
+    expert_gain, router_weight, gate_weight, up_weight, down_weight, doc_lengths, expert_choice,
+):
+    block, width = hidden_in.shape[1], hidden_in.shape[2]
+    hb = block // 2
+    experts, shard, half_ff = gate_weight.shape
+    ndoc, chosen = doc_lengths.shape[1], expert_choice.shape[2]
+    rows = nz * block
+    z, c = lax.axis_index("ctx"), lax.axis_index("tp")
+    packed = jnp.concatenate(
+        [
+            query_weight.reshape(shard, nz, 2 * HD),
+            key_weight.reshape(shard, nz, HD),
+            value_weight.reshape(shard, nz, HD),
+        ],
+        axis=2,
+    ).transpose(1, 0, 2)
+    base = jnp.concatenate(
+        [attention_gain[None], expert_gain[None], jnp.zeros((14, shard), bf16), router_weight.T], axis=0
+    )
+    blank = jnp.zeros_like(base)
+    even = lax.rem(z, 2) == 0
+    small = jnp.concatenate([jnp.where(even, base, blank), jnp.where(even, blank, base)], axis=1)
+    own_choice = lax.dynamic_slice_in_dim(expert_choice[0], c * hb, hb, axis=0)
+    route = jnp.concatenate([own_choice.T, jnp.zeros((chosen, 128 - hb), jnp.int32)], axis=1)
+    halfway = HD // 2
+    frequency = rope_base ** (-jnp.arange(halfway, dtype=f32) / halfway)
+    frequency = jnp.broadcast_to(jnp.tile(frequency, 4)[None], (8, 2 * HD))
+
+    vm = pl.BlockSpec(memory_space=pltpu.VMEM)
+    anywhere = pl.BlockSpec(memory_space=pl.ANY)
+    shape = lambda s, d: jax.ShapeDtypeStruct(s, d)
+    W = nz * 2 * HD
+    scratch = dict(
+        X=((2, nz, hb, width), bf16), WQ=((nf, nz, shard, 4 * HD), bf16), WO=((nf, nz, shard, W), bf16),
+        SMB=((nf, nz, 32, 128), bf16), SMW=((32, width), bf16), N1=((rows, width), bf16),
+        CT=((rows, 128), f32), ST=((rows, 128), f32), SEGC=((rows, 1), jnp.int32), POSC=((rows, 1), jnp.int32),
+        Q=((rows, 2 * HD), bf16), K=((rows, HD), bf16), V=((rows, HD), bf16), PSC=((2, rows, rows), f32),
+        ATT=((2, nz, hb, 2 * HD), bf16), AT=((2, hb, W), bf16), PP=((2, hb, width), f32), PR=((hb, width), f32),
+        RES=((hb, width), f32),
+        N2=((nf, 2, nz, hb, width), bf16), GTB=((nf, 2, nz, experts, 128), f32), GA=((nf, 2, nz, hb, width), bf16),
+        WGU=((nf * nz, shard, 2 * half_ff), bf16), WD=((nf * nz, shard, half_ff), bf16),
+        AA=((nf, rows, half_ff), f32), PSX=((rows, 2 * half_ff), f32), GC=((rows, 128), f32),
+        H=((rows, half_ff), bf16), UG=((rows, 2 * half_ff), bf16), PRD=((rows, half_ff), bf16),
+        MP=((nf, 2, nz, hb, width), bf16), MR=((nf, nz, hb, width), bf16),
+        BP=((nf, 2, nz, hb, width), bf16), BR=((nf, nz, hb, width), bf16),
+        DGU=((2 * half_ff, width), f32), DDT=((half_ff, width), f32),
+        GDS=((nf, 8, rows), f32), GD=((nf, nz, 2, 8, 128), f32),
+        RB=((nf, nz, hb, width), bf16),
+        RM=((nf, nz, hb, width), bf16),
+        TB=((nz, hb, width), bf16), RB2=((nz, hb, width), bf16),
+        TM=((nz, hb, width), bf16), RM2=((nz, hb, width), bf16),
+        BOWN=((nz, hb, width), f32), MOWN=((nz, hb, width), f32),
+        DGB=((nf, nz, shard, 2 * half_ff), bf16), GUL=((nf * nz, shard, 2 * half_ff), bf16),
+        DDB=((nf, nz, shard, half_ff), bf16), DDL=((nf * nz, shard, half_ff), bf16),
+        SG=((experts + 8, width), f32), RSG=((nf, nz, 2, experts + 8, 128), f32),
+        GRES=((hb, width), f32), RL=((2, hb, width), bf16),
+        AGS=((2, hb, W), bf16), AGR=((2, nz, hb, 2 * HD), bf16),
+        DWO=((nf, nz, shard, W), bf16), RWO=((nf, nz, shard, W), bf16),
+        ZWO=((nz, shard, W), bf16), LWO=((nz, shard, W), bf16),
+        DS=((2, rows, rows), bf16), DQ=((rows, 2 * HD), f32),
+        DQKV=((rows, 4 * HD), bf16), NG=((2, nz, hb, width), bf16), NR=((nz, hb, width), bf16),
+        NZ=((nz, hb, width), bf16),
+        DWQ=((nf, nz, shard, 4 * HD), bf16), RWQ=((nf, nz, shard, 4 * HD), bf16),
+        ZWQ=((nz, shard, 4 * HD), bf16), LWQ=((nz, shard, 4 * HD), bf16),
+        SG1=((8, width), f32), RSG1=((nf, nz, 2, 8, 128), f32),
+        EXB=((2, hb, width), bf16), EXG=((2, hb, width), f32),
+    )
+    slots = 400
+    out = pl.pallas_call(
+        functools.partial(layer_kernel, (nf, nz, hb, width, experts, half_ff, ndoc, chosen)),
+        name="layer",
+        out_shape=(
+            shape((block, width), bf16), shape((block, width), f32), shape((experts + 8, 128), f32),
+            shape((8, 128), f32), shape((nz, shard, 4 * HD), bf16), shape((shard, W), f32),
+            shape((nf * nz, shard, 2 * half_ff), bf16), shape((nf * nz, shard, half_ff), bf16),
+        ),
+        in_specs=[vm] * 5 + [anywhere] * 3 + [pl.BlockSpec(memory_space=pltpu.SMEM), vm, vm],
+        out_specs=(vm,) * 6 + (anywhere,) * 2,
+        scratch_shapes=[pltpu.VMEM(s, d) for s, d in scratch.values()]
+        + [pltpu.SemaphoreType.DMA((slots,)), pltpu.SemaphoreType.DMA((slots,)), pltpu.SemaphoreType.DMA((5,))],
+        compiler_params=pltpu.CompilerParams(
+            collective_id=0, has_side_effects=True, vmem_limit_bytes=67043328
+        ),
+    )(
+        hidden_in[0], out_grad[0], packed, small, output_weight, gate_weight, up_weight, down_weight,
+        doc_lengths, route, frequency,
+    )
+    block_out, input_grad, small, gain, dqkv, dwo, dgu, dd = out
+    lanes = lambda v: jnp.where(even, v[:, :shard], v[:, shard:])
+    small, gain = lanes(small), lanes(gain)
+    dqkv = dqkv.astype(f32)
+    return (
+        block_out[None],
+        input_grad[None],
+        gain[0],
+        dqkv[:, :, : 2 * HD].transpose(1, 0, 2).reshape(shard, -1),
+        dqkv[:, :, 2 * HD : 3 * HD].transpose(1, 0, 2).reshape(shard, -1),
+        dqkv[:, :, 3 * HD :].transpose(1, 0, 2).reshape(shard, -1),
+        dwo,
+        small[experts],
+        small[:experts].T,
+        dgu[:, :, :half_ff].astype(f32),
+        dgu[:, :, half_ff:].astype(f32),
+        dd.astype(f32),
+    )
+
+
+def fits(mesh, args):
+    nf, nz, nc = mesh.shape["fsdp"], mesh.shape["ctx"], mesh.shape["tp"]
+    hidden, query, key, gate = args[0], args[3], args[4], args[9]
+    width, block = hidden.shape[2], hidden.shape[1] // nz
+    return (
+        nc == 2
+        and nz % 2 == 0
+        and hidden.shape[0] == nf
+        and gate.shape[0] == nf * nz
+        and gate.shape[0] == 16
+        and width == 64 * nf * nz
+        and block == 128
+        and query.shape[1] == 2 * HD * nz * nc
+        and key.shape[1] == HD * nz * nc
+        and HD == 64
+    )
+
+
 def solution(mesh):
     in_specs = (
         P("fsdp", "ctx", None),
@@ -425,4 +1106,13 @@
         P(None, ("fsdp", "ctx"), "tp"),
         P(None, ("fsdp", "ctx"), "tp"),
     )
-    return jax.shard_map(local, mesh=mesh, in_specs=in_specs, out_specs=out_specs, check_vma=False)
+
+    def step(*args):
+        body = local
+        if fits(mesh, args):
+            body = functools.partial(fast_local, mesh.shape["fsdp"], mesh.shape["ctx"])
+        return jax.shard_map(
+            body, mesh=mesh, in_specs=in_specs, out_specs=out_specs, check_vma=False
+        )(*args)
+
+    return step

time: 2190 us -> 285 us (0.13)
  waiting for transfers between devices: 1710 us -> 0 us
  Pallas kernels: 0 us -> 266 us
  blocking collectives: 238 us -> 0 us
  matrix products: 106 us -> 0 us
  local copies, waits for them, and re-layouts: 75.4 us -> 11.7 us
  other arithmetic: 38.6 us -> 6.17 us
    reduce_scatter x9 -> x0, waiting for transfers between devices: 1370 us -> none  [the longest x1 352 us: local(): lax.psum_scatter(down_term, ('fsdp', 'ctx'), scatter_dimension=1, tiled=T...]
    pallas_call x0 -> x1, Pallas kernels: none -> 266 us  [fast_local(): pl.pallas_call(functools.partial(layer_kernel, (nf, nz, hb, width, expert...]
    all_gather x5 -> x0, waiting for transfers between devices: 263 us -> none  [the longest x1 107 us: local(): lax.all_gather(down_weight, ('fsdp', 'ctx'), axis=1, tiled=True)]
    all_gather x5 -> x0, blocking collectives: 155 us -> none  [the longest x1 48 us: local(): lax.all_gather(key_weight, ('fsdp', 'ctx'), axis=0, tiled=True)]
    dot_general x51 -> x0, matrix products: 105 us -> none  [the longest x1 11 us: expert_math(): jnp.einsum('gsd,gsf->gdf', slot_grads, activated, preferred_element_type=...]
    unnamed x2 -> x0, blocking collectives: 80.5 us -> none
    gather x10 -> x0, local copies, waits for them, and re-layouts: 43.2 us -> none  [the longest x1 9.21 us: local(): expert_out.reshape(experts * capacity, -1)[slot]]
    unnamed x19 -> x0, waiting for transfers between devices: 38.2 us -> none
  transfers between devices with their start and end apart: 18 -> 0, of which waited for: 15 -> 0; matrix products, arithmetic and copies ran while one was open for 6% -> 0% of each run, Pallas kernels for 0% -> 0%
where the time goes in v1:
time: 285 us
  Pallas kernels  266 us (93%)
  local copies, waits for them, and re-layouts  11.7 us (4%)
  other arithmetic  6.17 us (2%)
    pallas_call x1, Pallas kernels, fast_local(): pl.pallas_call(functools.partial(layer_kernel, (nf, nz, hb, width, expert...  266 us
    unnamed x27, local copies, waits for them, and re-layouts  5.73 us

profile of v1, /device:TPU:0, one launch (start us, length us, event | category | flops | bytes accessed | tf_op | source)
XLA Modules:
  0.0 284.7 jit_solution(4729839515134555640)
XLA Ops:
  0.6 0.9 reshape.52
  1.5 0.7 copy-done.6
  2.4 0.8 copy-done.5
  3.2 0.7 maximum_bitcast_fusion.wp_ref
  4.1 0.6 copy-done.9
  4.8 0.7 pad_maximum_fusion.1.sm_ref
  5.5 0.7 copy-done.8
  6.2 0.6 concatenate.15.ec_ref
  7.0 0.6 broadcast_in_dim.31.fr_ref
  7.6 266.0 %layer.1 = (bf16[128,1024]{1,0:T(8,128)(2,1)}, f32[128,1024]{1,0:T(8,128)}, f32[24,128]{1,0:T(8,128)}, f32[8,128]{1,0:T(8,128)}, bf16[4,64,256]{2,1,0:T(8,128)(2...) custom-call(bf16[128,1024]{1,0:T(8,128)(2,1)} %bitcast.35, ...), custom_call_target="tpu_custom_call" | custom-call | tf_op jit(solution)/shard_map/layer/pallas_call | solution.py:1021
  273.6 0.9 slice_select_fusion
  274.5 0.5 slice_bitcast_fusion.4
  275.1 1.0 convert_element_type.12
  276.1 0.7 copy_bitcast_fusion
  276.9 0.8 reshape.54
  277.8 0.8 reshape.55
  278.6 0.6 slice_bitcast_fusion.3
  279.2 1.6 slice_convert_fusion
  280.8 1.1 convert_element_type.15
  281.9 0.7 copy.39
  282.6 0.4 copy-done.2
  283.0 0.8 copy.40
  283.8 0.2 copy-done.4
  284.0 0.7 copy.41
  (33 shorter events, 0.9 us)
Async XLA Ops:
  1.5 0.8 copy-start.6
  2.4 0.8 copy-start.5
  4.0 0.7 copy-start.9
  4.1 0.7 copy-start.10
  4.1 0.7 copy-start.11
  5.5 0.7 copy-start.8
  273.6 0.9 copy-start.7
  275.1 4.1 %copy-start = (bf16[16,64,512]{2,1,0:T(8,128)(2,1)S(1)}, bf16[16,64,512]{2,1,0:T(8,128)(2,1)}, u32[]{:S(2)}) copy-start(bf16[16,64,512]{2,1,0:T(8,128)(2,1)} %get-tuple-element.26) | copy-start | bytes 3145732
  279.2 1.6 copy-start.1
  280.8 1.1 copy-start.3
  281.9 1.1 copy-start.2
  283.0 1.0 copy-start.4

commit v2 on v1

--- a/solution.py
+++ b/solution.py
@@ -2,6 +2,7 @@
 
 import jax
 import jax.numpy as jnp
+import numpy as np
 from jax import lax
 from jax.experimental import pallas as pl
 from jax.experimental.pallas import tpu as pltpu
@@ -417,9 +418,9 @@
 
 class Net:
     def __init__(self, send_sems, recv_sems):
-        self.send_sems, self.recv_sems, self.copies = send_sems, recv_sems, []
-
-    def send(self, source, target, device):
+        self.send_sems, self.recv_sems, self.copies, self.left = send_sems, recv_sems, [], set()
+
+    def make(self, source, target, device, sends=None):
         at = len(self.copies)
         copy = pltpu.make_async_remote_copy(
             src_ref=source,
@@ -429,65 +430,162 @@
             device_id=device,
             device_id_type=MESH,
         )
+        self.copies.append((copy, sends))
+        return copy
+
+    def send(self, source, target, device):
+        copy = self.make(source, target, device)
         copy.start()
-        self.copies.append(copy)
         return copy
 
-    def drain(self):
-        for copy in self.copies:
-            copy.wait_send()
+    def drain(self, among=None):
+        for at, (copy, sends) in enumerate(self.copies):
+            if at in self.left or (among is not None and at not in among):
+                continue
+            self.left.add(at)
+            if sends is None:
+                copy.wait_send()
+            else:
+                pl.when(sends)(copy.wait_send)
+
+
+class Line:
+    def __init__(self, net, z, nz, device):
+        self.net, self.z, self.nz, self.device = net, z, nz, device
+
+    def both(self):
+        z, nz = self.z, self.nz
+        right, left = self.device(lax.min(z + 1, nz - 1)), self.device(lax.max(z - 1, 0))
+        return ((z, right), (nz - 1 - z, left))
+
+    def pass_on(self, step, views):
+        copies = []
+        for way, (rank, target) in enumerate(self.both()):
+            sends = (rank >= step) & (rank < self.nz - 1)
+            arrives = rank >= step + 1
+            block = lax.clamp(0, self.z - step if way == 0 else self.z + step, self.nz - 1)
+            for view in views:
+                copy = self.net.make(view(block), view(block), target, sends)
+                pl.when(sends)(copy.start)
+                copies.append((copy, arrives))
+        return copies
+
+    def add_on(self, step, own, out, into):
+        copies = []
+        for way, (rank, target) in enumerate(self.both()):
+            sends = rank <= step
+            arrives = (rank >= 1) & (rank - 1 <= step)
+            dest = self.nz - 1 - step + rank
+            dest = lax.clamp(0, dest if way == 0 else self.nz - 1 - dest, self.nz - 1)
+            copy = self.net.make(out(way, step), into(way, step), target, sends)
+
+            def prepare():
+                out(way, step)[...] = own(dest)[...].astype(bf16)
+                if step > 0:
+
+                    def add():
+                        out(way, step)[...] = (own(dest)[...] + into(way, step - 1)[...].astype(f32)).astype(bf16)
+
+                    pl.when(rank >= 1)(add)
+                copy.start()
+
+            pl.when(sends)(prepare)
+            copies.append((copy, arrives))
+        return copies
+
+    def finish(self, total, into):
+        for way, (rank, target) in enumerate(self.both()):
+
+            def add():
+                total[...] += into(way, self.nz - 2)[...].astype(f32)
+
+            pl.when(rank >= 1)(add)
+
+
+def arrive(copies):
+    for copy, arrives in copies:
+        pl.when(arrives)(copy.wait_recv)
 
 
 def layer_kernel(
     dims,
-    x_ref, g_ref, wp_ref, sm_ref, wo_ref, wg_ref, wu_ref, wd_ref, dl_ref, ec_ref, fr_ref,
+    x_ref, g_ref, wq_ref, wk_ref, wv_ref, wo_ref, ga_ref, ge_ref, rt_ref, wg_ref, wu_ref, wd_ref, dl_ref, ec_ref,
+    fr_ref,
     block_out, input_grad, small_out, gain_out, dqkv_out, dwo_out, dgu_out, dd_out,
-    X, WQ, WO, SMB, SMW, N1, CT, ST, SEGC, POSC, Q, K, V, PSC, ATT, AT, PP, PR, RES,
+    WP, SMT, X, WQ, WO, SMB, SMW, N1, CT, ST, SEGC, POSC, Q, K, V, PSC, ATT, AT, PP, PR, RES,
     N2, GTB, GA, WGU, WD, AA, PSX, GC, H, UG, PRD, MP, MR, BP, BR, DGU, DDT, GDS, GD,
-    RB, RM, TB, RB2, TM, RM2, BOWN, MOWN, DGB, GUL, DDB, DDL, SG, RSG, GRES, RL,
-    AGS, AGR, DWO, RWO, ZWO, LWO, DS, DQ, DQKV, NG, NR, NZ, DWQ, RWQ, ZWQ, LWQ,
-    SG1, RSG1, EXB, EXG,
+    RB, RM, BOWN, MOWN, CO, CI, MO, MI, DGB, GUL, DDB, DDL, SG, SGF, SGT, SGZ, SGP, GRES, RL,
+    AGS, AGR, DWO, RWO, ZWO, LWO, DS, DQ, DQKV, NG, NR, DWQ, RWQ, ZWQ, LWQ,
+    SG1, SG1P, RSG1, EXB, EXG,
     send_sems, recv_sems, local_sems,
 ):
     nf, nz, hb, width, experts, half_ff, ndoc, chosen = dims
     rows = 2 * nz * hb
     half = nz * hb
     block = 2 * hb
+    shard = width // (nf * nz)
     f, z, c = lax.axis_index("fsdp"), lax.axis_index("ctx"), lax.axis_index("tp")
     other = 1 - c
     own = f * nz + z
     net = Net(send_sems, recv_sems)
     device = lambda df, dz, core: {"fsdp": df, "ctx": dz, "tp": core}
     partner = device(f, z, other)
+    line = Line(net, z, nz, lambda dz: device(f, dz, c))
     zs = [lax.rem(z + k, nz) for k in range(nz)]
     zback = [lax.rem(z + nz - k, nz) for k in range(nz)]
-    fs = [lax.rem(f + k, nf) for k in range(nf)]
-    fback = [lax.rem(f + nf - k, nf) for k in range(nf)]
+    fs = [f, f + 1 - 2 * lax.rem(f, 2), lax.rem(f + 2, 4), 3 - f]
     everyone = [(i, j, k) for k in range(2) for i in range(nf) for j in range(nz) if (i, j, k) != (0, 0, 0)]
     others = [device(fs[i], zs[j], lax.rem(c + k, 2)) for i, j, k in everyone]
+    same = [(i, j) for j in range(nz) for i in range(nf) if (i, j) != (0, 0)]
+
     mine = pl.ds(pl.multiple_of(c * hb, hb), hb)
-    yours = pl.ds(pl.multiple_of(other * hb, hb), hb)
-
+    loads = [
+        pltpu.make_async_copy(x_ref.at[mine], X.at[c, z], local_sems.at[0]),
+        pltpu.make_async_copy(g_ref.at[mine], GA.at[f, c, z], local_sems.at[1]),
+        pltpu.make_async_copy(wo_ref, WO.at[f, z], local_sems.at[2]),
+        pltpu.make_async_copy(wg_ref.at[own], WGU.at[own, :, pl.ds(0, half_ff)], local_sems.at[3]),
+        pltpu.make_async_copy(wu_ref.at[own], WGU.at[own, :, pl.ds(half_ff, half_ff)], local_sems.at[4]),
+        pltpu.make_async_copy(wd_ref.at[own], WD.at[own], local_sems.at[5]),
+    ]
+    for copy in loads:
+        copy.start()
     barrier = pltpu.get_barrier_semaphore()
     for peer in others:
         pl.semaphore_signal(barrier, inc=1, device_id=peer, device_id_type=MESH)
+
+    for j in range(nz):
+        WP[j, :, 0 : 2 * HD] = wq_ref[:, 2 * HD * j : 2 * HD * (j + 1)]
+        WP[j, :, 2 * HD : 4 * HD] = jnp.concatenate(
+            [wk_ref[:, HD * j : HD * (j + 1)], wv_ref[:, HD * j : HD * (j + 1)]], axis=1
+        )
+    base = jnp.concatenate(
+        [ga_ref[...].astype(f32), ge_ref[...].astype(f32), jnp.zeros((14, shard), f32), rt_ref[...].astype(f32)],
+        axis=0,
+    )
+    in_half = (lax.broadcasted_iota(jnp.int32, (32, 128), 1) < shard) == (lax.rem(z, 2) == 0)
+    SMT[...] = jnp.where(in_half, jnp.concatenate([base, base], axis=1), 0.0).astype(bf16)
+    SMB[f, z] = SMT[...]
+    WQ[f, z] = WP[z]
     pl.semaphore_wait(barrier, len(others))
 
-    sends_x = [net.send(x_ref.at[mine], X.at[c, z], device(f, zs[k], c)) for k in range(1, nz)]
-    sends_q = [net.send(wp_ref.at[zs[k]], WQ.at[f, z], device(f, zs[k], c)) for k in range(1, nz)]
-    sends_s = [
-        net.send(sm_ref, SMB.at[f, z], device(fs[i], zs[j], c))
-        for i in range(nf) for j in range(nz) if (i, j) != (0, 0)
-    ]
-    X[0, z] = x_ref[0:hb]
-    X[1, z] = x_ref[hb:block]
-    WQ[f, z] = wp_ref[z]
-    SMB[f, z] = sm_ref[...]
-    sends_o = [net.send(wo_ref, WO.at[f, z], device(f, zs[k], c)) for k in range(1, nz)]
-    WO[f, z] = wo_ref[...]
-    sends_g = [net.send(g_ref.at[mine], GA.at[f, c, z], device(f, zs[k], c)) for k in range(1, nz)]
-    GA[f, 0, z] = g_ref[0:hb]
-    GA[f, 1, z] = g_ref[hb:block]
+    sends_q = [net.send(WP.at[zs[k]], WQ.at[f, z], device(f, zs[k], c)) for k in range(1, nz)]
+    loads[0].wait()
+    view_x = [lambda at: X.at[c, at]]
+    chain_x = line.pass_on(0, view_x)
+    sends_s = [net.send(SMT, SMB.at[f, z], device(f, zs[k], c)) for k in range(1, nz)]
+    loads[2].wait()
+    view_o = [lambda at: WO.at[f, at]]
+    chain_o = line.pass_on(0, view_o)
+    weights = []
+
+    def send_weights(count):
+        for i, j in same[len(weights) // 3 : len(weights) // 3 + count]:
+            e, to = fs[i] * nz + zs[j], device(fs[i], zs[j], c)
+            weights.append(net.send(wg_ref.at[e], WGU.at[own, :, pl.ds(0, half_ff)], to))
+            weights.append(net.send(wu_ref.at[e], WGU.at[own, :, pl.ds(half_ff, half_ff)], to))
+            weights.append(net.send(wd_ref.at[e], WD.at[own], to))
+
+    send_weights(nf - 1)
 
     def places(shape, dim):
         at = lax.broadcasted_iota(jnp.int32, shape, dim)
@@ -506,61 +604,54 @@
             start = start + after * length
         return segment, position - start
 
-    pos_col = places((rows, 1), 0)
-    seg_col, offset = layout(pos_col)
-    POSC[...] = pos_col
-    SEGC[...] = seg_col
-    angle = offset.astype(f32) * fr_ref[0:1, :]
     lane = lax.broadcasted_iota(jnp.int32, (1, 2 * HD), 1)
     former = lax.rem(lane, HD) < HD // 2
-    CT[...] = jnp.cos(angle)
-    ST[...] = jnp.where(former, -1.0, 1.0) * jnp.sin(angle)
-    pos_row = places((1, rows), 1)
-    seg_row, unused = layout(pos_row)
     is_key = lane < HD
+
+    with jax.named_scope("tables0"):
+        pos_col = places((rows, 1), 0)
+        seg_col, offset = layout(pos_col)
+        POSC[...] = pos_col
+        SEGC[...] = seg_col
+        pos_row = places((1, rows), 1)
+        seg_row, unused = layout(pos_row)
 
     def swapped(v):
         return jnp.where(former, pltpu.roll(v, 2 * HD - HD // 2, 1), pltpu.roll(v, HD // 2, 1))
 
-    for k in range(1, nz):
-        sends_q[k - 1].wait_recv()
+    for copy in sends_q:
+        copy.wait_recv()
     sends_q2 = [net.send(WQ.at[f], WQ.at[f], device(fs[k], z, c)) for k in range(1, nf)]
-    forwards_x = []
-    for k in range(1, nz):
-        sends_x[k - 1].wait_recv()
-        forwards_x.append(net.send(X.at[c, zback[k]], X.at[c, zback[k]], partner))
-
-    sends_e = []
-    for i in range(nf):
-        for j in range(nz):
-            if (i, j) != (0, 0):
-                e = fs[i] * nz + zs[j]
-                to = device(fs[i], zs[j], c)
-                sends_e.append(net.send(wg_ref.at[e], WGU.at[own, :, pl.ds(0, half_ff)], to))
-                sends_e.append(net.send(wu_ref.at[e], WGU.at[own, :, pl.ds(half_ff, half_ff)], to))
-                sends_e.append(net.send(wd_ref.at[e], WD.at[own], to))
-    locals_e = [
-        pltpu.make_async_copy(wg_ref.at[own], WGU.at[own, :, pl.ds(0, half_ff)], local_sems.at[0]),
-        pltpu.make_async_copy(wu_ref.at[own], WGU.at[own, :, pl.ds(half_ff, half_ff)], local_sems.at[1]),
-        pltpu.make_async_copy(wd_ref.at[own], WD.at[own], local_sems.at[2]),
-    ]
-    for copy in locals_e:
-        copy.start()
-
+    arrive(chain_x)
+    chain_x = line.pass_on(1, view_x)
+    loads[1].wait()
+    view_g = [lambda at: GA.at[f, c, at]]
+    chain_g = line.pass_on(0, view_g)
     for copy in sends_s:
+        copy.wait_recv()
+    sends_s2 = [net.send(SMB.at[f], SMB.at[f], device(fs[k], z, c)) for k in range(1, nf)]
+    with jax.named_scope("tables1"):
+        angle = offset.astype(f32) * fr_ref[0:1, :]
+        CT[...] = jnp.cos(angle)
+    arrive(chain_x)
+    chain_x = line.pass_on(2, view_x)
+    arrive(chain_o)
+    chain_o = line.pass_on(1, view_o)
+    with jax.named_scope("tables2"):
+        ST[...] = jnp.where(former, -1.0, 1.0) * jnp.sin(angle)
+    arrive(chain_x)
+    forward_x = net.send(X.at[c], X.at[c], partner)
+    arrive(chain_g)
+    chain_g = line.pass_on(1, view_g)
+    for copy in sends_s2:
         copy.wait_recv()
     for pair in range(nf * nz // 2):
         at_f, at_z = pair // (nz // 2), 2 * (pair % (nz // 2))
         SMW[:, 128 * pair : 128 * pair + 128] = SMB[at_f, at_z] + SMB[at_f, at_z + 1]
-    gain_one = SMW[0:1, :].astype(f32)
-    gain_two = SMW[1:2, :].astype(f32)
-
-    for copy in sends_o:
-        copy.wait_recv()
-    sends_o2 = [net.send(WO.at[f], WO.at[f], device(fs[k], z, c)) for k in range(1, nf)]
-
-    for copy in forwards_x:
-        copy.wait_recv()
+    arrive(chain_o)
+    chain_o = line.pass_on(2, view_o)
+    send_weights(2)
+    forward_x.wait_recv()
 
     def norm_chunk(i, carry):
         at_c, at_z = lax.div(i, nz), lax.rem(i, nz)
@@ -572,14 +663,19 @@
     lax.fori_loop(0, 2 * nz, norm_chunk, 0)
     for copy in sends_q2:
         copy.wait_recv()
-    wq_full = WQ[...].reshape(width, 4 * HD)
-    projected = dot_nn(N1[...], wq_full)
-    cosine, sine = CT[...], ST[...]
-    q_part, kv_part = projected[:, : 2 * HD], projected[:, 2 * HD :]
-    Q[...] = (q_part * cosine + swapped(q_part) * sine).astype(bf16)
-    kv = jnp.where(is_key, kv_part * cosine + swapped(kv_part) * sine, kv_part).astype(bf16)
-    K[...] = kv[:, :HD]
-    V[...] = kv[:, HD:]
+    with jax.named_scope("qkv"):
+        projected = dot_nn(N1[...], WQ[...].reshape(width, 4 * HD))
+        cosine, sine = CT[...], ST[...]
+        q_part, kv_part = projected[:, : 2 * HD], projected[:, 2 * HD :]
+        Q[...] = (q_part * cosine + swapped(q_part) * sine).astype(bf16)
+        kv = jnp.where(is_key, kv_part * cosine + swapped(kv_part) * sine, kv_part).astype(bf16)
+        K[...] = kv[:, :HD]
+        V[...] = kv[:, HD:]
+    arrive(chain_g)
+    chain_g = line.pass_on(2, view_g)
+    arrive(chain_o)
+    sends_o2 = [net.send(WO.at[f], WO.at[f], device(fs[k], z, c)) for k in range(1, nf)]
+    send_weights(1)
 
     scale = HD ** (-0.5)
     step = 2 * hb
@@ -596,73 +692,87 @@
             weights = jnp.where(mask, jnp.exp(scores - peak), 0.0)
             total = jnp.sum(weights, axis=1, keepdims=True)
             pieces.append(dot_nn(weights.astype(bf16), V[...]) / total)
-            PSC[r, at, :] = weights / total
+            PSC[r, at, :] = (weights / total).astype(bf16)
         out = jnp.concatenate(pieces, axis=1).astype(bf16)
         at_c, at_z = lax.div(2 * i, nz), lax.rem(2 * i, nz)
         ATT[at_c, pl.ds(at_z, 2)] = out.reshape(2, hb, 2 * HD)
         return carry
 
-    lax.fori_loop(0, rows // step, attend, 0)
+    with jax.named_scope("attend"):
+        lax.fori_loop(0, rows // step, attend, 0)
     columns = pl.ds(pl.multiple_of(z * 2 * HD, 2 * HD), 2 * HD)
     sends_a = [
         net.send(ATT.at[:, zs[k]], AT.at[:, :, columns], device(f, zs[k], c)) for k in range(1, nz)
     ]
     AT[:, :, columns] = ATT[:, z]
-
-    for copy in sends_g:
+    send_weights(3)
+
+    arrive(chain_g)
+    sends_g2 = [net.send(GA.at[f, c], GA.at[f, c], device(fs[k], z, c)) for k in range(1, nf)]
+    forward_g = net.send(GA.at[f, c], GA.at[f, c], partner)
+
+    for copy in sends_a:
         copy.wait_recv()
-    sends_g2 = [net.send(GA.at[f, c], GA.at[f, c], device(fs[k], z, c)) for k in range(1, nf)]
-    forwards_g = [net.send(GA.at[f, c, zback[k]], GA.at[f, c, zback[k]], partner) for k in range(1, nz)]
-
     for copy in sends_o2:
         copy.wait_recv()
-    for copy in sends_a:
-        copy.wait_recv()
-    part = dot_nt(AT[...].reshape(block, nz * 2 * HD), WO[...].reshape(width, nz * 2 * HD))
-    PP[...] = part.reshape(2, hb, width)
+    with jax.named_scope("proj"):
+        part = dot_nt(AT[...].reshape(block, nz * 2 * HD), WO[...].reshape(width, nz * 2 * HD))
+        PP[...] = part.reshape(2, hb, width)
     send_p = net.send(PP.at[other], PR, partner)
-    x_own = x_ref[mine, :].astype(f32)
+    x_own = X[c, z].astype(f32)
+    gain_two = SMW[1:2, :].astype(f32)
     send_p.wait_recv()
     residual = x_own + PP[c] + PR[...]
     RES[...] = residual
     inverse_two = lax.rsqrt(jnp.mean(residual * residual, axis=1, keepdims=True) + epsilon)
     N2[f, c, z] = (residual * inverse_two * gain_two).astype(bf16)
-    sends_n = [net.send(N2.at[f, c, z], N2.at[f, c, z], device(f, zs[k], c)) for k in range(1, nz)]
     normed_two = N2[f, c, z]
     logits = dot_nt(SMW[16 : 16 + experts, :], normed_two)
     expert_at = lax.broadcasted_iota(jnp.int32, (experts, hb), 0)
+    route = ec_ref[...]
+    route = jnp.where(c == 0, route, pltpu.roll(route, 128 - hb, 1))
     picked = jnp.zeros((experts, hb), jnp.bool_)
     for j in range(chosen):
-        picked = picked | (ec_ref[j : j + 1, 0:hb] == expert_at)
+        picked = picked | (route[j : j + 1, 0:hb] == expert_at)
     peak = jnp.max(jnp.where(picked, logits, masked_score), axis=0, keepdims=True)
     weight = jnp.where(picked, jnp.exp(logits - peak), 0.0)
     gates = weight / jnp.sum(weight, axis=0, keepdims=True)
     GTB[f, c, z] = jnp.concatenate([gates, jnp.zeros((experts, 128 - hb), f32)], axis=1)
-    sends_t = [
-        net.send(GTB.at[f, c, z], GTB.at[f, c, z], device(fs[i], zs[j], lax.rem(c + k, 2)))
-        for i, j, k in everyone
-    ]
-
-    for copy in locals_e:
-        copy.wait()
-    for copy in sends_e:
-        copy.wait_recv()
-    for copy in forwards_g:
-        copy.wait_recv()
+    view_n = [lambda at: N2.at[f, c, at], lambda at: GTB.at[f, c, at]]
+    chain_n = line.pass_on(0, view_n)
+    send_weights(2)
+
     wd_full = lambda: WD[...].reshape(width, half_ff)
     wgu_full = lambda: WGU[...].reshape(width, 2 * half_ff)
-    AA[f] = dot_nn(GA[f].reshape(rows, width), wd_full())
-
-    for copy in sends_n:
-        copy.wait_recv()
-    sends_n2 = [net.send(N2.at[f, c], N2.at[f, c], device(fs[k], z, c)) for k in range(1, nf)]
-    forwards_n = [net.send(N2.at[f, c], N2.at[f, c], partner)]
     forwards_g2 = []
     for k in range(1, nf):
         sends_g2[k - 1].wait_recv()
-        forwards_g2.append(net.send(GA.at[fback[k], c], GA.at[fback[k], c], partner))
-    for copy in sends_t:
+        forwards_g2.append(net.send(GA.at[fs[k], c], GA.at[fs[k], c], partner))
+    arrive(chain_n)
+    chain_n = line.pass_on(1, view_n)
+    send_weights(2)
+    arrive(chain_n)
+    chain_n = line.pass_on(2, view_n)
+    send_weights(nf * nz)
+    arrive(chain_n)
+
+    def second_hop(ref, at_f, to):
+        return [net.send(ref.at[at_f, c], ref.at[at_f, c], to)]
+
+    sends_n2 = [
+        [net.send(N2.at[f, c], N2.at[f, c], device(fs[k], z, c)), net.send(GTB.at[f, c], GTB.at[f, c], device(fs[k], z, c))]
+        for k in range(1, nf)
+    ]
+    forwards_n = [
+        [net.send(N2.at[f, c], N2.at[f, c], partner), net.send(GTB.at[f, c], GTB.at[f, c], partner)]
+    ]
+    for copy in loads[3:]:
+        copy.wait()
+    for copy in weights:
         copy.wait_recv()
+    forward_g.wait_recv()
+    with jax.named_scope("cotangent"):
+        AA[f] = dot_nn(GA[f].reshape(rows, width), wd_full())
 
     chosen_row = jnp.where(
         lax.broadcasted_iota(jnp.int32, (experts, 128), 0) == own, 1.0, 0.0
@@ -673,18 +783,25 @@
     exchange_b, exchange_m = [], []
 
     for k in range(nf):
-        at_f = fback[k]
+        at_f = fs[k]
         if k > 0:
             forwards_g2[k - 1].wait_recv()
-            AA[at_f] = dot_nn(GA[at_f].reshape(rows, width), wd_full())
-            sends_n2[k - 1].wait_recv()
-            forwards_n.append(net.send(N2.at[at_f, c], N2.at[at_f, c], partner))
-        forwards_n[k].wait_recv()
+            with jax.named_scope("cotangent"):
+                AA[at_f] = dot_nn(GA[at_f].reshape(rows, width), wd_full())
+            for copy in sends_n2[k - 1]:
+                copy.wait_recv()
+            forwards_n.append(
+                [net.send(N2.at[at_f, c], N2.at[at_f, c], partner), net.send(GTB.at[at_f, c], GTB.at[at_f, c], partner)]
+            )
+        for copy in forwards_n[k]:
+            copy.wait_recv()
         tokens = N2[at_f].reshape(rows, width)
-        PSX[...] = dot_nn(tokens, wgu_full())
-        for piece in range(2 * nz):
-            tile = GTB[at_f, piece // nz, piece % nz][:, 0:hb]
-            GC[piece * hb : (piece + 1) * hb, :] = dot_tn(tile, chosen_row, lax.Precision.HIGHEST)
+        with jax.named_scope("gateup"):
+            PSX[...] = dot_nn(tokens, wgu_full())
+        with jax.named_scope("gatecol"):
+            for piece in range(2 * nz):
+                tile = GTB[at_f, piece // nz, piece % nz][:, 0:hb]
+                GC[piece * hb : (piece + 1) * hb, :] = dot_tn(tile, chosen_row, lax.Precision.HIGHEST)
 
         def expert_chunk(i, carry):
             at = pl.ds(pl.multiple_of(i * 32, 32), 32)
@@ -704,54 +821,56 @@
             UG[at, half_ff : 2 * half_ff] = (grad * silu).astype(bf16)
             return carry
 
-        lax.fori_loop(0, rows // 32, expert_chunk, 0)
-        BP[at_f] = dot_nt(UG[...], wgu_full()).astype(bf16).reshape(2, nz, hb, width)
+        with jax.named_scope("chunk"):
+            lax.fori_loop(0, rows // 32, expert_chunk, 0)
+        with jax.named_scope("back"):
+            BP[at_f] = dot_nt(UG[...], wgu_full()).astype(bf16).reshape(2, nz, hb, width)
         exchange_b.append(net.send(BP.at[at_f, other], BR.at[at_f], partner))
-        GDS[k] = dot_nt(jnp.ones((8, half_ff), bf16), PRD[...])
-        for j in range(nz):
-            for t in range(2):
-                if (k, j, t) != (0, 0, 0):
+        with jax.named_scope("gdot"):
+            GDS[k] = dot_nt(jnp.ones((8, half_ff), bf16), PRD[...])
+            for j in range(nz):
+                for t in range(2):
                     to_z, to_c = zs[j], lax.rem(c + t, 2)
                     lanes = pl.ds(pl.multiple_of((to_c * (nz // 2) + lax.div(to_z, 2)) * 128, 128), 128)
-                    sends_d.append(
-                        net.send(GDS.at[k, :, lanes], GD.at[f, z, c], device(at_f, to_z, to_c))
-                    )
-                else:
-                    lanes = pl.ds(pl.multiple_of((c * (nz // 2) + lax.div(z, 2)) * 128, 128), 128)
-                    GD[f, z, c] = GDS[0, :, lanes]
-        MP[at_f] = dot_nt(H[...], wd_full()).astype(bf16).reshape(2, nz, hb, width)
+                    if (k, j, t) != (0, 0, 0):
+                        sends_d.append(
+                            net.send(GDS.at[k, pl.ds(0, 1), lanes], GD.at[f, z, c, pl.ds(0, 1)], device(at_f, to_z, to_c))
+                        )
+                    else:
+                        GD[f, z, c] = GDS[0, :, lanes]
+        with jax.named_scope("mix"):
+            MP[at_f] = dot_nt(H[...], wd_full()).astype(bf16).reshape(2, nz, hb, width)
         exchange_m.append(net.send(MP.at[at_f, other], MR.at[at_f], partner))
         exchange_b[k].wait_recv()
         if k == 0:
             BOWN[...] = BP[at_f, c].astype(f32) + BR[at_f].astype(f32)
         else:
             BP[at_f, c] = (BP[at_f, c].astype(f32) + BR[at_f].astype(f32)).astype(bf16)
-            sends_b.append(net.send(BP.at[at_f, c], RB.at[f], device(at_f, z, c)))
-        DGU[...] += dot_tn(UG[...], tokens)
-        DDT[...] += dot_tn(H[...], GA[at_f].reshape(rows, width))
+            sends_b.append(net.send(BP.at[at_f, c], RB.at[k - 1], device(at_f, z, c)))
+        with jax.named_scope("wgrad"):
+            DGU[...] += dot_tn(UG[...], tokens)
+            DDT[...] += dot_tn(H[...], GA[at_f].reshape(rows, width))
         exchange_m[k].wait_recv()
         if k == 0:
             MOWN[...] = MP[at_f, c].astype(f32) + MR[at_f].astype(f32)
         else:
             MP[at_f, c] = (MP[at_f, c].astype(f32) + MR[at_f].astype(f32)).astype(bf16)
-            sends_m.append(net.send(MP.at[at_f, c], RM.at[f], device(at_f, z, c)))
 
     for k in range(1, nf):
-        sends_b[k - 1].wait_recv()
-        source = lax.rem(f + k, nf)
-        BOWN[...] += RB[source].astype(f32)
-    TB[...] = BOWN[...].astype(bf16)
-    sends_b2 = [net.send(TB.at[zs[k]], RB2.at[z], device(f, zs[k], c)) for k in range(1, nz)]
-
-    DGB[...] = jnp.transpose(DGU[...]).astype(bf16).reshape(nf, nz, width // (nf * nz), 2 * half_ff)
-    DDB[...] = jnp.transpose(DDT[...]).astype(bf16).reshape(nf, nz, width // (nf * nz), half_ff)
-    sends_w = []
-    for i in range(nf):
-        for j in range(nz):
-            if (i, j) != (0, 0):
-                to = device(fs[i], zs[j], c)
-                sends_w.append(net.send(DGB.at[fs[i], zs[j]], GUL.at[own], to))
-                sends_w.append(net.send(DDB.at[fs[i], zs[j]], DDL.at[own], to))
+        sends_m.append(net.send(MP.at[fs[k], c], RM.at[k - 1], device(fs[k], z, c)))
+    with jax.named_scope("transpose"):
+        DGB[...] = jnp.transpose(DGU[...]).astype(bf16).reshape(nf, nz, shard, 2 * half_ff)
+        DDB[...] = jnp.transpose(DDT[...]).astype(bf16).reshape(nf, nz, shard, half_ff)
+    grads_at = []
+    far = same[nf - 1 :] + same[: nf - 1]
+
+    def send_grads(count):
+        for i, j in far[len(grads_at) // 2 : len(grads_at) // 2 + count]:
+            to = device(fs[i], zs[j], c)
+            grads_at.append(net.send(DGB.at[fs[i], zs[j]], GUL.at[own], to))
+            grads_at.append(net.send(DDB.at[fs[i], zs[j]], DDL.at[own], to))
+
+    send_grads(2)
     GUL[own] = DGB[f, z]
     DDL[own] = DDB[f, z]
 
@@ -764,22 +883,32 @@
         ],
         axis=0,
     )
-    dots = jnp.where(lax.rem(z, 2) == 0, dots, pltpu.roll(dots, 64, 1))[:, 0:hb]
+    dots = jnp.where(lax.rem(z, 2) == 0, dots, pltpu.roll(dots, 128 - hb, 1))[:, 0:hb]
     gates = GTB[f, c, z][:, 0:hb]
     logit_grad = gates * (dots - jnp.sum(gates * dots, axis=0, keepdims=True))
     router_t = SMW[16 : 16 + experts, :].astype(f32)
-    router_term = dot_nn(logit_grad, N2[f, c, z].astype(f32), lax.Precision.HIGHEST)
-    router_input = dot_tn(logit_grad, router_t, lax.Precision.HIGHEST)
-    moe = BOWN[z]
-    for k in range(1, nz):
-        sends_b2[k - 1].wait_recv()
-        moe = moe + RB2[zback[k]].astype(f32)
-    grad_two = moe + router_input
+    SG[0:experts, :] = dot_nn(logit_grad, N2[f, c, z].astype(f32), lax.Precision.HIGHEST)
+    GRES[...] = dot_tn(logit_grad, router_t, lax.Precision.HIGHEST)
     residual = RES[...]
     inverse_two = lax.rsqrt(jnp.mean(residual * residual, axis=1, keepdims=True) + epsilon)
+
+    for k in range(1, nf):
+        sends_b[k - 1].wait_recv()
+        BOWN[...] += RB[k - 1].astype(f32)
+    own_b, out_b, into_b = (lambda at: BOWN.at[at]), (lambda w, t: CO.at[w, t]), (lambda w, t: CI.at[w, t])
+    sums = []
+    for t in range(nz - 1):
+        at_sums = len(net.copies)
+        chain_b = line.add_on(t, own_b, out_b, into_b)
+        sums.extend(range(at_sums, len(net.copies)))
+        send_grads(1)
+        arrive(chain_b)
+    line.finish(BOWN.at[z], into_b)
+
+    grad_two = BOWN[z] + GRES[...]
     scaled = grad_two * gain_two
     grad_res = (
-        g_ref[mine, :].astype(f32)
+        GA[f, c, z].astype(f32)
         + inverse_two * scaled
         - residual * (inverse_two * inverse_two * inverse_two) * jnp.mean(scaled * residual, axis=1, keepdims=True)
     )
@@ -787,17 +916,14 @@
     RL[c] = grad_res.astype(bf16)
     send_r = net.send(RL.at[c], RL.at[c], partner)
     gain_term = jnp.sum(grad_two * residual * inverse_two, axis=0, keepdims=True)
-    SG[0:experts, :] = router_term
     SG[experts : experts + 8, :] = jnp.broadcast_to(gain_term, (8, width))
-    sends_sg = []
-    for (i, j, k), to in zip(everyone, others):
-        lanes = pl.ds(pl.multiple_of((fs[i] * (nz // 2) + lax.div(zs[j], 2)) * 128, 128), 128)
-        sends_sg.append(net.send(SG.at[:, lanes], RSG.at[f, z, c], to))
-    own_lanes = pl.ds(pl.multiple_of((f * (nz // 2) + lax.div(z, 2)) * 128, 128), 128)
-    RSG[f, z, c] = SG[:, own_lanes]
+    wide = width // nf
+    block_lanes = lambda at: pl.ds(pl.multiple_of(at * wide, 128), wide)
+    sends_sg = [net.send(SG.at[:, block_lanes(fs[k])], SGF.at[k - 1], device(fs[k], z, c)) for k in range(1, nf)]
     send_r.wait_recv()
     low = RL[...].reshape(block, width)
-    AGS[...] = dot_nn(low, WO[...].reshape(width, nz * 2 * HD)).astype(bf16).reshape(2, hb, nz * 2 * HD)
+    with jax.named_scope("attgrad"):
+        AGS[...] = dot_nn(low, WO[...].reshape(width, nz * 2 * HD)).astype(bf16).reshape(2, hb, nz * 2 * HD)
     sends_ag = [
         net.send(
             AGS.at[:, :, pl.ds(pl.multiple_of(zs[k] * 2 * HD, 2 * HD), 2 * HD)],
@@ -807,13 +933,14 @@
         for k in range(1, nz)
     ]
     AGR[:, z] = AGS[:, :, columns]
-    shard = width // (nf * nz)
-    DWO[...] = (
-        dot_tn(low, AT[...].reshape(block, nz * 2 * HD))
-        .astype(bf16)
-        .reshape(nf, nz, shard, nz * 2 * HD)
-    )
-    sends_wo = [net.send(DWO.at[fs[k]], RWO.at[f], device(fs[k], z, c)) for k in range(1, nf)]
+    send_grads(3)
+    with jax.named_scope("outgrad"):
+        DWO[...] = (
+            dot_tn(low, AT[...].reshape(block, nz * 2 * HD))
+            .astype(bf16)
+            .reshape(nf, nz, shard, nz * 2 * HD)
+        )
+    sends_wo = [net.send(DWO.at[fs[k]], RWO.at[k - 1], device(fs[k], z, c)) for k in range(1, nf)]
 
     for copy in sends_ag:
         copy.wait_recv()
@@ -828,70 +955,90 @@
         for r in range(2):
             delta = jnp.sum(both[:, r * HD : (r + 1) * HD], axis=1, keepdims=True)
             prob_grad = dot_nt(grad[:, r * HD : (r + 1) * HD], V[...])
-            probs = PSC[r, at, :]
+            probs = PSC[r, at, :].astype(f32)
             score_grad = (probs * (prob_grad - delta) * scale).astype(bf16)
             DS[r, at, :] = score_grad
             pieces.append(dot_nn(score_grad, K[...]))
         DQ[at, :] = jnp.concatenate(pieces, axis=1)
         return carry
 
-    lax.fori_loop(0, rows // step, backward, 0)
-    grads = AGR[...].reshape(rows, 2 * HD)
-    key_t = dot_tn(Q[:, 0:HD], DS[0]) + dot_tn(Q[:, HD : 2 * HD], DS[1])
-    value_t = dot_tn(grads[:, 0:HD], PSC[0].astype(bf16)) + dot_tn(
-        grads[:, HD : 2 * HD], PSC[1].astype(bf16)
-    )
-    kv_grad = jnp.transpose(jnp.concatenate([key_t, value_t], axis=0))
-    cosine, sine = CT[...], ST[...]
-    q_grad = DQ[...]
-    DQKV[:, 0 : 2 * HD] = (q_grad * cosine - swapped(q_grad) * sine).astype(bf16)
-    DQKV[:, 2 * HD : 4 * HD] = jnp.where(
-        is_key, kv_grad * cosine - swapped(kv_grad) * sine, kv_grad
-    ).astype(bf16)
-    NG[...] = dot_nt(DQKV[...], WQ[...].reshape(width, 4 * HD)).astype(bf16).reshape(2, nz, hb, width)
+    with jax.named_scope("attback"):
+        lax.fori_loop(0, rows // step, backward, 0)
+    with jax.named_scope("kvgrad"):
+        grads = AGR[...].reshape(rows, 2 * HD)
+        key_t = dot_tn(Q[:, 0:HD], DS[0]) + dot_tn(Q[:, HD : 2 * HD], DS[1])
+        value_t = dot_tn(grads[:, 0:HD], PSC[0]) + dot_tn(grads[:, HD : 2 * HD], PSC[1])
+        kv_grad = jnp.transpose(jnp.concatenate([key_t, value_t], axis=0))
+        cosine, sine = CT[...], ST[...]
+        q_grad = DQ[...]
+        DQKV[:, 0 : 2 * HD] = (q_grad * cosine - swapped(q_grad) * sine).astype(bf16)
+        DQKV[:, 2 * HD : 4 * HD] = jnp.where(
+            is_key, kv_grad * cosine - swapped(kv_grad) * sine, kv_grad
+        ).astype(bf16)
+    with jax.named_scope("ingrad"):
+        NG[...] = dot_nt(DQKV[...], WQ[...].reshape(width, 4 * HD)).astype(bf16).reshape(2, nz, hb, width)
     send_ng = net.send(NG.at[other], NR, partner)
-    DWQ[...] = (
-        jnp.transpose(dot_tn(DQKV[...], N1[...])).astype(bf16).reshape(nf, nz, shard, 4 * HD)
-    )
+    with jax.named_scope("qkvgrad"):
+        DWQ[...] = (
+            jnp.transpose(dot_tn(DQKV[...], N1[...])).astype(bf16).reshape(nf, nz, shard, 4 * HD)
+        )
+    sends_wq = [net.send(DWQ.at[fs[k]], RWQ.at[k - 1], device(fs[k], z, c)) for k in range(1, nf)]
     send_ng.wait_recv()
-    NG[c] = (NG[c].astype(f32) + NR[...].astype(f32)).astype(bf16)
-    sends_nz = [net.send(NG.at[c, zs[k]], NZ.at[z], device(f, zs[k], c)) for k in range(1, nz)]
-    sends_wq = [net.send(DWQ.at[fs[k]], RWQ.at[f], device(fs[k], z, c)) for k in range(1, nf)]
+    BOWN[...] = NG[c].astype(f32) + NR[...].astype(f32)
+    net.drain(sums)
+    chain_g1 = line.add_on(0, own_b, out_b, into_b)
 
     for k in range(1, nf):
         sends_m[k - 1].wait_recv()
-        MOWN[...] += RM[lax.rem(f + k, nf)].astype(f32)
-    TM[...] = MOWN[...].astype(bf16)
-    sends_m2 = [net.send(TM.at[zs[k]], RM2.at[z], device(f, zs[k], c)) for k in range(1, nz)]
+        MOWN[...] += RM[k - 1].astype(f32)
+    own_m, out_m, into_m = (lambda at: MOWN.at[at]), (lambda w, t: MO.at[w, t]), (lambda w, t: MI.at[w, t])
+    chain_m = line.add_on(0, own_m, out_m, into_m)
+    arrive(chain_g1)
+    chain_g1 = line.add_on(1, own_b, out_b, into_b)
 
     total = DWO[f].astype(f32)
     for k in range(1, nf):
         sends_wo[k - 1].wait_recv()
-        total = total + RWO[fback[k]].astype(f32)
+        total = total + RWO[k - 1].astype(f32)
     ZWO[...] = total.astype(bf16)
     sends_wo2 = [net.send(ZWO.at[zs[k]], LWO.at[z], device(f, zs[k], c)) for k in range(1, nz)]
     LWO[z] = ZWO[z]
+    small = SG[:, block_lanes(f)]
+    for k in range(1, nf):
+        sends_sg[k - 1].wait_recv()
+        small = small + SGF[k - 1]
+    SGT[...] = small
+    pair_lanes = lambda at: pl.ds(pl.multiple_of(lax.div(at, 2) * 128, 128), 128)
+    sends_sz = [net.send(SGT.at[:, pair_lanes(zs[k])], SGZ.at[k - 1], device(f, zs[k], c)) for k in range(1, nz)]
+    arrive(chain_g1)
+    chain_g1 = line.add_on(2, own_b, out_b, into_b)
+    arrive(chain_m)
+    chain_m = line.add_on(1, own_m, out_m, into_m)
+
     total = DWQ[f].astype(f32)
     for k in range(1, nf):
         sends_wq[k - 1].wait_recv()
-        total = total + RWQ[fback[k]].astype(f32)
+        total = total + RWQ[k - 1].astype(f32)
     ZWQ[...] = total.astype(bf16)
     sends_wq2 = [net.send(ZWQ.at[zs[k]], LWQ.at[z], device(f, zs[k], c)) for k in range(1, nz)]
     LWQ[z] = ZWQ[z]
-
-    grad_one = NG[c, z].astype(f32)
+    send_grads(nf * nz)
+    small = SGT[:, pair_lanes(z)]
     for k in range(1, nz):
-        sends_nz[k - 1].wait_recv()
-        grad_one = grad_one + NZ[zback[k]].astype(f32)
-    x_own = x_ref[mine, :].astype(f32)
+        sends_sz[k - 1].wait_recv()
+        small = small + SGZ[k - 1]
+    SGP[0] = small
+    send_sp = net.send(SGP.at[0], SGP.at[1], partner)
+
+    arrive(chain_g1)
+    line.finish(BOWN.at[z], into_b)
+    grad_one = BOWN[z]
+    gain_one = SMW[0:1, :].astype(f32)
+    x_own = X[c, z].astype(f32)
     inverse = lax.rsqrt(jnp.mean(x_own * x_own, axis=1, keepdims=True) + epsilon)
     gain_term = jnp.sum(grad_one * x_own * inverse, axis=0, keepdims=True)
-    SG1[...] = jnp.broadcast_to(gain_term, (8, width))
-    sends_g1 = []
-    for (i, j, k), to in zip(everyone, others):
-        lanes = pl.ds(pl.multiple_of((fs[i] * (nz // 2) + lax.div(zs[j], 2)) * 128, 128), 128)
-        sends_g1.append(net.send(SG1.at[:, lanes], RSG1.at[f, z, c], to))
-    RSG1[f, z, c] = SG1[:, own_lanes]
+    SG1[0] = jnp.broadcast_to(gain_term, (8, width))
+    send_g1 = net.send(SG1.at[0], SG1.at[1], partner)
     scaled = grad_one * gain_one
     EXG[c] = (
         GRES[...]
@@ -899,45 +1046,47 @@
         - x_own * (inverse * inverse * inverse) * jnp.mean(scaled * x_own, axis=1, keepdims=True)
     )
     send_ig = net.send(EXG.at[c], EXG.at[c], partner)
-
-    mixed = MOWN[z]
-    for k in range(1, nz):
-        sends_m2[k - 1].wait_recv()
-        mixed = mixed + RM2[zback[k]].astype(f32)
-    EXB[c] = (RES[...] + mixed).astype(bf16)
-    send_bo = net.send(EXB.at[c], EXB.at[c], partner)
-
-    for copy in sends_sg:
-        copy.wait_recv()
-    small = jnp.zeros((experts + 8, 128), f32)
-    for i in range(nf):
-        for j in range(nz):
-            small = small + RSG[i, j, 0] + RSG[i, j, 1]
-    small_out[...] = small
+    send_g1.wait_recv()
+    SG1P[...] = SG1[0] + SG1[1]
+    lanes_of = lambda df, dz: pl.ds(pl.multiple_of((df * (nz // 2) + lax.div(dz, 2)) * 128, 128), 128)
+    sends_g1 = [
+        net.send(SG1P.at[pl.ds(0, 1), lanes_of(fs[i], zs[j])], RSG1.at[f, z, pl.ds(0, 1)], device(fs[i], zs[j], c))
+        for i, j in same
+    ]
+    RSG1[f, z] = SG1P[:, lanes_of(f, z)]
+
+    arrive(chain_m)
+    chain_m = line.add_on(2, own_m, out_m, into_m)
+    send_sp.wait_recv()
+    small_out[...] = SGP[0] + SGP[1]
     for copy in sends_wo2:
         copy.wait_recv()
     total = LWO[0].astype(f32)
     for j in range(1, nz):
         total = total + LWO[j].astype(f32)
     dwo_out[...] = total
+    arrive(chain_m)
+    line.finish(MOWN.at[z], into_m)
+    EXB[c] = (RES[...] + MOWN[z]).astype(bf16)
+    send_bo = net.send(EXB.at[c], EXB.at[c], partner)
     for copy in sends_wq2:
         copy.wait_recv()
     dqkv_out[...] = LWQ[...]
-    for copy in sends_w:
+    for copy in grads_at:
         copy.wait_recv()
     outs = [
-        pltpu.make_async_copy(GUL, dgu_out, local_sems.at[3]),
-        pltpu.make_async_copy(DDL, dd_out, local_sems.at[4]),
+        pltpu.make_async_copy(GUL, dgu_out, local_sems.at[6]),
+        pltpu.make_async_copy(DDL, dd_out, local_sems.at[7]),
     ]
     for copy in outs:
         copy.start()
     for copy in sends_g1:
         copy.wait_recv()
-    small = jnp.zeros((8, 128), f32)
+    small = jnp.zeros((1, 128), f32)
     for i in range(nf):
         for j in range(nz):
-            small = small + RSG1[i, j, 0] + RSG1[i, j, 1]
-    gain_out[...] = small
+            small = small + RSG1[i, j, 0:1]
+    gain_out[...] = jnp.broadcast_to(small, (8, 128))
     send_bo.wait_recv()
     block_out[...] = EXB[...].reshape(block, width)
     send_ig.wait_recv()
@@ -945,6 +1094,35 @@
     for copy in outs:
         copy.wait()
     net.drain()
+
+
+def finish_kernel(
+    dims, block_ref, input_ref, small_ref, gain_ref, dqkv_ref, dwo_ref, dgu_ref, dd_ref,
+    block_out, input_out, gain1_out, q_out, k_out, v_out, o_out, gain2_out, router_out, gate_out, up_out, down_out,
+):
+    nz, experts, half_ff, shard = dims
+    block_out[...] = block_ref[...]
+    input_out[...] = input_ref[...]
+    gate_out[...] = dgu_ref[:, :, 0:half_ff].astype(f32)
+    up_out[...] = dgu_ref[:, :, half_ff : 2 * half_ff].astype(f32)
+    down_out[...] = dd_ref[...].astype(f32)
+    even = lax.rem(lax.axis_index("ctx"), 2) == 0
+    pick = lambda v: jnp.where(even, v, pltpu.roll(v, 128 - shard, 1))[:, 0:shard]
+
+    def once():
+        gain1_out[...] = pick(gain_ref[...])[0:1]
+        small = pick(small_ref[...])
+        router_out[...] = small[0:experts]
+        gain2_out[...] = small[experts : experts + 1]
+        o_out[...] = dwo_ref[...]
+        for j in range(nz):
+            q_out[:, 2 * HD * j : 2 * HD * (j + 1)] = dqkv_ref[j, :, 0 : 2 * HD].astype(f32)
+        for at, ref in ((2, k_out), (3, v_out)):
+            ref[...] = jnp.concatenate(
+                [dqkv_ref[j, :, at * HD : (at + 1) * HD].astype(f32) for j in range(nz)], axis=1
+            )
+
+    pl.when(pl.program_id(0) == 0)(once)
 
 
 def fast_local(
@@ -957,36 +1135,20 @@
     experts, shard, half_ff = gate_weight.shape
     ndoc, chosen = doc_lengths.shape[1], expert_choice.shape[2]
     rows = nz * block
-    z, c = lax.axis_index("ctx"), lax.axis_index("tp")
-    packed = jnp.concatenate(
-        [
-            query_weight.reshape(shard, nz, 2 * HD),
-            key_weight.reshape(shard, nz, HD),
-            value_weight.reshape(shard, nz, HD),
-        ],
-        axis=2,
-    ).transpose(1, 0, 2)
-    base = jnp.concatenate(
-        [attention_gain[None], expert_gain[None], jnp.zeros((14, shard), bf16), router_weight.T], axis=0
-    )
-    blank = jnp.zeros_like(base)
-    even = lax.rem(z, 2) == 0
-    small = jnp.concatenate([jnp.where(even, base, blank), jnp.where(even, blank, base)], axis=1)
-    own_choice = lax.dynamic_slice_in_dim(expert_choice[0], c * hb, hb, axis=0)
-    route = jnp.concatenate([own_choice.T, jnp.zeros((chosen, 128 - hb), jnp.int32)], axis=1)
     halfway = HD // 2
-    frequency = rope_base ** (-jnp.arange(halfway, dtype=f32) / halfway)
-    frequency = jnp.broadcast_to(jnp.tile(frequency, 4)[None], (8, 2 * HD))
+    frequency = np.float32(rope_base) ** (-np.arange(halfway, dtype=np.float32) / np.float32(halfway))
+    frequency = jnp.asarray(np.tile(np.tile(frequency, 4)[None], (8, 1)).astype(np.float32))
 
     vm = pl.BlockSpec(memory_space=pltpu.VMEM)
     anywhere = pl.BlockSpec(memory_space=pl.ANY)
     shape = lambda s, d: jax.ShapeDtypeStruct(s, d)
     W = nz * 2 * HD
     scratch = dict(
+        WP=((nz, shard, 4 * HD), bf16), SMT=((32, 128), bf16),
         X=((2, nz, hb, width), bf16), WQ=((nf, nz, shard, 4 * HD), bf16), WO=((nf, nz, shard, W), bf16),
         SMB=((nf, nz, 32, 128), bf16), SMW=((32, width), bf16), N1=((rows, width), bf16),
         CT=((rows, 128), f32), ST=((rows, 128), f32), SEGC=((rows, 1), jnp.int32), POSC=((rows, 1), jnp.int32),
-        Q=((rows, 2 * HD), bf16), K=((rows, HD), bf16), V=((rows, HD), bf16), PSC=((2, rows, rows), f32),
+        Q=((rows, 2 * HD), bf16), K=((rows, HD), bf16), V=((rows, HD), bf16), PSC=((2, rows, rows), bf16),
         ATT=((2, nz, hb, 2 * HD), bf16), AT=((2, hb, W), bf16), PP=((2, hb, width), f32), PR=((hb, width), f32),
         RES=((hb, width), f32),
         N2=((nf, 2, nz, hb, width), bf16), GTB=((nf, 2, nz, experts, 128), f32), GA=((nf, 2, nz, hb, width), bf16),
@@ -997,27 +1159,26 @@
         BP=((nf, 2, nz, hb, width), bf16), BR=((nf, nz, hb, width), bf16),
         DGU=((2 * half_ff, width), f32), DDT=((half_ff, width), f32),
         GDS=((nf, 8, rows), f32), GD=((nf, nz, 2, 8, 128), f32),
-        RB=((nf, nz, hb, width), bf16),
-        RM=((nf, nz, hb, width), bf16),
-        TB=((nz, hb, width), bf16), RB2=((nz, hb, width), bf16),
-        TM=((nz, hb, width), bf16), RM2=((nz, hb, width), bf16),
+        RB=((nf - 1, nz, hb, width), bf16), RM=((nf - 1, nz, hb, width), bf16),
         BOWN=((nz, hb, width), f32), MOWN=((nz, hb, width), f32),
+        CO=((2, nz - 1, hb, width), bf16), CI=((2, nz - 1, hb, width), bf16),
+        MO=((2, nz - 1, hb, width), bf16), MI=((2, nz - 1, hb, width), bf16),
         DGB=((nf, nz, shard, 2 * half_ff), bf16), GUL=((nf * nz, shard, 2 * half_ff), bf16),
         DDB=((nf, nz, shard, half_ff), bf16), DDL=((nf * nz, shard, half_ff), bf16),
-        SG=((experts + 8, width), f32), RSG=((nf, nz, 2, experts + 8, 128), f32),
+        SG=((experts + 8, width), f32), SGF=((nf - 1, experts + 8, width // nf), f32),
+        SGT=((experts + 8, width // nf), f32), SGZ=((nz - 1, experts + 8, 128), f32), SGP=((2, experts + 8, 128), f32),
         GRES=((hb, width), f32), RL=((2, hb, width), bf16),
         AGS=((2, hb, W), bf16), AGR=((2, nz, hb, 2 * HD), bf16),
-        DWO=((nf, nz, shard, W), bf16), RWO=((nf, nz, shard, W), bf16),
+        DWO=((nf, nz, shard, W), bf16), RWO=((nf - 1, nz, shard, W), bf16),
         ZWO=((nz, shard, W), bf16), LWO=((nz, shard, W), bf16),
         DS=((2, rows, rows), bf16), DQ=((rows, 2 * HD), f32),
         DQKV=((rows, 4 * HD), bf16), NG=((2, nz, hb, width), bf16), NR=((nz, hb, width), bf16),
-        NZ=((nz, hb, width), bf16),
-        DWQ=((nf, nz, shard, 4 * HD), bf16), RWQ=((nf, nz, shard, 4 * HD), bf16),
+        DWQ=((nf, nz, shard, 4 * HD), bf16), RWQ=((nf - 1, nz, shard, 4 * HD), bf16),
         ZWQ=((nz, shard, 4 * HD), bf16), LWQ=((nz, shard, 4 * HD), bf16),
-        SG1=((8, width), f32), RSG1=((nf, nz, 2, 8, 128), f32),
+        SG1=((2, 8, width), f32), SG1P=((8, width), f32), RSG1=((nf, nz, 8, 128), f32),
         EXB=((2, hb, width), bf16), EXG=((2, hb, width), f32),
     )
-    slots = 400
+    slots = 320
     out = pl.pallas_call(
         functools.partial(layer_kernel, (nf, nz, hb, width, experts, half_ff, ndoc, chosen)),
         name="layer",
@@ -1026,34 +1187,48 @@
             shape((8, 128), f32), shape((nz, shard, 4 * HD), bf16), shape((shard, W), f32),
             shape((nf * nz, shard, 2 * half_ff), bf16), shape((nf * nz, shard, half_ff), bf16),
         ),
-        in_specs=[vm] * 5 + [anywhere] * 3 + [pl.BlockSpec(memory_space=pltpu.SMEM), vm, vm],
+        in_specs=[anywhere] * 2 + [vm] * 3 + [anywhere] + [vm] * 3 + [anywhere] * 3
+        + [pl.BlockSpec(memory_space=pltpu.SMEM), vm, vm],
         out_specs=(vm,) * 6 + (anywhere,) * 2,
         scratch_shapes=[pltpu.VMEM(s, d) for s, d in scratch.values()]
-        + [pltpu.SemaphoreType.DMA((slots,)), pltpu.SemaphoreType.DMA((slots,)), pltpu.SemaphoreType.DMA((5,))],
+        + [pltpu.SemaphoreType.DMA((slots,)), pltpu.SemaphoreType.DMA((slots,)), pltpu.SemaphoreType.DMA((8,))],
         compiler_params=pltpu.CompilerParams(
             collective_id=0, has_side_effects=True, vmem_limit_bytes=67043328
         ),
     )(
-        hidden_in[0], out_grad[0], packed, small, output_weight, gate_weight, up_weight, down_weight,
-        doc_lengths, route, frequency,
-    )
-    block_out, input_grad, small, gain, dqkv, dwo, dgu, dd = out
-    lanes = lambda v: jnp.where(even, v[:, :shard], v[:, shard:])
-    small, gain = lanes(small), lanes(gain)
-    dqkv = dqkv.astype(f32)
+        hidden_in[0], out_grad[0], query_weight, key_weight, value_weight, output_weight,
+        attention_gain[None], expert_gain[None], router_weight.T, gate_weight, up_weight, down_weight,
+        doc_lengths, expert_choice[0].T, frequency,
+    )
+    steps = nz
+    some = lambda *s: pl.BlockSpec(s, lambda i: (i,) + (0,) * (len(s) - 1))
+    whole = lambda *s: pl.BlockSpec(s, lambda i: (0,) * len(s))
+    per = nf * nz // steps
+    out = pl.pallas_call(
+        functools.partial(finish_kernel, (nz, experts, half_ff, shard)),
+        name="finish",
+        grid=(steps,),
+        out_shape=(
+            shape((block, width), bf16), shape((block, width), f32), shape((1, shard), f32),
+            shape((shard, nz * 2 * HD), f32), shape((shard, nz * HD), f32), shape((shard, nz * HD), f32),
+            shape((shard, W), f32), shape((1, shard), f32), shape((experts, shard), f32),
+            shape((experts, shard, half_ff), f32), shape((experts, shard, half_ff), f32),
+            shape((experts, shard, half_ff), f32),
+        ),
+        in_specs=[
+            some(block // steps, width), some(block // steps, width), whole(experts + 8, 128), whole(8, 128),
+            whole(nz, shard, 4 * HD), whole(shard, W), some(per, shard, 2 * half_ff), some(per, shard, half_ff),
+        ],
+        out_specs=(
+            some(block // steps, width), some(block // steps, width), whole(1, shard),
+            whole(shard, nz * 2 * HD), whole(shard, nz * HD), whole(shard, nz * HD), whole(shard, W), whole(1, shard),
+            whole(experts, shard), some(per, shard, half_ff), some(per, shard, half_ff), some(per, shard, half_ff),
+        ),
+        compiler_params=pltpu.CompilerParams(vmem_limit_bytes=33554432),
+    )(*out)
+    block_out, input_grad, gain1, q, k, v, o, gain2, router, gate, up, down = out
     return (
-        block_out[None],
-        input_grad[None],
-        gain[0],
-        dqkv[:, :, : 2 * HD].transpose(1, 0, 2).reshape(shard, -1),
-        dqkv[:, :, 2 * HD : 3 * HD].transpose(1, 0, 2).reshape(shard, -1),
-        dqkv[:, :, 3 * HD :].transpose(1, 0, 2).reshape(shard, -1),
-        dwo,
-        small[experts],
-        small[:experts].T,
-        dgu[:, :, :half_ff].astype(f32),
-        dgu[:, :, half_ff:].astype(f32),
-        dd.astype(f32),
+        block_out[None], input_grad[None], gain1[0], q, k, v, o, gain2[0], router.T, gate, up, down,
     )
 
 
@@ -1063,7 +1238,8 @@
     width, block = hidden.shape[2], hidden.shape[1] // nz
     return (
         nc == 2
-        and nz % 2 == 0
+        and nz == 4
+        and nf == 4
         and hidden.shape[0] == nf
         and gate.shape[0] == nf * nz
         and gate.shape[0] == 16

time: 285 us -> 234 us (0.82)
  Pallas kernels: 266 us -> 223 us
  other arithmetic: 6.17 us -> 0 us
  local copies, waits for them, and re-layouts: 11.7 us -> 7.44 us
    pallas_call x1, Pallas kernels: 266 us -> 220 us  [fast_local(): pl.pallas_call(functools.partial(layer_kernel, (nf, nz, hb, width, expert...]
    convert_element_type x3 -> x0, other arithmetic: 3.73 us -> none  [the longest x1 1.64 us: fast_local(): dgu[:, :, half_ff:].astype(f32)]
    reshape x8 -> x0, local copies, waits for them, and re-layouts: 3.19 us -> none  [the longest x2 0.87 us: fast_local(): value_weight.reshape(shard, nz, HD)]
    unnamed x27 -> x16, local copies, waits for them, and re-layouts: 5.73 us -> 7.44 us
where the time goes in v2:
time: 234 us; the launch traced here: 231 us
  Pallas kernels  223 us (95%)
  local copies, waits for them, and re-layouts  7.44 us (3%)
    pallas_call x1, Pallas kernels, fast_local(): pl.pallas_call(functools.partial(layer_kernel, (nf, nz, hb, width, expert...  220 us
    unnamed x16, local copies, waits for them, and re-layouts  7.44 us

profile of v2, /device:TPU:0, one launch (start us, length us, event | category | flops | bytes accessed | tf_op | source)
XLA Modules:
  0.0 231.2 jit_solution(11034867117670364449)
XLA Ops:
  0.6 220.4 %layer.1 = (bf16[128,1024]{1,0:T(8,128)(2,1)}, f32[128,1024]{1,0:T(8,128)}, f32[24,128]{1,0:T(8,128)}, f32[8,128]{1,0:T(8,128)}, bf16[4,64,256]{2,1,0:T(8,128)(2...) custom-call(bf16[128,1024]{1,0:T(8,128)(2,1)} %bitcast.13, ...), custom_call_target="tpu_custom_call" | custom-call | tf_op jit(solution)/shard_map/layer/pallas_call | solution.py:1182
  221.1 0.0 copy-start.6
  221.1 0.7 copy-done.6
  221.8 0.0 copy-start
  221.8 1.2 copy-done
  223.0 0.0 copy-start.1
  223.0 1.0 copy-done.1
  224.1 0.0 copy-start.2
  224.1 1.0 copy-done.2
  225.1 0.0 copy-start.3
  225.1 0.9 copy-done.3
  226.1 0.0 copy-start.4
  226.1 0.9 copy-done.4
  227.0 0.0 copy-start.5
  227.0 0.9 copy-done.5
  227.9 0.0 copy-start.7
  227.9 0.7 copy-done.7
  228.6 2.5 %finish.1 = (bf16[128,1024]{1,0:T(8,128)(2,1)}, f32[128,1024]{1,0:T(8,128)}, f32[1,64]{1,0:T(1,128)}, f32[64,512]{1,0:T(8,128)}, f32[64,256]{1,0:T(8,128)}, /*in...) custom-call(bf16[128,1024]{1,0:T(8,128)(2,1)S(1)} %copy-done.3, ...), custom_call_target="tpu_custom_call" | custom-call | tf_op jit(solution)/shard_map/finish/pallas_call | solution.py:1207
Async XLA Ops:
  221.1 0.7 copy-start.6
  221.8 1.2 copy-start
  223.0 1.0 copy-start.1
  224.1 1.0 copy-start.2
  225.1 0.9 copy-start.3
  226.1 0.9 copy-start.4
  227.0 0.9 copy-start.5
  227.9 0.7 copy-start.7

commit v3 on v2

--- a/solution.py
+++ b/solution.py
@@ -513,8 +513,8 @@
     fr_ref,
     block_out, input_grad, small_out, gain_out, dqkv_out, dwo_out, dgu_out, dd_out,
     WP, SMT, X, WQ, WO, SMB, SMW, N1, CT, ST, SEGC, POSC, Q, K, V, PSC, ATT, AT, PP, PR, RES,
-    N2, GTB, GA, WGU, WD, AA, PSX, GC, H, UG, PRD, MP, MR, BP, BR, DGU, DDT, GDS, GD,
-    RB, RM, BOWN, MOWN, CO, CI, MO, MI, DGB, GUL, DDB, DDL, SG, SGF, SGT, SGZ, SGP, GRES, RL,
+    N2, GTB, GA, WGU, WD, SWG, SWU, SWD, AA, PSX, GC, H, UG, PRD, MP, MR, BP, BR, DGU, DDT, GDS, GD,
+    RB, RM, RBV, RMV, BOWN, MOWN, CO, CI, MO, MI, DGB, GUL, ZG, DDB, DDL, ZD, SG, SGF, SGT, SGZ, SGP, GRES, RL,
     AGS, AGR, DWO, RWO, ZWO, LWO, DS, DQ, DQKV, NG, NR, DWQ, RWQ, ZWQ, LWQ,
     SG1, SG1P, RSG1, EXB, EXG,
     send_sems, recv_sems, local_sems,
@@ -531,22 +531,26 @@
     device = lambda df, dz, core: {"fsdp": df, "ctx": dz, "tp": core}
     partner = device(f, z, other)
     line = Line(net, z, nz, lambda dz: device(f, dz, c))
-    zs = [lax.rem(z + k, nz) for k in range(nz)]
-    zback = [lax.rem(z + nz - k, nz) for k in range(nz)]
+    zs = [z, z + 1 - 2 * lax.rem(z, 2), lax.rem(z + 2, 4), 3 - z]
     fs = [f, f + 1 - 2 * lax.rem(f, 2), lax.rem(f + 2, 4), 3 - f]
     everyone = [(i, j, k) for k in range(2) for i in range(nf) for j in range(nz) if (i, j, k) != (0, 0, 0)]
     others = [device(fs[i], zs[j], lax.rem(c + k, 2)) for i, j, k in everyone]
-    same = [(i, j) for j in range(nz) for i in range(nf) if (i, j) != (0, 0)]
+    same = [(i, 0) for i in range(1, nf)] + [(i, j) for i in range(nf) for j in (3, 1, 2)]
 
     mine = pl.ds(pl.multiple_of(c * hb, hb), hb)
     loads = [
         pltpu.make_async_copy(x_ref.at[mine], X.at[c, z], local_sems.at[0]),
         pltpu.make_async_copy(g_ref.at[mine], GA.at[f, c, z], local_sems.at[1]),
         pltpu.make_async_copy(wo_ref, WO.at[f, z], local_sems.at[2]),
-        pltpu.make_async_copy(wg_ref.at[own], WGU.at[own, :, pl.ds(0, half_ff)], local_sems.at[3]),
-        pltpu.make_async_copy(wu_ref.at[own], WGU.at[own, :, pl.ds(half_ff, half_ff)], local_sems.at[4]),
-        pltpu.make_async_copy(wd_ref.at[own], WD.at[own], local_sems.at[5]),
     ]
+    row_experts = lambda at: pl.ds(at * nz, nz)
+    shards = ((wg_ref, SWG), (wu_ref, SWU), (wd_ref, SWD))
+    loads += [
+        pltpu.make_async_copy(ref.at[row_experts(f)], staged.at[f], local_sems.at[3 + at])
+        for at, (ref, staged) in enumerate(shards)
+    ]
+    unit = half_ff // 2
+    units = lambda h: pl.ds(h * unit, unit)
     for copy in loads:
         copy.start()
     barrier = pltpu.get_barrier_semaphore()
@@ -569,23 +573,24 @@
     pl.semaphore_wait(barrier, len(others))
 
     sends_q = [net.send(WP.at[zs[k]], WQ.at[f, z], device(f, zs[k], c)) for k in range(1, nz)]
+    sends_s = [net.send(SMT, SMB.at[f, z], device(f, zs[k], c)) for k in range(1, nz)]
     loads[0].wait()
-    view_x = [lambda at: X.at[c, at]]
-    chain_x = line.pass_on(0, view_x)
-    sends_s = [net.send(SMT, SMB.at[f, z], device(f, zs[k], c)) for k in range(1, nz)]
+    sends_x = [net.send(X.at[c, z], X.at[c, z], device(f, zs[k], c)) for k in range(1, nz)]
+    forwards_x = [net.send(X.at[c, z], X.at[c, z], partner)]
     loads[2].wait()
-    view_o = [lambda at: WO.at[f, at]]
-    chain_o = line.pass_on(0, view_o)
-    weights = []
-
-    def send_weights(count):
-        for i, j in same[len(weights) // 3 : len(weights) // 3 + count]:
-            e, to = fs[i] * nz + zs[j], device(fs[i], zs[j], c)
-            weights.append(net.send(wg_ref.at[e], WGU.at[own, :, pl.ds(0, half_ff)], to))
-            weights.append(net.send(wu_ref.at[e], WGU.at[own, :, pl.ds(half_ff, half_ff)], to))
-            weights.append(net.send(wd_ref.at[e], WD.at[own], to))
-
-    send_weights(nf - 1)
+    sends_o = [net.send(WO.at[f, z], WO.at[f, z], device(f, zs[k], c)) for k in range(1, nz)]
+    loads[1].wait()
+    view_g = [lambda at: GA.at[f, c, at]]
+    chain_g = line.pass_on(0, view_g)
+    weights = ([], [])
+
+    def send_weights(h, k, which=(0, 1, 2)):
+        for at in which:
+            target, (ref, staged) = (units(2 * h), units(2 * h + 1), units(h))[at], shards[at]
+            into = WD if staged is SWD else WGU
+            weights[h].append(
+                net.send(staged.at[:, zs[k], :, units(h)], into.at[:, z, :, target], device(f, zs[k], c))
+            )
 
     def places(shape, dim):
         at = lax.broadcasted_iota(jnp.int32, shape, dim)
@@ -622,45 +627,38 @@
     for copy in sends_q:
         copy.wait_recv()
     sends_q2 = [net.send(WQ.at[f], WQ.at[f], device(fs[k], z, c)) for k in range(1, nf)]
-    arrive(chain_x)
-    chain_x = line.pass_on(1, view_x)
-    loads[1].wait()
-    view_g = [lambda at: GA.at[f, c, at]]
-    chain_g = line.pass_on(0, view_g)
     for copy in sends_s:
         copy.wait_recv()
     sends_s2 = [net.send(SMB.at[f], SMB.at[f], device(fs[k], z, c)) for k in range(1, nf)]
+    sends_e = [
+        net.send(ref.at[row_experts(fs[k])], staged.at[f], device(fs[k], z, c))
+        for k in range(1, nf)
+        for ref, staged in shards
+    ]
     with jax.named_scope("tables1"):
         angle = offset.astype(f32) * fr_ref[0:1, :]
         CT[...] = jnp.cos(angle)
-    arrive(chain_x)
-    chain_x = line.pass_on(2, view_x)
-    arrive(chain_o)
-    chain_o = line.pass_on(1, view_o)
-    with jax.named_scope("tables2"):
         ST[...] = jnp.where(former, -1.0, 1.0) * jnp.sin(angle)
-    arrive(chain_x)
-    forward_x = net.send(X.at[c], X.at[c], partner)
-    arrive(chain_g)
-    chain_g = line.pass_on(1, view_g)
     for copy in sends_s2:
         copy.wait_recv()
     for pair in range(nf * nz // 2):
         at_f, at_z = pair // (nz // 2), 2 * (pair % (nz // 2))
         SMW[:, 128 * pair : 128 * pair + 128] = SMB[at_f, at_z] + SMB[at_f, at_z + 1]
-    arrive(chain_o)
-    chain_o = line.pass_on(2, view_o)
-    send_weights(2)
-    forward_x.wait_recv()
-
-    def norm_chunk(i, carry):
-        at_c, at_z = lax.div(i, nz), lax.rem(i, nz)
+
+    def norm_block(at_c, at_z):
         v = X[at_c, at_z].astype(f32)
         inverse = lax.rsqrt(jnp.mean(v * v, axis=1, keepdims=True) + epsilon)
-        N1[pl.ds(pl.multiple_of(i * hb, hb), hb), :] = (v * inverse * SMW[0:1, :].astype(f32)).astype(bf16)
-        return carry
-
-    lax.fori_loop(0, 2 * nz, norm_chunk, 0)
+        at = pl.ds(pl.multiple_of((at_c * nz + at_z) * hb, hb), hb)
+        N1[at, :] = (v * inverse * SMW[0:1, :].astype(f32)).astype(bf16)
+
+    norm_block(c, z)
+    for k in range(1, nz):
+        sends_x[k - 1].wait_recv()
+        forwards_x.append(net.send(X.at[c, zs[k]], X.at[c, zs[k]], partner))
+        norm_block(c, zs[k])
+    for k in range(nz):
+        forwards_x[k].wait_recv()
+        norm_block(other, zs[k])
     for copy in sends_q2:
         copy.wait_recv()
     with jax.named_scope("qkv"):
@@ -672,10 +670,10 @@
         K[...] = kv[:, :HD]
         V[...] = kv[:, HD:]
     arrive(chain_g)
-    chain_g = line.pass_on(2, view_g)
-    arrive(chain_o)
+    chain_g = line.pass_on(1, view_g)
+    for copy in sends_o:
+        copy.wait_recv()
     sends_o2 = [net.send(WO.at[f], WO.at[f], device(fs[k], z, c)) for k in range(1, nf)]
-    send_weights(1)
 
     scale = HD ** (-0.5)
     step = 2 * hb
@@ -705,16 +703,32 @@
         net.send(ATT.at[:, zs[k]], AT.at[:, :, columns], device(f, zs[k], c)) for k in range(1, nz)
     ]
     AT[:, :, columns] = ATT[:, z]
-    send_weights(3)
-
     arrive(chain_g)
-    sends_g2 = [net.send(GA.at[f, c], GA.at[f, c], device(fs[k], z, c)) for k in range(1, nf)]
-    forward_g = net.send(GA.at[f, c], GA.at[f, c], partner)
-
+    chain_g = line.pass_on(2, view_g)
+    for copy in loads[3:]:
+        copy.wait()
+    for copy in sends_e:
+        copy.wait_recv()
+    send_weights(0, 3, (0, 1))
     for copy in sends_a:
         copy.wait_recv()
     for copy in sends_o2:
         copy.wait_recv()
+    wd_full = lambda: WD[...].reshape(width, half_ff)
+    wgu_full = lambda: WGU[...].reshape(width, 2 * half_ff)
+    lower, upper = pl.ds(0, nz // 2), pl.ds(nz // 2, nz // 2)
+    across = [None, device(fs[1], z, c), device(fs[2], z, c), device(fs[3], z, c)]
+
+    def second_hop(ref):
+        return [net.send(ref.at[f, c], ref.at[f, c], across[k]) for k in (1, 2)]
+
+    def third_hop(ref, k):
+        part, to = ((lower, across[2]), (upper, across[1]))[k - 1]
+        return net.send(ref.at[fs[k], c, part], ref.at[fs[k], c, part], to)
+
+    arrive(chain_g)
+    sends_g2 = second_hop(GA)
+    forwards_g = [net.send(GA.at[f, c], GA.at[f, c], partner)]
     with jax.named_scope("proj"):
         part = dot_nt(AT[...].reshape(block, nz * 2 * HD), WO[...].reshape(width, nz * 2 * HD))
         PP[...] = part.reshape(2, hb, width)
@@ -740,94 +754,104 @@
     GTB[f, c, z] = jnp.concatenate([gates, jnp.zeros((experts, 128 - hb), f32)], axis=1)
     view_n = [lambda at: N2.at[f, c, at], lambda at: GTB.at[f, c, at]]
     chain_n = line.pass_on(0, view_n)
-    send_weights(2)
-
-    wd_full = lambda: WD[...].reshape(width, half_ff)
-    wgu_full = lambda: WGU[...].reshape(width, 2 * half_ff)
-    forwards_g2 = []
-    for k in range(1, nf):
-        sends_g2[k - 1].wait_recv()
-        forwards_g2.append(net.send(GA.at[fs[k], c], GA.at[fs[k], c], partner))
+    send_weights(0, 3, (2,))
+
     arrive(chain_n)
     chain_n = line.pass_on(1, view_n)
-    send_weights(2)
+    send_weights(0, 2, (0,))
     arrive(chain_n)
     chain_n = line.pass_on(2, view_n)
-    send_weights(nf * nz)
+    send_weights(0, 2, (1, 2))
+    send_weights(0, 1)
+    for k in (3, 2, 1):
+        send_weights(1, k)
+    sends_g3 = []
+    for k in (1, 2):
+        sends_g2[k - 1].wait_recv()
+        sends_g3.append(third_hop(GA, k))
+        forwards_g.append(net.send(GA.at[fs[k], c], GA.at[fs[k], c], partner))
     arrive(chain_n)
-
-    def second_hop(ref, at_f, to):
-        return [net.send(ref.at[at_f, c], ref.at[at_f, c], to)]
-
-    sends_n2 = [
-        [net.send(N2.at[f, c], N2.at[f, c], device(fs[k], z, c)), net.send(GTB.at[f, c], GTB.at[f, c], device(fs[k], z, c))]
-        for k in range(1, nf)
-    ]
-    forwards_n = [
-        [net.send(N2.at[f, c], N2.at[f, c], partner), net.send(GTB.at[f, c], GTB.at[f, c], partner)]
-    ]
-    for copy in loads[3:]:
-        copy.wait()
-    for copy in weights:
-        copy.wait_recv()
-    forward_g.wait_recv()
-    with jax.named_scope("cotangent"):
-        AA[f] = dot_nn(GA[f].reshape(rows, width), wd_full())
-
+    sends_n2 = second_hop(N2)
+    sends_t2 = [net.send(GTB.at[f, c], GTB.at[f, c], across[k]) for k in (1, 2, 3)]
+    forwards_n = [net.send(N2.at[f, c], N2.at[f, c], partner)]
+    forwards_t = [net.send(GTB.at[f, c], GTB.at[f, c], partner)]
+    for copy in sends_g3:
+        copy.wait_recv()
+    forwards_g.append(net.send(GA.at[fs[3], c], GA.at[fs[3], c], partner))
+
+    WGU[:, z, :, 0:unit] = SWG[:, z, :, 0:unit]
+    WGU[:, z, :, unit : 2 * unit] = SWU[:, z, :, 0:unit]
+    WGU[:, z, :, 2 * unit : 3 * unit] = SWG[:, z, :, unit : 2 * unit]
+    WGU[:, z, :, 3 * unit : 4 * unit] = SWU[:, z, :, unit : 2 * unit]
+    WD[:, z] = SWD[:, z]
     chosen_row = jnp.where(
         lax.broadcasted_iota(jnp.int32, (experts, 128), 0) == own, 1.0, 0.0
     ).astype(f32)
-    DGU[...] = jnp.zeros_like(DGU)
-    DDT[...] = jnp.zeros_like(DDT)
-    sends_d, sends_b, sends_m = [], [], []
-    exchange_b, exchange_m = [], []
-
-    for k in range(nf):
+    sends_d, sends_b, exchange_b, exchange_m = [], {}, {}, {}
+    low_half = z < nz // 2
+    in_order = [jnp.where(low_half, 3, 0), jnp.where(low_half, 2, 1), zs[1], z]
+    grads_z, grads_f = ([], []), ([], [])
+
+    def send_grads(h, k):
+        to = device(f, zs[k], c)
+        grads_z[h].append(net.send(DGB.at[h, :, zs[k]], ZG.at[h, z], to))
+        grads_z[h].append(net.send(DDB.at[h, :, zs[k]], ZD.at[h, z], to))
+
+    def spread_grads(h):
+        ZG[h, z] = DGB[h, :, z]
+        ZD[h, z] = DDB[h, :, z]
+        for copy in grads_z[h]:
+            copy.wait_recv()
+        for k in range(1, nf):
+            grads_f[h].append(
+                net.send(ZG.at[h, :, fs[k]], GUL.at[f, :, :, pl.ds(2 * h * unit, 2 * unit)], across[k])
+            )
+            grads_f[h].append(net.send(ZD.at[h, :, fs[k]], DDL.at[f, :, :, units(h)], across[k]))
+        GUL[f, :, :, 2 * h * unit : 2 * (h + 1) * unit] = ZG[h, :, f]
+        DDL[f, :, :, h * unit : (h + 1) * unit] = ZD[h, :, f]
+
+    def expert_part(h, k):
         at_f = fs[k]
-        if k > 0:
-            forwards_g2[k - 1].wait_recv()
-            with jax.named_scope("cotangent"):
-                AA[at_f] = dot_nn(GA[at_f].reshape(rows, width), wd_full())
-            for copy in sends_n2[k - 1]:
-                copy.wait_recv()
-            forwards_n.append(
-                [net.send(N2.at[at_f, c], N2.at[at_f, c], partner), net.send(GTB.at[at_f, c], GTB.at[at_f, c], partner)]
-            )
-        for copy in forwards_n[k]:
-            copy.wait_recv()
         tokens = N2[at_f].reshape(rows, width)
+        grads = GA[at_f].reshape(rows, width)
         with jax.named_scope("gateup"):
-            PSX[...] = dot_nn(tokens, wgu_full())
-        with jax.named_scope("gatecol"):
-            for piece in range(2 * nz):
-                tile = GTB[at_f, piece // nz, piece % nz][:, 0:hb]
-                GC[piece * hb : (piece + 1) * hb, :] = dot_tn(tile, chosen_row, lax.Precision.HIGHEST)
+            PSX[...] = dot_nn(tokens, WGU[:, :, :, 2 * h * unit : 2 * (h + 1) * unit].reshape(width, 2 * unit))
+        with jax.named_scope("cotangent"):
+            AA[...] = dot_nn(grads, WD[:, :, :, h * unit : (h + 1) * unit].reshape(width, unit))
+        if h == 0:
+            with jax.named_scope("gatecol"):
+                for piece in range(2 * nz):
+                    tile = GTB[at_f, piece // nz, piece % nz][:, 0:hb]
+                    GC[k, piece * hb : (piece + 1) * hb, :] = dot_tn(tile, chosen_row, lax.Precision.HIGHEST)
 
         def expert_chunk(i, carry):
-            at = pl.ds(pl.multiple_of(i * 32, 32), 32)
-            gate_pre = PSX[at, 0:half_ff]
-            up_pre = PSX[at, half_ff : 2 * half_ff]
-            raw = AA[at_f, at, :]
-            gate = GC[at, 0:1]
+            at = pl.ds(pl.multiple_of(i * 64, 64), 64)
+            gate_pre = PSX[at, 0:unit]
+            up_pre = PSX[at, unit : 2 * unit]
+            raw = AA[at, :]
+            gate = GC[k, at, :]
             sigmoid = jax.nn.sigmoid(gate_pre)
             silu = gate_pre * sigmoid
             act = silu * up_pre
             PRD[at, :] = (act * raw).astype(bf16)
-            H[at, :] = (act * gate).astype(bf16)
+            H[k, at, h * unit : (h + 1) * unit] = (act * gate).astype(bf16)
             grad = raw * gate
-            UG[at, 0:half_ff] = (
+            UG[k, at, 2 * h * unit : (2 * h + 1) * unit] = (
                 grad * up_pre * sigmoid * (1.0 + gate_pre * (1.0 - sigmoid))
             ).astype(bf16)
-            UG[at, half_ff : 2 * half_ff] = (grad * silu).astype(bf16)
+            UG[k, at, (2 * h + 1) * unit : 2 * (h + 1) * unit] = (grad * silu).astype(bf16)
             return carry
 
         with jax.named_scope("chunk"):
-            lax.fori_loop(0, rows // 32, expert_chunk, 0)
-        with jax.named_scope("back"):
-            BP[at_f] = dot_nt(UG[...], wgu_full()).astype(bf16).reshape(2, nz, hb, width)
-        exchange_b.append(net.send(BP.at[at_f, other], BR.at[at_f], partner))
+            lax.fori_loop(0, rows // 64, expert_chunk, 0)
+        if h == 1:
+            with jax.named_scope("back"):
+                BP[at_f] = dot_nt(UG[k], WGU[...].reshape(width, 2 * half_ff)).astype(bf16).reshape(2, nz, hb, width)
+            exchange_b[k] = net.send(BP.at[at_f, other], BR.at[at_f], partner)
         with jax.named_scope("gdot"):
-            GDS[k] = dot_nt(jnp.ones((8, half_ff), bf16), PRD[...])
+            dots = dot_nt(jnp.ones((8, unit), bf16), PRD[...])
+            GDS[k] = dots if h == 0 else GDS[k] + dots
+        if h == 1:
             for j in range(nz):
                 for t in range(2):
                     to_z, to_c = zs[j], lax.rem(c + t, 2)
@@ -838,41 +862,90 @@
                         )
                     else:
                         GD[f, z, c] = GDS[0, :, lanes]
-        with jax.named_scope("mix"):
-            MP[at_f] = dot_nt(H[...], wd_full()).astype(bf16).reshape(2, nz, hb, width)
-        exchange_m.append(net.send(MP.at[at_f, other], MR.at[at_f], partner))
+            with jax.named_scope("mix"):
+                MP[at_f] = dot_nt(H[k], WD[...].reshape(width, half_ff)).astype(bf16).reshape(2, nz, hb, width)
+            exchange_m[k] = net.send(MP.at[at_f, other], MR.at[at_f], partner)
+        with jax.named_scope("wgrad"):
+            gate_up = dot_tn(UG[k, :, 2 * h * unit : 2 * (h + 1) * unit], tokens)
+            down = dot_tn(H[k, :, h * unit : (h + 1) * unit], grads)
+            first = k == (0, 3)[h]
+            DGU[...] = gate_up if first else DGU[...] + gate_up
+            DDT[...] = down if first else DDT[...] + down
+
+    def shed(h):
+        with jax.named_scope("transpose"):
+            DGB[h] = jnp.transpose(DGU[...]).astype(bf16).reshape(nf, nz, shard, 2 * unit)
+            DDB[h] = jnp.transpose(DDT[...]).astype(bf16).reshape(nf, nz, shard, unit)
+
+    for copy in weights[0]:
+        copy.wait_recv()
+    for k in range(nf):
+        if k == 1:
+            sends_n3 = []
+            for i in (1, 2):
+                sends_n2[i - 1].wait_recv()
+                sends_n3.append(third_hop(N2, i))
+                forwards_n.append(net.send(N2.at[fs[i], c], N2.at[fs[i], c], partner))
+                sends_t2[i - 1].wait_recv()
+                forwards_t.append(net.send(GTB.at[fs[i], c], GTB.at[fs[i], c], partner))
+        if k == 3:
+            for copy in sends_n3:
+                copy.wait_recv()
+            forwards_n.append(net.send(N2.at[fs[k], c], N2.at[fs[k], c], partner))
+            sends_t2[2].wait_recv()
+            forwards_t.append(net.send(GTB.at[fs[k], c], GTB.at[fs[k], c], partner))
+        forwards_g[k].wait_recv()
+        forwards_n[k].wait_recv()
+        forwards_t[k].wait_recv()
+        expert_part(0, k)
+    shed(0)
+    for k in (3, 2, 1):
+        send_grads(0, k)
+    for copy in weights[1]:
+        copy.wait_recv()
+    own_half = ((lower, 1), (upper, 2))
+
+    def spread(k, exchange, part, back, total, via, into, order):
+        at_f = fs[k]
+        exchange[k].wait_recv()
+        if k == 0:
+            total[...] = part[at_f, c].astype(f32) + back[at_f].astype(f32)
+            return []
+        if k == 3:
+            part[at_f, c] = (part[at_f, c].astype(f32) + back[at_f].astype(f32)).astype(bf16)
+            return [net.send(part.at[at_f, c, half_at], via.at[to - 1], across[to]) for half_at, to in own_half]
+        return None
+
+    def spread_near(k, firsts, part, back, via, into, order):
+        at_f = fs[k]
+        half_at, other_half = (upper, lower) if k == 1 else (lower, upper)
+        firsts[2 - k].wait_recv()
+        part[at_f, c, half_at] = (
+            part[at_f, c, half_at].astype(f32) + back[at_f, half_at].astype(f32) + via[2 - k].astype(f32)
+        ).astype(bf16)
+        part[at_f, c, other_half] = (
+            part[at_f, c, other_half].astype(f32) + back[at_f, other_half].astype(f32)
+        ).astype(bf16)
+        return [net.send(part.at[at_f, c, at], into.at[k - 1, at], across[k]) for at in order]
+
+    sends_m = {}
+    expert_part(1, 3)
+    firsts_b = spread(3, exchange_b, BP, BR, BOWN, RBV, RB, in_order)
+    firsts_m = spread(3, exchange_m, MP, MR, MOWN, RMV, RM, in_order)
+    expert_part(1, 1)
+    expert_part(1, 2)
+    for k in (1, 2):
         exchange_b[k].wait_recv()
-        if k == 0:
-            BOWN[...] = BP[at_f, c].astype(f32) + BR[at_f].astype(f32)
-        else:
-            BP[at_f, c] = (BP[at_f, c].astype(f32) + BR[at_f].astype(f32)).astype(bf16)
-            sends_b.append(net.send(BP.at[at_f, c], RB.at[k - 1], device(at_f, z, c)))
-        with jax.named_scope("wgrad"):
-            DGU[...] += dot_tn(UG[...], tokens)
-            DDT[...] += dot_tn(H[...], GA[at_f].reshape(rows, width))
+        sends_b[k] = spread_near(k, firsts_b, BP, BR, RBV, RB, in_order)
+    expert_part(1, 0)
+    for k in (1, 2):
         exchange_m[k].wait_recv()
-        if k == 0:
-            MOWN[...] = MP[at_f, c].astype(f32) + MR[at_f].astype(f32)
-        else:
-            MP[at_f, c] = (MP[at_f, c].astype(f32) + MR[at_f].astype(f32)).astype(bf16)
-
-    for k in range(1, nf):
-        sends_m.append(net.send(MP.at[fs[k], c], RM.at[k - 1], device(fs[k], z, c)))
-    with jax.named_scope("transpose"):
-        DGB[...] = jnp.transpose(DGU[...]).astype(bf16).reshape(nf, nz, shard, 2 * half_ff)
-        DDB[...] = jnp.transpose(DDT[...]).astype(bf16).reshape(nf, nz, shard, half_ff)
-    grads_at = []
-    far = same[nf - 1 :] + same[: nf - 1]
-
-    def send_grads(count):
-        for i, j in far[len(grads_at) // 2 : len(grads_at) // 2 + count]:
-            to = device(fs[i], zs[j], c)
-            grads_at.append(net.send(DGB.at[fs[i], zs[j]], GUL.at[own], to))
-            grads_at.append(net.send(DDB.at[fs[i], zs[j]], DDL.at[own], to))
-
-    send_grads(2)
-    GUL[own] = DGB[f, z]
-    DDL[own] = DDB[f, z]
+        sends_m[k] = spread_near(k, firsts_m, MP, MR, RMV, RM, in_order)
+    spread(0, exchange_b, BP, BR, BOWN, RBV, RB, in_order)
+    spread(0, exchange_m, MP, MR, MOWN, RMV, RM, in_order)
+
+    shed(1)
+    send_grads(1, 3)
 
     for copy in sends_d:
         copy.wait_recv()
@@ -892,17 +965,22 @@
     residual = RES[...]
     inverse_two = lax.rsqrt(jnp.mean(residual * residual, axis=1, keepdims=True) + epsilon)
 
-    for k in range(1, nf):
-        sends_b[k - 1].wait_recv()
-        BOWN[...] += RB[k - 1].astype(f32)
     own_b, out_b, into_b = (lambda at: BOWN.at[at]), (lambda w, t: CO.at[w, t]), (lambda w, t: CI.at[w, t])
+
+    def take_block(at):
+        for k in (1, 2):
+            sends_b[k][at].wait_recv()
+            BOWN[in_order[at]] += RB[k - 1, in_order[at]].astype(f32)
+
     sums = []
-    for t in range(nz - 1):
-        at_sums = len(net.copies)
-        chain_b = line.add_on(t, own_b, out_b, into_b)
-        sums.extend(range(at_sums, len(net.copies)))
-        send_grads(1)
-        arrive(chain_b)
+    for t in range(nz):
+        take_block(t)
+        if t > 0:
+            arrive(chain_b)
+        if t < nz - 1:
+            at_sums = len(net.copies)
+            chain_b = line.add_on(t, own_b, out_b, into_b)
+            sums.extend(range(at_sums, len(net.copies)))
     line.finish(BOWN.at[z], into_b)
 
     grad_two = BOWN[z] + GRES[...]
@@ -933,7 +1011,14 @@
         for k in range(1, nz)
     ]
     AGR[:, z] = AGS[:, :, columns]
-    send_grads(3)
+    for k in (1, 2):
+        for at in range(nz):
+            sends_m[k][at].wait_recv()
+        MOWN[...] += RM[k - 1].astype(f32)
+    own_m, out_m, into_m = (lambda at: MOWN.at[at]), (lambda w, t: MO.at[w, t]), (lambda w, t: MI.at[w, t])
+    chain_m = line.add_on(0, own_m, out_m, into_m)
+    send_grads(1, 2)
+    send_grads(1, 1)
     with jax.named_scope("outgrad"):
         DWO[...] = (
             dot_tn(low, AT[...].reshape(block, nz * 2 * HD))
@@ -978,23 +1063,32 @@
     with jax.named_scope("ingrad"):
         NG[...] = dot_nt(DQKV[...], WQ[...].reshape(width, 4 * HD)).astype(bf16).reshape(2, nz, hb, width)
     send_ng = net.send(NG.at[other], NR, partner)
+    arrive(chain_m)
+    chain_m = line.add_on(1, own_m, out_m, into_m)
     with jax.named_scope("qkvgrad"):
         DWQ[...] = (
             jnp.transpose(dot_tn(DQKV[...], N1[...])).astype(bf16).reshape(nf, nz, shard, 4 * HD)
         )
     sends_wq = [net.send(DWQ.at[fs[k]], RWQ.at[k - 1], device(fs[k], z, c)) for k in range(1, nf)]
+    small = SG[:, block_lanes(f)]
+    for k in range(1, nf):
+        sends_sg[k - 1].wait_recv()
+        small = small + SGF[k - 1]
+    SGT[...] = small
+    pair_lanes = lambda at: pl.ds(pl.multiple_of(lax.div(at, 2) * 128, 128), 128)
+    sends_sz = [net.send(SGT.at[:, pair_lanes(zs[k])], SGZ.at[k - 1], device(f, zs[k], c)) for k in range(1, nz)]
     send_ng.wait_recv()
+    net.drain(sums)
     BOWN[...] = NG[c].astype(f32) + NR[...].astype(f32)
-    net.drain(sums)
     chain_g1 = line.add_on(0, own_b, out_b, into_b)
-
-    for k in range(1, nf):
-        sends_m[k - 1].wait_recv()
-        MOWN[...] += RM[k - 1].astype(f32)
-    own_m, out_m, into_m = (lambda at: MOWN.at[at]), (lambda w, t: MO.at[w, t]), (lambda w, t: MI.at[w, t])
-    chain_m = line.add_on(0, own_m, out_m, into_m)
+    arrive(chain_m)
+    chain_m = line.add_on(2, own_m, out_m, into_m)
     arrive(chain_g1)
     chain_g1 = line.add_on(1, own_b, out_b, into_b)
+
+    spread_grads(0)
+    arrive(chain_g1)
+    chain_g1 = line.add_on(2, own_b, out_b, into_b)
 
     total = DWO[f].astype(f32)
     for k in range(1, nf):
@@ -1003,18 +1097,6 @@
     ZWO[...] = total.astype(bf16)
     sends_wo2 = [net.send(ZWO.at[zs[k]], LWO.at[z], device(f, zs[k], c)) for k in range(1, nz)]
     LWO[z] = ZWO[z]
-    small = SG[:, block_lanes(f)]
-    for k in range(1, nf):
-        sends_sg[k - 1].wait_recv()
-        small = small + SGF[k - 1]
-    SGT[...] = small
-    pair_lanes = lambda at: pl.ds(pl.multiple_of(lax.div(at, 2) * 128, 128), 128)
-    sends_sz = [net.send(SGT.at[:, pair_lanes(zs[k])], SGZ.at[k - 1], device(f, zs[k], c)) for k in range(1, nz)]
-    arrive(chain_g1)
-    chain_g1 = line.add_on(2, own_b, out_b, into_b)
-    arrive(chain_m)
-    chain_m = line.add_on(1, own_m, out_m, into_m)
-
     total = DWQ[f].astype(f32)
     for k in range(1, nf):
         sends_wq[k - 1].wait_recv()
@@ -1022,14 +1104,13 @@
     ZWQ[...] = total.astype(bf16)
     sends_wq2 = [net.send(ZWQ.at[zs[k]], LWQ.at[z], device(f, zs[k], c)) for k in range(1, nz)]
     LWQ[z] = ZWQ[z]
-    send_grads(nf * nz)
+    spread_grads(1)
     small = SGT[:, pair_lanes(z)]
     for k in range(1, nz):
         sends_sz[k - 1].wait_recv()
         small = small + SGZ[k - 1]
     SGP[0] = small
     send_sp = net.send(SGP.at[0], SGP.at[1], partner)
-
     arrive(chain_g1)
     line.finish(BOWN.at[z], into_b)
     grad_one = BOWN[z]
@@ -1056,7 +1137,9 @@
     RSG1[f, z] = SG1P[:, lanes_of(f, z)]
 
     arrive(chain_m)
-    chain_m = line.add_on(2, own_m, out_m, into_m)
+    line.finish(MOWN.at[z], into_m)
+    EXB[c] = (RES[...] + MOWN[z]).astype(bf16)
+    send_bo = net.send(EXB.at[c], EXB.at[c], partner)
     send_sp.wait_recv()
     small_out[...] = SGP[0] + SGP[1]
     for copy in sends_wo2:
@@ -1065,18 +1148,14 @@
     for j in range(1, nz):
         total = total + LWO[j].astype(f32)
     dwo_out[...] = total
-    arrive(chain_m)
-    line.finish(MOWN.at[z], into_m)
-    EXB[c] = (RES[...] + MOWN[z]).astype(bf16)
-    send_bo = net.send(EXB.at[c], EXB.at[c], partner)
     for copy in sends_wq2:
         copy.wait_recv()
     dqkv_out[...] = LWQ[...]
-    for copy in grads_at:
+    for copy in grads_f[0] + grads_f[1]:
         copy.wait_recv()
     outs = [
-        pltpu.make_async_copy(GUL, dgu_out, local_sems.at[6]),
-        pltpu.make_async_copy(DDL, dd_out, local_sems.at[7]),
+        pltpu.make_async_copy(GUL, dgu_out, local_sems.at[8]),
+        pltpu.make_async_copy(DDL, dd_out, local_sems.at[9]),
     ]
     for copy in outs:
         copy.start()
@@ -1103,8 +1182,10 @@
     nz, experts, half_ff, shard = dims
     block_out[...] = block_ref[...]
     input_out[...] = input_ref[...]
-    gate_out[...] = dgu_ref[:, :, 0:half_ff].astype(f32)
-    up_out[...] = dgu_ref[:, :, half_ff : 2 * half_ff].astype(f32)
+    unit = half_ff // 2
+    for h in range(2):
+        gate_out[:, :, h * unit : (h + 1) * unit] = dgu_ref[:, :, 2 * h * unit : (2 * h + 1) * unit].astype(f32)
+        up_out[:, :, h * unit : (h + 1) * unit] = dgu_ref[:, :, (2 * h + 1) * unit : 2 * (h + 1) * unit].astype(f32)
     down_out[...] = dd_ref[...].astype(f32)
     even = lax.rem(lax.axis_index("ctx"), 2) == 0
     pick = lambda v: jnp.where(even, v, pltpu.roll(v, 128 - shard, 1))[:, 0:shard]
@@ -1152,19 +1233,21 @@
         ATT=((2, nz, hb, 2 * HD), bf16), AT=((2, hb, W), bf16), PP=((2, hb, width), f32), PR=((hb, width), f32),
         RES=((hb, width), f32),
         N2=((nf, 2, nz, hb, width), bf16), GTB=((nf, 2, nz, experts, 128), f32), GA=((nf, 2, nz, hb, width), bf16),
-        WGU=((nf * nz, shard, 2 * half_ff), bf16), WD=((nf * nz, shard, half_ff), bf16),
-        AA=((nf, rows, half_ff), f32), PSX=((rows, 2 * half_ff), f32), GC=((rows, 128), f32),
-        H=((rows, half_ff), bf16), UG=((rows, 2 * half_ff), bf16), PRD=((rows, half_ff), bf16),
+        WGU=((nf, nz, shard, 2 * half_ff), bf16), WD=((nf, nz, shard, half_ff), bf16),
+        SWG=((nf, nz, shard, half_ff), bf16), SWU=((nf, nz, shard, half_ff), bf16), SWD=((nf, nz, shard, half_ff), bf16),
+        AA=((rows, half_ff // 2), f32), PSX=((rows, half_ff), f32), GC=((nf, rows, 128), f32),
+        H=((nf, rows, half_ff), bf16), UG=((nf, rows, 2 * half_ff), bf16), PRD=((rows, half_ff // 2), bf16),
         MP=((nf, 2, nz, hb, width), bf16), MR=((nf, nz, hb, width), bf16),
         BP=((nf, 2, nz, hb, width), bf16), BR=((nf, nz, hb, width), bf16),
-        DGU=((2 * half_ff, width), f32), DDT=((half_ff, width), f32),
+        DGU=((half_ff, width), f32), DDT=((half_ff // 2, width), f32),
         GDS=((nf, 8, rows), f32), GD=((nf, nz, 2, 8, 128), f32),
-        RB=((nf - 1, nz, hb, width), bf16), RM=((nf - 1, nz, hb, width), bf16),
+        RB=((2, nz, hb, width), bf16), RM=((2, nz, hb, width), bf16),
+        RBV=((2, nz // 2, hb, width), bf16), RMV=((2, nz // 2, hb, width), bf16),
         BOWN=((nz, hb, width), f32), MOWN=((nz, hb, width), f32),
         CO=((2, nz - 1, hb, width), bf16), CI=((2, nz - 1, hb, width), bf16),
         MO=((2, nz - 1, hb, width), bf16), MI=((2, nz - 1, hb, width), bf16),
-        DGB=((nf, nz, shard, 2 * half_ff), bf16), GUL=((nf * nz, shard, 2 * half_ff), bf16),
-        DDB=((nf, nz, shard, half_ff), bf16), DDL=((nf * nz, shard, half_ff), bf16),
+        DGB=((2, nf, nz, shard, half_ff), bf16), GUL=((nf, nz, shard, 2 * half_ff), bf16), ZG=((2, nz, nf, shard, half_ff), bf16),
+        DDB=((2, nf, nz, shard, half_ff // 2), bf16), DDL=((nf, nz, shard, half_ff), bf16), ZD=((2, nz, nf, shard, half_ff // 2), bf16),
         SG=((experts + 8, width), f32), SGF=((nf - 1, experts + 8, width // nf), f32),
         SGT=((experts + 8, width // nf), f32), SGZ=((nz - 1, experts + 8, 128), f32), SGP=((2, experts + 8, 128), f32),
         GRES=((hb, width), f32), RL=((2, hb, width), bf16),
@@ -1185,13 +1268,13 @@
         out_shape=(
             shape((block, width), bf16), shape((block, width), f32), shape((experts + 8, 128), f32),
             shape((8, 128), f32), shape((nz, shard, 4 * HD), bf16), shape((shard, W), f32),
-            shape((nf * nz, shard, 2 * half_ff), bf16), shape((nf * nz, shard, half_ff), bf16),
+            shape((nf, nz, shard, 2 * half_ff), bf16), shape((nf, nz, shard, half_ff), bf16),
         ),
         in_specs=[anywhere] * 2 + [vm] * 3 + [anywhere] + [vm] * 3 + [anywhere] * 3
         + [pl.BlockSpec(memory_space=pltpu.SMEM), vm, vm],
         out_specs=(vm,) * 6 + (anywhere,) * 2,
         scratch_shapes=[pltpu.VMEM(s, d) for s, d in scratch.values()]
-        + [pltpu.SemaphoreType.DMA((slots,)), pltpu.SemaphoreType.DMA((slots,)), pltpu.SemaphoreType.DMA((8,))],
+        + [pltpu.SemaphoreType.DMA((slots,)), pltpu.SemaphoreType.DMA((slots,)), pltpu.SemaphoreType.DMA((10,))],
         compiler_params=pltpu.CompilerParams(
             collective_id=0, has_side_effects=True, vmem_limit_bytes=67043328
         ),
@@ -1225,7 +1308,7 @@
             whole(experts, shard), some(per, shard, half_ff), some(per, shard, half_ff), some(per, shard, half_ff),
         ),
         compiler_params=pltpu.CompilerParams(vmem_limit_bytes=33554432),
-    )(*out)
+    )(*out[:6], out[6].reshape(experts, shard, 2 * half_ff), out[7].reshape(experts, shard, half_ff))
     block_out, input_grad, gain1, q, k, v, o, gain2, router, gate, up, down = out
     return (
         block_out[None], input_grad[None], gain1[0], q, k, v, o, gain2[0], router.T, gate, up, down,

time: 234 us -> 193 us (0.82); the launches traced: 231 us -> 193 us
  Pallas kernels: 223 us -> 185 us
    pallas_call x1, Pallas kernels: 220 us -> 183 us  [fast_local(): pl.pallas_call(functools.partial(layer_kernel, (nf, nz, hb, width, expert...]
where the time goes in v3:
time: 193 us
  Pallas kernels  185 us (96%)
  local copies, waits for them, and re-layouts  6.76 us (4%)
    pallas_call x1, Pallas kernels, fast_local(): pl.pallas_call(functools.partial(layer_kernel, (nf, nz, hb, width, expert...  183 us
    unnamed x16, local copies, waits for them, and re-layouts  6.76 us

profile of v3, /device:TPU:0, one launch (start us, length us, event | category | flops | bytes accessed | tf_op | source)
XLA Modules:
  0.0 192.6 jit_solution(17304088311187712743)
XLA Ops:
  0.6 182.5 %layer.1 = (bf16[128,1024]{1,0:T(8,128)(2,1)}, f32[128,1024]{1,0:T(8,128)}, f32[24,128]{1,0:T(8,128)}, f32[8,128]{1,0:T(8,128)}, bf16[4,64,256]{2,1,0:T(8,128)(2...) custom-call(bf16[128,1024]{1,0:T(8,128)(2,1)} %bitcast.17, ...), custom_call_target="tpu_custom_call" | custom-call | tf_op jit(solution)/shard_map/layer/pallas_call | solution.py:1265
  183.2 0.0 copy-start.6
  183.2 0.0 copy-start.7
  183.2 0.7 copy-done.6
  183.9 0.0 copy-done.7
  183.9 0.0 copy-start
  183.9 1.2 copy-done
  185.1 0.0 copy-start.1
  185.1 1.0 copy-done.1
  186.2 0.0 copy-start.2
  186.2 1.0 copy-done.2
  187.2 0.0 copy-start.3
  187.2 0.9 copy-done.3
  188.1 0.0 copy-start.4
  188.1 0.9 copy-done.4
  189.1 0.0 copy-start.5
  189.1 0.9 copy-done.5
  190.0 2.6 %finish.1 = (bf16[128,1024]{1,0:T(8,128)(2,1)}, f32[128,1024]{1,0:T(8,128)}, f32[1,64]{1,0:T(1,128)}, f32[64,512]{1,0:T(8,128)}, f32[64,256]{1,0:T(8,128)}, /*in...) custom-call(bf16[128,1024]{1,0:T(8,128)(2,1)S(1)} %copy-done.3, ...), custom_call_target="tpu_custom_call" | custom-call | tf_op jit(solution)/shard_map/finish/pallas_call | solution.py:1290
Async XLA Ops:
  183.2 0.7 copy-start.6
  183.2 0.7 copy-start.7
  183.9 1.2 copy-start
  185.1 1.0 copy-start.1
  186.2 1.0 copy-start.2
  187.2 0.9 copy-start.3
  188.1 0.9 copy-start.4
  189.1 0.9 copy-start.5

commit v4 on v3

--- a/solution.py
+++ b/solution.py
@@ -419,30 +419,55 @@
 class Net:
     def __init__(self, send_sems, recv_sems):
         self.send_sems, self.recv_sems, self.copies, self.left = send_sems, recv_sems, [], set()
+        self.slots, self.free_send, self.free_recv = [], [], []
+        self.top_send = self.top_recv = 0
 
     def make(self, source, target, device, sends=None):
-        at = len(self.copies)
+        if self.free_send:
+            send_at = self.free_send.pop(0)
+        else:
+            send_at, self.top_send = self.top_send, self.top_send + 1
+        if self.free_recv:
+            recv_at = self.free_recv.pop(0)
+        else:
+            recv_at, self.top_recv = self.top_recv, self.top_recv + 1
+        assert max(send_at + 1 - self.send_sems.shape[0], recv_at + 1 - self.recv_sems.shape[0]) <= 0
         copy = pltpu.make_async_remote_copy(
             src_ref=source,
             dst_ref=target,
-            send_sem=self.send_sems.at[at],
-            recv_sem=self.recv_sems.at[at],
+            send_sem=self.send_sems.at[send_at],
+            recv_sem=self.recv_sems.at[recv_at],
             device_id=device,
             device_id_type=MESH,
         )
         self.copies.append((copy, sends))
+        self.slots.append((send_at, recv_at))
         return copy
 
     def send(self, source, target, device):
         copy = self.make(source, target, device)
         copy.start()
         return copy
+
+    def free(self, among):
+        self.free_recv.extend(self.slots[at][1] for at in among)
+
+    def numbers(self, *groups):
+        found = []
+        for group in groups:
+            if isinstance(group, list):
+                found += self.numbers(*group)
+            else:
+                copy = group[0] if isinstance(group, tuple) else group
+                found += [at for at, (one, sends) in enumerate(self.copies) if one is copy]
+        return found
 
     def drain(self, among=None):
         for at, (copy, sends) in enumerate(self.copies):
             if at in self.left or (among is not None and at not in among):
                 continue
             self.left.add(at)
+            self.free_send.append(self.slots[at][0])
             if sends is None:
                 copy.wait_send()
             else:
@@ -572,6 +597,18 @@
     WQ[f, z] = WP[z]
     pl.semaphore_wait(barrier, len(others))
 
+    wd_full = lambda: WD[...].reshape(width, half_ff)
+    wgu_full = lambda: WGU[...].reshape(width, 2 * half_ff)
+    lower, upper = pl.ds(0, nz // 2), pl.ds(nz // 2, nz // 2)
+    across = [None, device(fs[1], z, c), device(fs[2], z, c), device(fs[3], z, c)]
+
+    def second_hop(ref):
+        return [net.send(ref.at[f, c], ref.at[f, c], across[k]) for k in (1, 2)]
+
+    def third_hop(ref, k):
+        part, to = ((lower, across[2]), (upper, across[1]))[k - 1]
+        return net.send(ref.at[fs[k], c, part], ref.at[fs[k], c, part], to)
+
     sends_q = [net.send(WP.at[zs[k]], WQ.at[f, z], device(f, zs[k], c)) for k in range(1, nz)]
     sends_s = [net.send(SMT, SMB.at[f, z], device(f, zs[k], c)) for k in range(1, nz)]
     loads[0].wait()
@@ -582,14 +619,26 @@
     loads[1].wait()
     view_g = [lambda at: GA.at[f, c, at]]
     chain_g = line.pass_on(0, view_g)
-    weights = ([], [])
-
-    def send_weights(h, k, which=(0, 1, 2)):
-        for at in which:
-            target, (ref, staged) = (units(2 * h), units(2 * h + 1), units(h))[at], shards[at]
-            into = WD if staged is SWD else WGU
-            weights[h].append(
-                net.send(staged.at[:, zs[k], :, units(h)], into.at[:, z, :, target], device(f, zs[k], c))
+    chains = [chain_g]
+    weights = ([], [], [])
+
+    def send_row(k, at):
+        ref, staged = shards[at]
+        return net.send(ref.at[row_experts(fs[k])], staged.at[f], device(fs[k], z, c))
+
+    sends_e = [[send_row(k, at) for k in (1, 2)] for at in range(3)]
+
+    def send_weights(k, *what):
+        for at in what:
+            staged, into, lanes, target = (
+                (SWG, WGU, units(0), units(0)),
+                (SWU, WGU, units(0), units(1)),
+                (SWG, WGU, units(1), units(2)),
+                (SWU, WGU, units(1), units(3)),
+                (SWD, WD, pl.ds(0, half_ff), pl.ds(0, half_ff)),
+            )[at]
+            weights[at // 2].append(
+                net.send(staged.at[:, zs[k], :, lanes], into.at[:, z, :, target], device(f, zs[k], c))
             )
 
     def places(shape, dim):
@@ -630,11 +679,8 @@
     for copy in sends_s:
         copy.wait_recv()
     sends_s2 = [net.send(SMB.at[f], SMB.at[f], device(fs[k], z, c)) for k in range(1, nf)]
-    sends_e = [
-        net.send(ref.at[row_experts(fs[k])], staged.at[f], device(fs[k], z, c))
-        for k in range(1, nf)
-        for ref, staged in shards
-    ]
+    for at in (0, 1):
+        sends_e[at].append(send_row(3, at))
     with jax.named_scope("tables1"):
         angle = offset.astype(f32) * fr_ref[0:1, :]
         CT[...] = jnp.cos(angle)
@@ -669,11 +715,10 @@
         kv = jnp.where(is_key, kv_part * cosine + swapped(kv_part) * sine, kv_part).astype(bf16)
         K[...] = kv[:, :HD]
         V[...] = kv[:, HD:]
-    arrive(chain_g)
-    chain_g = line.pass_on(1, view_g)
     for copy in sends_o:
         copy.wait_recv()
-    sends_o2 = [net.send(WO.at[f], WO.at[f], device(fs[k], z, c)) for k in range(1, nf)]
+    sends_o2 = [net.send(WO.at[f], WO.at[f], across[k]) for k in (1, 2)]
+    sends_e[2].append(send_row(3, 2))
 
     scale = HD ** (-0.5)
     step = 2 * hb
@@ -703,36 +748,28 @@
         net.send(ATT.at[:, zs[k]], AT.at[:, :, columns], device(f, zs[k], c)) for k in range(1, nz)
     ]
     AT[:, :, columns] = ATT[:, z]
+    for k in (1, 2):
+        part, to = ((lower, across[2]), (upper, across[1]))[k - 1]
+        sends_o2[k - 1].wait_recv()
+        sends_o2.append(net.send(WO.at[fs[k], part], WO.at[fs[k], part], to))
     arrive(chain_g)
-    chain_g = line.pass_on(2, view_g)
+    chain_g = line.pass_on(1, view_g)
+    chains.append(chain_g)
     for copy in loads[3:]:
         copy.wait()
-    for copy in sends_e:
-        copy.wait_recv()
-    send_weights(0, 3, (0, 1))
-    for copy in sends_a:
-        copy.wait_recv()
-    for copy in sends_o2:
-        copy.wait_recv()
-    wd_full = lambda: WD[...].reshape(width, half_ff)
-    wgu_full = lambda: WGU[...].reshape(width, 2 * half_ff)
-    lower, upper = pl.ds(0, nz // 2), pl.ds(nz // 2, nz // 2)
-    across = [None, device(fs[1], z, c), device(fs[2], z, c), device(fs[3], z, c)]
-
-    def second_hop(ref):
-        return [net.send(ref.at[f, c], ref.at[f, c], across[k]) for k in (1, 2)]
-
-    def third_hop(ref, k):
-        part, to = ((lower, across[2]), (upper, across[1]))[k - 1]
-        return net.send(ref.at[fs[k], c, part], ref.at[fs[k], c, part], to)
-
-    arrive(chain_g)
-    sends_g2 = second_hop(GA)
-    forwards_g = [net.send(GA.at[f, c], GA.at[f, c], partner)]
+    for copy in sends_e[0] + sends_e[1]:
+        copy.wait_recv()
+    send_weights(3, 0, 1)
+    for copy in sends_a + sends_o2[2:]:
+        copy.wait_recv()
+
     with jax.named_scope("proj"):
         part = dot_nt(AT[...].reshape(block, nz * 2 * HD), WO[...].reshape(width, nz * 2 * HD))
         PP[...] = part.reshape(2, hb, width)
     send_p = net.send(PP.at[other], PR, partner)
+    arrive(chain_g)
+    chain_g = line.pass_on(2, view_g)
+    chains.append(chain_g)
     x_own = X[c, z].astype(f32)
     gain_two = SMW[1:2, :].astype(f32)
     send_p.wait_recv()
@@ -753,18 +790,28 @@
     gates = weight / jnp.sum(weight, axis=0, keepdims=True)
     GTB[f, c, z] = jnp.concatenate([gates, jnp.zeros((experts, 128 - hb), f32)], axis=1)
     view_n = [lambda at: N2.at[f, c, at], lambda at: GTB.at[f, c, at]]
+    early = net.numbers(
+        sends_q, sends_s, sends_x, forwards_x, sends_o, sends_e[:2], sends_q2, sends_s2, sends_o2, sends_a, chains[:2], send_p
+    )
     chain_n = line.pass_on(0, view_n)
-    send_weights(0, 3, (2,))
-
+    chains = [chains[2], chain_n]
+    send_weights(2, 0)
+
+    arrive(chain_g)
+    sends_g2 = second_hop(GA)
+    forwards_g = [net.send(GA.at[f, c], GA.at[f, c], partner)]
     arrive(chain_n)
     chain_n = line.pass_on(1, view_n)
-    send_weights(0, 2, (0,))
+    chains.append(chain_n)
+    send_weights(2, 1)
     arrive(chain_n)
     chain_n = line.pass_on(2, view_n)
-    send_weights(0, 2, (1, 2))
-    send_weights(0, 1)
+    chains.append(chain_n)
+    send_weights(1, 0, 1)
+    for copy in sends_e[2]:
+        copy.wait_recv()
     for k in (3, 2, 1):
-        send_weights(1, k)
+        send_weights(k, 4)
     sends_g3 = []
     for k in (1, 2):
         sends_g2[k - 1].wait_recv()
@@ -775,9 +822,9 @@
     sends_t2 = [net.send(GTB.at[f, c], GTB.at[f, c], across[k]) for k in (1, 2, 3)]
     forwards_n = [net.send(N2.at[f, c], N2.at[f, c], partner)]
     forwards_t = [net.send(GTB.at[f, c], GTB.at[f, c], partner)]
-    for copy in sends_g3:
-        copy.wait_recv()
-    forwards_g.append(net.send(GA.at[fs[3], c], GA.at[fs[3], c], partner))
+    for k in (3, 2, 1):
+        send_weights(k, 2, 3)
+    before = range(len(net.copies) - 20)
 
     WGU[:, z, :, 0:unit] = SWG[:, z, :, 0:unit]
     WGU[:, z, :, unit : 2 * unit] = SWU[:, z, :, 0:unit]
@@ -813,11 +860,8 @@
     def expert_part(h, k):
         at_f = fs[k]
         tokens = N2[at_f].reshape(rows, width)
-        grads = GA[at_f].reshape(rows, width)
         with jax.named_scope("gateup"):
             PSX[...] = dot_nn(tokens, WGU[:, :, :, 2 * h * unit : 2 * (h + 1) * unit].reshape(width, 2 * unit))
-        with jax.named_scope("cotangent"):
-            AA[...] = dot_nn(grads, WD[:, :, :, h * unit : (h + 1) * unit].reshape(width, unit))
         if h == 0:
             with jax.named_scope("gatecol"):
                 for piece in range(2 * nz):
@@ -828,7 +872,7 @@
             at = pl.ds(pl.multiple_of(i * 64, 64), 64)
             gate_pre = PSX[at, 0:unit]
             up_pre = PSX[at, unit : 2 * unit]
-            raw = AA[at, :]
+            raw = AA[k, at, h * unit : (h + 1) * unit]
             gate = GC[k, at, :]
             sigmoid = jax.nn.sigmoid(gate_pre)
             silu = gate_pre * sigmoid
@@ -862,12 +906,16 @@
                         )
                     else:
                         GD[f, z, c] = GDS[0, :, lanes]
-            with jax.named_scope("mix"):
-                MP[at_f] = dot_nt(H[k], WD[...].reshape(width, half_ff)).astype(bf16).reshape(2, nz, hb, width)
-            exchange_m[k] = net.send(MP.at[at_f, other], MR.at[at_f], partner)
+
+    def mix(k):
+        with jax.named_scope("mix"):
+            MP[fs[k]] = dot_nt(H[k], WD[...].reshape(width, half_ff)).astype(bf16).reshape(2, nz, hb, width)
+        exchange_m[k] = net.send(MP.at[fs[k], other], MR.at[fs[k]], partner)
+
+    def weight_terms(h, k):
         with jax.named_scope("wgrad"):
-            gate_up = dot_tn(UG[k, :, 2 * h * unit : 2 * (h + 1) * unit], tokens)
-            down = dot_tn(H[k, :, h * unit : (h + 1) * unit], grads)
+            gate_up = dot_tn(UG[k, :, 2 * h * unit : 2 * (h + 1) * unit], N2[fs[k]].reshape(rows, width))
+            down = dot_tn(H[k, :, h * unit : (h + 1) * unit], GA[fs[k]].reshape(rows, width))
             first = k == (0, 3)[h]
             DGU[...] = gate_up if first else DGU[...] + gate_up
             DDT[...] = down if first else DDT[...] + down
@@ -877,6 +925,16 @@
             DGB[h] = jnp.transpose(DGU[...]).astype(bf16).reshape(nf, nz, shard, 2 * unit)
             DDB[h] = jnp.transpose(DDT[...]).astype(bf16).reshape(nf, nz, shard, unit)
 
+    def cotangent(k):
+        forwards_g[k].wait_recv()
+        with jax.named_scope("cotangent"):
+            AA[k] = dot_nn(GA[fs[k]].reshape(rows, width), WD[...].reshape(width, half_ff))
+
+    net.drain(before)
+    for copy in weights[2]:
+        copy.wait_recv()
+    for k in range(nf - 1):
+        cotangent(k)
     for copy in weights[0]:
         copy.wait_recv()
     for k in range(nf):
@@ -888,16 +946,20 @@
                 forwards_n.append(net.send(N2.at[fs[i], c], N2.at[fs[i], c], partner))
                 sends_t2[i - 1].wait_recv()
                 forwards_t.append(net.send(GTB.at[fs[i], c], GTB.at[fs[i], c], partner))
+            for copy in sends_g3:
+                copy.wait_recv()
+            forwards_g.append(net.send(GA.at[fs[3], c], GA.at[fs[3], c], partner))
         if k == 3:
+            cotangent(k)
             for copy in sends_n3:
                 copy.wait_recv()
             forwards_n.append(net.send(N2.at[fs[k], c], N2.at[fs[k], c], partner))
             sends_t2[2].wait_recv()
             forwards_t.append(net.send(GTB.at[fs[k], c], GTB.at[fs[k], c], partner))
-        forwards_g[k].wait_recv()
         forwards_n[k].wait_recv()
         forwards_t[k].wait_recv()
         expert_part(0, k)
+        weight_terms(0, k)
     shed(0)
     for k in (3, 2, 1):
         send_grads(0, k)
@@ -929,41 +991,45 @@
         return [net.send(part.at[at_f, c, at], into.at[k - 1, at], across[k]) for at in order]
 
     sends_m = {}
+    middle = net.numbers(
+        sends_e[2:], sends_g2, sends_g3, forwards_g, *weights, chains, sends_n2, sends_n3, sends_t2,
+        forwards_n, forwards_t,
+    )
+    net.free(early)
     expert_part(1, 3)
+    weight_terms(1, 3)
+    mix(3)
     firsts_b = spread(3, exchange_b, BP, BR, BOWN, RBV, RB, in_order)
-    firsts_m = spread(3, exchange_m, MP, MR, MOWN, RMV, RM, in_order)
-    expert_part(1, 1)
-    expert_part(1, 2)
+    for k in (1, 2, 0):
+        expert_part(1, k)
     for k in (1, 2):
         exchange_b[k].wait_recv()
         sends_b[k] = spread_near(k, firsts_b, BP, BR, RBV, RB, in_order)
-    expert_part(1, 0)
-    for k in (1, 2):
-        exchange_m[k].wait_recv()
-        sends_m[k] = spread_near(k, firsts_m, MP, MR, RMV, RM, in_order)
     spread(0, exchange_b, BP, BR, BOWN, RBV, RB, in_order)
-    spread(0, exchange_m, MP, MR, MOWN, RMV, RM, in_order)
-
+    firsts_m = spread(3, exchange_m, MP, MR, MOWN, RMV, RM, in_order)
+    for k in (1, 2, 0):
+        mix(k)
+        weight_terms(1, k)
+
+    expert_copies = len(net.copies)
     shed(1)
-    send_grads(1, 3)
-
-    for copy in sends_d:
-        copy.wait_recv()
-    dots = jnp.concatenate(
-        [
-            GD[e // nz, e % nz, 0][0:1, :] + GD[e // nz, e % nz, 1][0:1, :]
-            for e in range(experts)
-        ],
-        axis=0,
-    )
-    dots = jnp.where(lax.rem(z, 2) == 0, dots, pltpu.roll(dots, 128 - hb, 1))[:, 0:hb]
-    gates = GTB[f, c, z][:, 0:hb]
-    logit_grad = gates * (dots - jnp.sum(gates * dots, axis=0, keepdims=True))
-    router_t = SMW[16 : 16 + experts, :].astype(f32)
-    SG[0:experts, :] = dot_nn(logit_grad, N2[f, c, z].astype(f32), lax.Precision.HIGHEST)
-    GRES[...] = dot_tn(logit_grad, router_t, lax.Precision.HIGHEST)
-    residual = RES[...]
-    inverse_two = lax.rsqrt(jnp.mean(residual * residual, axis=1, keepdims=True) + epsilon)
+
+    def dots_back():
+        for copy in sends_d:
+            copy.wait_recv()
+        dots = jnp.concatenate(
+            [
+                GD[e // nz, e % nz, 0][0:1, :] + GD[e // nz, e % nz, 1][0:1, :]
+                for e in range(experts)
+            ],
+            axis=0,
+        )
+        dots = jnp.where(lax.rem(z, 2) == 0, dots, pltpu.roll(dots, 128 - hb, 1))[:, 0:hb]
+        gates = GTB[f, c, z][:, 0:hb]
+        logit_grad = gates * (dots - jnp.sum(gates * dots, axis=0, keepdims=True))
+        router_t = SMW[16 : 16 + experts, :].astype(f32)
+        SG[0:experts, :] = dot_nn(logit_grad, N2[f, c, z].astype(f32), lax.Precision.HIGHEST)
+        GRES[...] = dot_tn(logit_grad, router_t, lax.Precision.HIGHEST)
 
     own_b, out_b, into_b = (lambda at: BOWN.at[at]), (lambda w, t: CO.at[w, t]), (lambda w, t: CI.at[w, t])
 
@@ -981,8 +1047,13 @@
             at_sums = len(net.copies)
             chain_b = line.add_on(t, own_b, out_b, into_b)
             sums.extend(range(at_sums, len(net.copies)))
+        if t == 0:
+            dots_back()
     line.finish(BOWN.at[z], into_b)
-
+    net.free(middle)
+
+    residual = RES[...]
+    inverse_two = lax.rsqrt(jnp.mean(residual * residual, axis=1, keepdims=True) + epsilon)
     grad_two = BOWN[z] + GRES[...]
     scaled = grad_two * gain_two
     grad_res = (
@@ -993,6 +1064,10 @@
     GRES[...] = grad_res
     RL[c] = grad_res.astype(bf16)
     send_r = net.send(RL.at[c], RL.at[c], partner)
+    for k in (1, 2):
+        exchange_m[k].wait_recv()
+        sends_m[k] = spread_near(k, firsts_m, MP, MR, RMV, RM, in_order)
+    spread(0, exchange_m, MP, MR, MOWN, RMV, RM, in_order)
     gain_term = jnp.sum(grad_two * residual * inverse_two, axis=0, keepdims=True)
     SG[experts : experts + 8, :] = jnp.broadcast_to(gain_term, (8, width))
     wide = width // nf
@@ -1011,14 +1086,8 @@
         for k in range(1, nz)
     ]
     AGR[:, z] = AGS[:, :, columns]
-    for k in (1, 2):
-        for at in range(nz):
-            sends_m[k][at].wait_recv()
-        MOWN[...] += RM[k - 1].astype(f32)
-    own_m, out_m, into_m = (lambda at: MOWN.at[at]), (lambda w, t: MO.at[w, t]), (lambda w, t: MI.at[w, t])
-    chain_m = line.add_on(0, own_m, out_m, into_m)
-    send_grads(1, 2)
-    send_grads(1, 1)
+    for k in (1, 3, 2):
+        send_grads(1, k)
     with jax.named_scope("outgrad"):
         DWO[...] = (
             dot_tn(low, AT[...].reshape(block, nz * 2 * HD))
@@ -1027,6 +1096,7 @@
         )
     sends_wo = [net.send(DWO.at[fs[k]], RWO.at[k - 1], device(fs[k], z, c)) for k in range(1, nf)]
 
+    net.drain(range(expert_copies))
     for copy in sends_ag:
         copy.wait_recv()
 
@@ -1063,8 +1133,6 @@
     with jax.named_scope("ingrad"):
         NG[...] = dot_nt(DQKV[...], WQ[...].reshape(width, 4 * HD)).astype(bf16).reshape(2, nz, hb, width)
     send_ng = net.send(NG.at[other], NR, partner)
-    arrive(chain_m)
-    chain_m = line.add_on(1, own_m, out_m, into_m)
     with jax.named_scope("qkvgrad"):
         DWQ[...] = (
             jnp.transpose(dot_tn(DQKV[...], N1[...])).astype(bf16).reshape(nf, nz, shard, 4 * HD)
@@ -1081,14 +1149,21 @@
     net.drain(sums)
     BOWN[...] = NG[c].astype(f32) + NR[...].astype(f32)
     chain_g1 = line.add_on(0, own_b, out_b, into_b)
-    arrive(chain_m)
-    chain_m = line.add_on(2, own_m, out_m, into_m)
+    for k in (1, 2):
+        for at in range(nz):
+            sends_m[k][at].wait_recv()
+        MOWN[...] += RM[k - 1].astype(f32)
+    own_m, out_m, into_m = (lambda at: MOWN.at[at]), (lambda w, t: MO.at[w, t]), (lambda w, t: MI.at[w, t])
+    chain_m = line.add_on(0, own_m, out_m, into_m)
     arrive(chain_g1)
     chain_g1 = line.add_on(1, own_b, out_b, into_b)
-
+    arrive(chain_m)
+    chain_m = line.add_on(1, own_m, out_m, into_m)
     spread_grads(0)
     arrive(chain_g1)
     chain_g1 = line.add_on(2, own_b, out_b, into_b)
+    arrive(chain_m)
+    chain_m = line.add_on(2, own_m, out_m, into_m)
 
     total = DWO[f].astype(f32)
     for k in range(1, nf):
@@ -1104,13 +1179,6 @@
     ZWQ[...] = total.astype(bf16)
     sends_wq2 = [net.send(ZWQ.at[zs[k]], LWQ.at[z], device(f, zs[k], c)) for k in range(1, nz)]
     LWQ[z] = ZWQ[z]
-    spread_grads(1)
-    small = SGT[:, pair_lanes(z)]
-    for k in range(1, nz):
-        sends_sz[k - 1].wait_recv()
-        small = small + SGZ[k - 1]
-    SGP[0] = small
-    send_sp = net.send(SGP.at[0], SGP.at[1], partner)
     arrive(chain_g1)
     line.finish(BOWN.at[z], into_b)
     grad_one = BOWN[z]
@@ -1127,6 +1195,13 @@
         - x_own * (inverse * inverse * inverse) * jnp.mean(scaled * x_own, axis=1, keepdims=True)
     )
     send_ig = net.send(EXG.at[c], EXG.at[c], partner)
+    small = SGT[:, pair_lanes(z)]
+    for k in range(1, nz):
+        sends_sz[k - 1].wait_recv()
+        small = small + SGZ[k - 1]
+    SGP[0] = small
+    send_sp = net.send(SGP.at[0], SGP.at[1], partner)
+    net.drain(range(expert_copies))
     send_g1.wait_recv()
     SG1P[...] = SG1[0] + SG1[1]
     lanes_of = lambda df, dz: pl.ds(pl.multiple_of((df * (nz // 2) + lax.div(dz, 2)) * 128, 128), 128)
@@ -1136,6 +1211,7 @@
     ]
     RSG1[f, z] = SG1P[:, lanes_of(f, z)]
 
+    spread_grads(1)
     arrive(chain_m)
     line.finish(MOWN.at[z], into_m)
     EXB[c] = (RES[...] + MOWN[z]).astype(bf16)
@@ -1148,17 +1224,20 @@
     for j in range(1, nz):
         total = total + LWO[j].astype(f32)
     dwo_out[...] = total
+    outs = []
+
+    def leave(source, target):
+        copy = pltpu.make_async_copy(source, target, local_sems.at[6 + len(outs)])
+        copy.start()
+        outs.append(copy)
+
     for copy in sends_wq2:
         copy.wait_recv()
-    dqkv_out[...] = LWQ[...]
-    for copy in grads_f[0] + grads_f[1]:
-        copy.wait_recv()
-    outs = [
-        pltpu.make_async_copy(GUL, dgu_out, local_sems.at[8]),
-        pltpu.make_async_copy(DDL, dd_out, local_sems.at[9]),
-    ]
-    for copy in outs:
-        copy.start()
+    leave(LWQ, dqkv_out)
+    send_bo.wait_recv()
+    leave(EXB, block_out)
+    send_ig.wait_recv()
+    leave(EXG, input_grad)
     for copy in sends_g1:
         copy.wait_recv()
     small = jnp.zeros((1, 128), f32)
@@ -1166,13 +1245,15 @@
         for j in range(nz):
             small = small + RSG1[i, j, 0:1]
     gain_out[...] = jnp.broadcast_to(small, (8, 128))
-    send_bo.wait_recv()
-    block_out[...] = EXB[...].reshape(block, width)
-    send_ig.wait_recv()
-    input_grad[...] = EXG[...].reshape(block, width)
-    for copy in outs:
-        copy.wait()
-    net.drain()
+    for copy in grads_f[0] + grads_f[1]:
+        copy.wait_recv()
+    leave(GUL, dgu_out)
+    leave(DDL, dd_out)
+    with jax.named_scope("drain"):
+        net.drain()
+    with jax.named_scope("outs"):
+        for copy in outs:
+            copy.wait()
 
 
 def finish_kernel(
@@ -1235,7 +1316,7 @@
         N2=((nf, 2, nz, hb, width), bf16), GTB=((nf, 2, nz, experts, 128), f32), GA=((nf, 2, nz, hb, width), bf16),
         WGU=((nf, nz, shard, 2 * half_ff), bf16), WD=((nf, nz, shard, half_ff), bf16),
         SWG=((nf, nz, shard, half_ff), bf16), SWU=((nf, nz, shard, half_ff), bf16), SWD=((nf, nz, shard, half_ff), bf16),
-        AA=((rows, half_ff // 2), f32), PSX=((rows, half_ff), f32), GC=((nf, rows, 128), f32),
+        AA=((nf, rows, half_ff), f32), PSX=((rows, half_ff), f32), GC=((nf, rows, 128), f32),
         H=((nf, rows, half_ff), bf16), UG=((nf, rows, 2 * half_ff), bf16), PRD=((rows, half_ff // 2), bf16),
         MP=((nf, 2, nz, hb, width), bf16), MR=((nf, nz, hb, width), bf16),
         BP=((nf, 2, nz, hb, width), bf16), BR=((nf, nz, hb, width), bf16),
@@ -1261,20 +1342,20 @@
         SG1=((2, 8, width), f32), SG1P=((8, width), f32), RSG1=((nf, nz, 8, 128), f32),
         EXB=((2, hb, width), bf16), EXG=((2, hb, width), f32),
     )
-    slots = 320
+    slots = (136, 160)
     out = pl.pallas_call(
         functools.partial(layer_kernel, (nf, nz, hb, width, experts, half_ff, ndoc, chosen)),
         name="layer",
         out_shape=(
-            shape((block, width), bf16), shape((block, width), f32), shape((experts + 8, 128), f32),
+            shape((2, hb, width), bf16), shape((2, hb, width), f32), shape((experts + 8, 128), f32),
             shape((8, 128), f32), shape((nz, shard, 4 * HD), bf16), shape((shard, W), f32),
             shape((nf, nz, shard, 2 * half_ff), bf16), shape((nf, nz, shard, half_ff), bf16),
         ),
         in_specs=[anywhere] * 2 + [vm] * 3 + [anywhere] + [vm] * 3 + [anywhere] * 3
         + [pl.BlockSpec(memory_space=pltpu.SMEM), vm, vm],
-        out_specs=(vm,) * 6 + (anywhere,) * 2,
+        out_specs=(anywhere,) * 2 + (vm,) * 2 + (anywhere, vm) + (anywhere,) * 2,
         scratch_shapes=[pltpu.VMEM(s, d) for s, d in scratch.values()]
-        + [pltpu.SemaphoreType.DMA((slots,)), pltpu.SemaphoreType.DMA((slots,)), pltpu.SemaphoreType.DMA((10,))],
+        + [pltpu.SemaphoreType.DMA((slots[0],)), pltpu.SemaphoreType.DMA((slots[1],)), pltpu.SemaphoreType.DMA((11,))],
         compiler_params=pltpu.CompilerParams(
             collective_id=0, has_side_effects=True, vmem_limit_bytes=67043328
         ),
@@ -1283,7 +1364,7 @@
         attention_gain[None], expert_gain[None], router_weight.T, gate_weight, up_weight, down_weight,
         doc_lengths, expert_choice[0].T, frequency,
     )
-    steps = nz
+    steps = nz // 2
     some = lambda *s: pl.BlockSpec(s, lambda i: (i,) + (0,) * (len(s) - 1))
     whole = lambda *s: pl.BlockSpec(s, lambda i: (0,) * len(s))
     per = nf * nz // steps
@@ -1307,8 +1388,8 @@
             whole(shard, nz * 2 * HD), whole(shard, nz * HD), whole(shard, nz * HD), whole(shard, W), whole(1, shard),
             whole(experts, shard), some(per, shard, half_ff), some(per, shard, half_ff), some(per, shard, half_ff),
         ),
-        compiler_params=pltpu.CompilerParams(vmem_limit_bytes=33554432),
-    )(*out[:6], out[6].reshape(experts, shard, 2 * half_ff), out[7].reshape(experts, shard, half_ff))
+        compiler_params=pltpu.CompilerParams(vmem_limit_bytes=67043328),
+    )(out[0].reshape(block, width), out[1].reshape(block, width), *out[2:6], out[6].reshape(experts, shard, 2 * half_ff), out[7].reshape(experts, shard, half_ff))
     block_out, input_grad, gain1, q, k, v, o, gain2, router, gate, up, down = out
     return (
         block_out[None], input_grad[None], gain1[0], q, k, v, o, gain2[0], router.T, gate, up, down,

time: 193 us -> 180 us (0.933)
  local copies, waits for them, and re-layouts: 6.76 us -> 0 us
  Pallas kernels: 185 us -> 179 us
    pallas_call x1, Pallas kernels: 183 us -> 175 us  [fast_local(): pl.pallas_call(functools.partial(layer_kernel, (nf, nz, hb, width, expert...]
    unnamed x16 -> x0, local copies, waits for them, and re-layouts: 6.76 us -> none
where the time goes in v4:
time: 180 us; the launch traced here: 179 us
  Pallas kernels  179 us (99%)
    pallas_call x1, Pallas kernels, fast_local(): pl.pallas_call(functools.partial(layer_kernel, (nf, nz, hb, width, expert...  175 us
    pallas_call x1, Pallas kernels, fast_local(): pl.pallas_call(functools.partial(finish_kernel, (nz, experts, half_ff, sh...  3.75 us

profile of v4, /device:TPU:0, one launch (start us, length us, event | category | flops | bytes accessed | tf_op | source)
XLA Modules:
  0.0 179.4 jit_solution(11465475343975529561)
XLA Ops:
  0.6 174.8 %layer.1 = (bf16[2,64,1024]{2,1,0:T(8,128)(2,1)}, f32[2,64,1024]{2,1,0:T(8,128)}, f32[24,128]{1,0:T(8,128)}, f32[8,128]{1,0:T(8,128)}, bf16[4,64,256]{2,1,0:T(8,...) custom-call(bf16[128,1024]{1,0:T(8,128)(2,1)} %bitcast.20, ...), custom_call_target="tpu_custom_call" | custom-call | tf_op jit(solution)/shard_map/layer/pallas_call | solution.py:1346
  175.5 3.7 %finish.1 = (bf16[128,1024]{1,0:T(8,128)(2,1)}, f32[128,1024]{1,0:T(8,128)}, f32[1,64]{1,0:T(1,128)}, f32[64,512]{1,0:T(8,128)}, f32[64,256]{1,0:T(8,128)}, /*in...) custom-call(bf16[128,1024]{1,0:T(8,128)(2,1)} %bitcast.22, ...), custom_call_target="tpu_custom_call" | custom-call | tf_op jit(solution)/shard_map/finish/pallas_call | solution.py:1371

commit v5 on v4

--- a/solution.py
+++ b/solution.py
@@ -449,6 +449,26 @@
         copy.start()
         return copy
 
+    def together(self, triples, whole):
+        first = self.make(*triples[0])
+        send_at, recv_at = self.slots[-1]
+        first.start()
+        for source, target, device in triples[1:]:
+            pltpu.make_async_remote_copy(
+                src_ref=source,
+                dst_ref=target,
+                send_sem=self.send_sems.at[send_at],
+                recv_sem=self.recv_sems.at[recv_at],
+                device_id=device,
+                device_id_type=MESH,
+            ).start()
+        waits = Whole(
+            pltpu.make_async_copy(whole, whole, self.send_sems.at[send_at]),
+            pltpu.make_async_copy(whole, whole, self.recv_sems.at[recv_at]),
+        )
+        self.copies[-1] = (waits, None)
+        return waits
+
     def free(self, among):
         self.free_recv.extend(self.slots[at][1] for at in among)
 
@@ -472,6 +492,11 @@
                 copy.wait_send()
             else:
                 pl.when(sends)(copy.wait_send)
+
+
+class Whole:
+    def __init__(self, sent, received):
+        self.wait_send, self.wait_recv = sent.wait, received.wait
 
 
 class Line:
@@ -541,7 +566,7 @@
     N2, GTB, GA, WGU, WD, SWG, SWU, SWD, AA, PSX, GC, H, UG, PRD, MP, MR, BP, BR, DGU, DDT, GDS, GD,
     RB, RM, RBV, RMV, BOWN, MOWN, CO, CI, MO, MI, DGB, GUL, ZG, DDB, DDL, ZD, SG, SGF, SGT, SGZ, SGP, GRES, RL,
     AGS, AGR, DWO, RWO, ZWO, LWO, DS, DQ, DQKV, NG, NR, DWQ, RWQ, ZWQ, LWQ,
-    SG1, SG1P, RSG1, EXB, EXG,
+    SGW, SG1, SG1P, RSG1, EXB, EXG,
     send_sems, recv_sems, local_sems,
 ):
     nf, nz, hb, width, experts, half_ff, ndoc, chosen = dims
@@ -896,16 +921,18 @@
             dots = dot_nt(jnp.ones((8, unit), bf16), PRD[...])
             GDS[k] = dots if h == 0 else GDS[k] + dots
         if h == 1:
+            sets = []
             for j in range(nz):
                 for t in range(2):
                     to_z, to_c = zs[j], lax.rem(c + t, 2)
                     lanes = pl.ds(pl.multiple_of((to_c * (nz // 2) + lax.div(to_z, 2)) * 128, 128), 128)
                     if (k, j, t) != (0, 0, 0):
-                        sends_d.append(
-                            net.send(GDS.at[k, pl.ds(0, 1), lanes], GD.at[f, z, c, pl.ds(0, 1)], device(at_f, to_z, to_c))
+                        sets.append(
+                            (GDS.at[k, pl.ds(0, 1), lanes], GD.at[f, z, c, pl.ds(0, 1)], device(at_f, to_z, to_c))
                         )
                     else:
                         GD[f, z, c] = GDS[0, :, lanes]
+            sends_d.append(net.together(sets, SGW.at[pl.ds(0, len(sets))]))
 
     def mix(k):
         with jax.named_scope("mix"):
@@ -1049,6 +1076,8 @@
             sums.extend(range(at_sums, len(net.copies)))
         if t == 0:
             dots_back()
+        if t == 2:
+            spread_grads(0)
     line.finish(BOWN.at[z], into_b)
     net.free(middle)
 
@@ -1064,15 +1093,15 @@
     GRES[...] = grad_res
     RL[c] = grad_res.astype(bf16)
     send_r = net.send(RL.at[c], RL.at[c], partner)
-    for k in (1, 2):
-        exchange_m[k].wait_recv()
-        sends_m[k] = spread_near(k, firsts_m, MP, MR, RMV, RM, in_order)
-    spread(0, exchange_m, MP, MR, MOWN, RMV, RM, in_order)
     gain_term = jnp.sum(grad_two * residual * inverse_two, axis=0, keepdims=True)
     SG[experts : experts + 8, :] = jnp.broadcast_to(gain_term, (8, width))
     wide = width // nf
     block_lanes = lambda at: pl.ds(pl.multiple_of(at * wide, 128), wide)
     sends_sg = [net.send(SG.at[:, block_lanes(fs[k])], SGF.at[k - 1], device(fs[k], z, c)) for k in range(1, nf)]
+    for k in (1, 2):
+        exchange_m[k].wait_recv()
+        sends_m[k] = spread_near(k, firsts_m, MP, MR, RMV, RM, in_order)
+    spread(0, exchange_m, MP, MR, MOWN, RMV, RM, in_order)
     send_r.wait_recv()
     low = RL[...].reshape(block, width)
     with jax.named_scope("attgrad"):
@@ -1138,13 +1167,6 @@
             jnp.transpose(dot_tn(DQKV[...], N1[...])).astype(bf16).reshape(nf, nz, shard, 4 * HD)
         )
     sends_wq = [net.send(DWQ.at[fs[k]], RWQ.at[k - 1], device(fs[k], z, c)) for k in range(1, nf)]
-    small = SG[:, block_lanes(f)]
-    for k in range(1, nf):
-        sends_sg[k - 1].wait_recv()
-        small = small + SGF[k - 1]
-    SGT[...] = small
-    pair_lanes = lambda at: pl.ds(pl.multiple_of(lax.div(at, 2) * 128, 128), 128)
-    sends_sz = [net.send(SGT.at[:, pair_lanes(zs[k])], SGZ.at[k - 1], device(f, zs[k], c)) for k in range(1, nz)]
     send_ng.wait_recv()
     net.drain(sums)
     BOWN[...] = NG[c].astype(f32) + NR[...].astype(f32)
@@ -1159,12 +1181,34 @@
     chain_g1 = line.add_on(1, own_b, out_b, into_b)
     arrive(chain_m)
     chain_m = line.add_on(1, own_m, out_m, into_m)
-    spread_grads(0)
     arrive(chain_g1)
     chain_g1 = line.add_on(2, own_b, out_b, into_b)
     arrive(chain_m)
     chain_m = line.add_on(2, own_m, out_m, into_m)
 
+    arrive(chain_g1)
+    line.finish(BOWN.at[z], into_b)
+    grad_one = BOWN[z]
+    gain_one = SMW[0:1, :].astype(f32)
+    x_own = X[c, z].astype(f32)
+    inverse = lax.rsqrt(jnp.mean(x_own * x_own, axis=1, keepdims=True) + epsilon)
+    gain_term = jnp.sum(grad_one * x_own * inverse, axis=0, keepdims=True)
+    SG1[0] = jnp.broadcast_to(gain_term, (8, width))
+    send_g1 = net.send(SG1.at[0], SG1.at[1], partner)
+    scaled = grad_one * gain_one
+    EXG[c] = (
+        GRES[...]
+        + inverse * scaled
+        - x_own * (inverse * inverse * inverse) * jnp.mean(scaled * x_own, axis=1, keepdims=True)
+    )
+    send_ig = net.send(EXG.at[c], EXG.at[c], partner)
+    small = SG[:, block_lanes(f)]
+    for k in range(1, nf):
+        sends_sg[k - 1].wait_recv()
+        small = small + SGF[k - 1]
+    SGT[...] = small
+    pair_lanes = lambda at: pl.ds(pl.multiple_of(lax.div(at, 2) * 128, 128), 128)
+    sends_sz = [net.send(SGT.at[:, pair_lanes(zs[k])], SGZ.at[k - 1], device(f, zs[k], c)) for k in range(1, nz)]
     total = DWO[f].astype(f32)
     for k in range(1, nf):
         sends_wo[k - 1].wait_recv()
@@ -1179,22 +1223,6 @@
     ZWQ[...] = total.astype(bf16)
     sends_wq2 = [net.send(ZWQ.at[zs[k]], LWQ.at[z], device(f, zs[k], c)) for k in range(1, nz)]
     LWQ[z] = ZWQ[z]
-    arrive(chain_g1)
-    line.finish(BOWN.at[z], into_b)
-    grad_one = BOWN[z]
-    gain_one = SMW[0:1, :].astype(f32)
-    x_own = X[c, z].astype(f32)
-    inverse = lax.rsqrt(jnp.mean(x_own * x_own, axis=1, keepdims=True) + epsilon)
-    gain_term = jnp.sum(grad_one * x_own * inverse, axis=0, keepdims=True)
-    SG1[0] = jnp.broadcast_to(gain_term, (8, width))
-    send_g1 = net.send(SG1.at[0], SG1.at[1], partner)
-    scaled = grad_one * gain_one
-    EXG[c] = (
-        GRES[...]
-        + inverse * scaled
-        - x_own * (inverse * inverse * inverse) * jnp.mean(scaled * x_own, axis=1, keepdims=True)
-    )
-    send_ig = net.send(EXG.at[c], EXG.at[c], partner)
     small = SGT[:, pair_lanes(z)]
     for k in range(1, nz):
         sends_sz[k - 1].wait_recv()
@@ -1205,10 +1233,11 @@
     send_g1.wait_recv()
     SG1P[...] = SG1[0] + SG1[1]
     lanes_of = lambda df, dz: pl.ds(pl.multiple_of((df * (nz // 2) + lax.div(dz, 2)) * 128, 128), 128)
-    sends_g1 = [
-        net.send(SG1P.at[pl.ds(0, 1), lanes_of(fs[i], zs[j])], RSG1.at[f, z, pl.ds(0, 1)], device(fs[i], zs[j], c))
+    sets = [
+        (SG1P.at[pl.ds(0, 1), lanes_of(fs[i], zs[j])], RSG1.at[f, z, pl.ds(0, 1)], device(fs[i], zs[j], c))
         for i, j in same
     ]
+    sends_g1 = [net.together(sets, SGW.at[pl.ds(0, len(sets))])]
     RSG1[f, z] = SG1P[:, lanes_of(f, z)]
 
     spread_grads(1)
@@ -1339,10 +1368,10 @@
         DQKV=((rows, 4 * HD), bf16), NG=((2, nz, hb, width), bf16), NR=((nz, hb, width), bf16),
         DWQ=((nf, nz, shard, 4 * HD), bf16), RWQ=((nf - 1, nz, shard, 4 * HD), bf16),
         ZWQ=((nz, shard, 4 * HD), bf16), LWQ=((nz, shard, 4 * HD), bf16),
-        SG1=((2, 8, width), f32), SG1P=((8, width), f32), RSG1=((nf, nz, 8, 128), f32),
+        SGW=((16, 128), f32), SG1=((2, 8, width), f32), SG1P=((8, width), f32), RSG1=((nf, nz, 8, 128), f32),
         EXB=((2, hb, width), bf16), EXG=((2, hb, width), f32),
     )
-    slots = (136, 160)
+    slots = (96, 104)
     out = pl.pallas_call(
         functools.partial(layer_kernel, (nf, nz, hb, width, experts, half_ff, ndoc, chosen)),
         name="layer",

time: 180 us -> 179 us (level)
  no operation moved by 1% of the time
where the time goes in v5:
time: 179 us; the launch traced here: 178 us
  Pallas kernels  178 us (99%)
    pallas_call x1, Pallas kernels, fast_local(): pl.pallas_call(functools.partial(layer_kernel, (nf, nz, hb, width, expert...  174 us
    pallas_call x1, Pallas kernels, fast_local(): pl.pallas_call(functools.partial(finish_kernel, (nz, experts, half_ff, sh...  3.75 us

profile of v5, /device:TPU:0, one launch (start us, length us, event | category | flops | bytes accessed | tf_op | source)
XLA Modules:
  0.0 178.5 jit_solution(3172091517111925409)
XLA Ops:
  0.6 173.9 %layer.1 = (bf16[2,64,1024]{2,1,0:T(8,128)(2,1)}, f32[2,64,1024]{2,1,0:T(8,128)}, f32[24,128]{1,0:T(8,128)}, f32[8,128]{1,0:T(8,128)}, bf16[4,64,256]{2,1,0:T(8,...) custom-call(bf16[128,1024]{1,0:T(8,128)(2,1)} %bitcast.20, ...), custom_call_target="tpu_custom_call" | custom-call | tf_op jit(solution)/shard_map/layer/pallas_call | solution.py:1375
  174.5 3.7 %finish.1 = (bf16[128,1024]{1,0:T(8,128)(2,1)}, f32[128,1024]{1,0:T(8,128)}, f32[1,64]{1,0:T(1,128)}, f32[64,512]{1,0:T(8,128)}, f32[64,256]{1,0:T(8,128)}, /*in...) custom-call(bf16[128,1024]{1,0:T(8,128)(2,1)} %bitcast.22, ...), custom_call_target="tpu_custom_call" | custom-call | tf_op jit(solution)/shard_map/finish/pallas_call | solution.py:1400

commit v6 on v5

--- a/solution.py
+++ b/solution.py
@@ -566,7 +566,7 @@
     N2, GTB, GA, WGU, WD, SWG, SWU, SWD, AA, PSX, GC, H, UG, PRD, MP, MR, BP, BR, DGU, DDT, GDS, GD,
     RB, RM, RBV, RMV, BOWN, MOWN, CO, CI, MO, MI, DGB, GUL, ZG, DDB, DDL, ZD, SG, SGF, SGT, SGZ, SGP, GRES, RL,
     AGS, AGR, DWO, RWO, ZWO, LWO, DS, DQ, DQKV, NG, NR, DWQ, RWQ, ZWQ, LWQ,
-    SGW, SG1, SG1P, RSG1, EXB, EXG,
+    SMO, GNO, DWF, SGW, SG1, SG1P, RSG1, EXB, EXG,
     send_sems, recv_sems, local_sems,
 ):
     nf, nz, hb, width, experts, half_ff, ndoc, chosen = dims
@@ -742,7 +742,7 @@
         V[...] = kv[:, HD:]
     for copy in sends_o:
         copy.wait_recv()
-    sends_o2 = [net.send(WO.at[f], WO.at[f], across[k]) for k in (1, 2)]
+    sends_o2 = [net.send(WO.at[f], WO.at[f], across[k]) for k in (1, 2, 3)]
     sends_e[2].append(send_row(3, 2))
 
     scale = HD ** (-0.5)
@@ -773,10 +773,6 @@
         net.send(ATT.at[:, zs[k]], AT.at[:, :, columns], device(f, zs[k], c)) for k in range(1, nz)
     ]
     AT[:, :, columns] = ATT[:, z]
-    for k in (1, 2):
-        part, to = ((lower, across[2]), (upper, across[1]))[k - 1]
-        sends_o2[k - 1].wait_recv()
-        sends_o2.append(net.send(WO.at[fs[k], part], WO.at[fs[k], part], to))
     arrive(chain_g)
     chain_g = line.pass_on(1, view_g)
     chains.append(chain_g)
@@ -785,7 +781,7 @@
     for copy in sends_e[0] + sends_e[1]:
         copy.wait_recv()
     send_weights(3, 0, 1)
-    for copy in sends_a + sends_o2[2:]:
+    for copy in sends_a + sends_o2:
         copy.wait_recv()
 
     with jax.named_scope("proj"):
@@ -1098,10 +1094,6 @@
     wide = width // nf
     block_lanes = lambda at: pl.ds(pl.multiple_of(at * wide, 128), wide)
     sends_sg = [net.send(SG.at[:, block_lanes(fs[k])], SGF.at[k - 1], device(fs[k], z, c)) for k in range(1, nf)]
-    for k in (1, 2):
-        exchange_m[k].wait_recv()
-        sends_m[k] = spread_near(k, firsts_m, MP, MR, RMV, RM, in_order)
-    spread(0, exchange_m, MP, MR, MOWN, RMV, RM, in_order)
     send_r.wait_recv()
     low = RL[...].reshape(block, width)
     with jax.named_scope("attgrad"):
@@ -1115,6 +1107,10 @@
         for k in range(1, nz)
     ]
     AGR[:, z] = AGS[:, :, columns]
+    for k in (1, 2):
+        exchange_m[k].wait_recv()
+        sends_m[k] = spread_near(k, firsts_m, MP, MR, RMV, RM, in_order)
+    spread(0, exchange_m, MP, MR, MOWN, RMV, RM, in_order)
     for k in (1, 3, 2):
         send_grads(1, k)
     with jax.named_scope("outgrad"):
@@ -1245,14 +1241,6 @@
     line.finish(MOWN.at[z], into_m)
     EXB[c] = (RES[...] + MOWN[z]).astype(bf16)
     send_bo = net.send(EXB.at[c], EXB.at[c], partner)
-    send_sp.wait_recv()
-    small_out[...] = SGP[0] + SGP[1]
-    for copy in sends_wo2:
-        copy.wait_recv()
-    total = LWO[0].astype(f32)
-    for j in range(1, nz):
-        total = total + LWO[j].astype(f32)
-    dwo_out[...] = total
     outs = []
 
     def leave(source, target):
@@ -1260,6 +1248,16 @@
         copy.start()
         outs.append(copy)
 
+    send_sp.wait_recv()
+    SMO[...] = SGP[0] + SGP[1]
+    leave(SMO, small_out)
+    for copy in sends_wo2:
+        copy.wait_recv()
+    total = LWO[0].astype(f32)
+    for j in range(1, nz):
+        total = total + LWO[j].astype(f32)
+    DWF[...] = total
+    leave(DWF, dwo_out)
     for copy in sends_wq2:
         copy.wait_recv()
     leave(LWQ, dqkv_out)
@@ -1273,7 +1271,8 @@
     for i in range(nf):
         for j in range(nz):
             small = small + RSG1[i, j, 0:1]
-    gain_out[...] = jnp.broadcast_to(small, (8, 128))
+    GNO[...] = jnp.broadcast_to(small, (8, 128))
+    leave(GNO, gain_out)
     for copy in grads_f[0] + grads_f[1]:
         copy.wait_recv()
     leave(GUL, dgu_out)
@@ -1368,7 +1367,7 @@
         DQKV=((rows, 4 * HD), bf16), NG=((2, nz, hb, width), bf16), NR=((nz, hb, width), bf16),
         DWQ=((nf, nz, shard, 4 * HD), bf16), RWQ=((nf - 1, nz, shard, 4 * HD), bf16),
         ZWQ=((nz, shard, 4 * HD), bf16), LWQ=((nz, shard, 4 * HD), bf16),
-        SGW=((16, 128), f32), SG1=((2, 8, width), f32), SG1P=((8, width), f32), RSG1=((nf, nz, 8, 128), f32),
+        SMO=((experts + 8, 128), f32), GNO=((8, 128), f32), DWF=((shard, W), f32), SGW=((16, 128), f32), SG1=((2, 8, width), f32), SG1P=((8, width), f32), RSG1=((nf, nz, 8, 128), f32),
         EXB=((2, hb, width), bf16), EXG=((2, hb, width), f32),
     )
     slots = (96, 104)
@@ -1382,9 +1381,9 @@
         ),
         in_specs=[anywhere] * 2 + [vm] * 3 + [anywhere] + [vm] * 3 + [anywhere] * 3
         + [pl.BlockSpec(memory_space=pltpu.SMEM), vm, vm],
-        out_specs=(anywhere,) * 2 + (vm,) * 2 + (anywhere, vm) + (anywhere,) * 2,
+        out_specs=(anywhere,) * 8,
         scratch_shapes=[pltpu.VMEM(s, d) for s, d in scratch.values()]
-        + [pltpu.SemaphoreType.DMA((slots[0],)), pltpu.SemaphoreType.DMA((slots[1],)), pltpu.SemaphoreType.DMA((11,))],
+        + [pltpu.SemaphoreType.DMA((slots[0],)), pltpu.SemaphoreType.DMA((slots[1],)), pltpu.SemaphoreType.DMA((14,))],
         compiler_params=pltpu.CompilerParams(
             collective_id=0, has_side_effects=True, vmem_limit_bytes=67043328
         ),

time: 179 us -> 178 us (level)
  no operation moved by 1% of the time
where the time goes in v6:
time: 178 us; the launch traced here: 177 us
  Pallas kernels  177 us (99%)
    pallas_call x1, Pallas kernels, fast_local(): pl.pallas_call(functools.partial(layer_kernel, (nf, nz, hb, width, expert...  173 us
    pallas_call x1, Pallas kernels, fast_local(): pl.pallas_call(functools.partial(finish_kernel, (nz, experts, half_ff, sh...  3.75 us

profile of v6, /device:TPU:0, one launch (start us, length us, event | category | flops | bytes accessed | tf_op | source)
XLA Modules:
  0.0 177.3 jit_solution(8935849605118496634)
XLA Ops:
  0.6 172.8 %layer.1 = (bf16[2,64,1024]{2,1,0:T(8,128)(2,1)}, f32[2,64,1024]{2,1,0:T(8,128)}, f32[24,128]{1,0:T(8,128)}, f32[8,128]{1,0:T(8,128)}, bf16[4,64,256]{2,1,0:T(8,...) custom-call(bf16[128,1024]{1,0:T(8,128)(2,1)} %bitcast.20, ...), custom_call_target="tpu_custom_call" | custom-call | tf_op jit(solution)/shard_map/layer/pallas_call | solution.py:1374
  173.4 3.7 %finish.1 = (bf16[128,1024]{1,0:T(8,128)(2,1)}, f32[128,1024]{1,0:T(8,128)}, f32[1,64]{1,0:T(1,128)}, f32[64,512]{1,0:T(8,128)}, f32[64,256]{1,0:T(8,128)}, /*in...) custom-call(bf16[128,1024]{1,0:T(8,128)(2,1)} %bitcast.22, ...), custom_call_target="tpu_custom_call" | custom-call | tf_op jit(solution)/shard_map/finish/pallas_call | solution.py:1399

commit v7 on v6

--- a/solution.py
+++ b/solution.py
@@ -833,6 +833,8 @@
         copy.wait_recv()
     for k in (3, 2, 1):
         send_weights(k, 4)
+    for k in (3, 2, 1):
+        send_weights(k, 2, 3)
     sends_g3 = []
     for k in (1, 2):
         sends_g2[k - 1].wait_recv()
@@ -843,8 +845,6 @@
     sends_t2 = [net.send(GTB.at[f, c], GTB.at[f, c], across[k]) for k in (1, 2, 3)]
     forwards_n = [net.send(N2.at[f, c], N2.at[f, c], partner)]
     forwards_t = [net.send(GTB.at[f, c], GTB.at[f, c], partner)]
-    for k in (3, 2, 1):
-        send_weights(k, 2, 3)
     before = range(len(net.copies) - 20)
 
     WGU[:, z, :, 0:unit] = SWG[:, z, :, 0:unit]

time: 178 us -> 178 us (level)
  no operation moved by 1% of the time
where the time goes in v7:
time: 178 us; the launch traced here: 177 us
  Pallas kernels  177 us (99%)
    pallas_call x1, Pallas kernels, fast_local(): pl.pallas_call(functools.partial(layer_kernel, (nf, nz, hb, width, expert...  173 us
    pallas_call x1, Pallas kernels, fast_local(): pl.pallas_call(functools.partial(finish_kernel, (nz, experts, half_ff, sh...  3.75 us

profile of v7, /device:TPU:0, one launch (start us, length us, event | category | flops | bytes accessed | tf_op | source)
XLA Modules:
  0.0 177.3 jit_solution(3397381615278272952)
XLA Ops:
  0.6 172.8 %layer.1 = (bf16[2,64,1024]{2,1,0:T(8,128)(2,1)}, f32[2,64,1024]{2,1,0:T(8,128)}, f32[24,128]{1,0:T(8,128)}, f32[8,128]{1,0:T(8,128)}, bf16[4,64,256]{2,1,0:T(8,...) custom-call(bf16[128,1024]{1,0:T(8,128)(2,1)} %bitcast.20, ...), custom_call_target="tpu_custom_call" | custom-call | tf_op jit(solution)/shard_map/layer/pallas_call | solution.py:1374
  173.4 3.7 %finish.1 = (bf16[128,1024]{1,0:T(8,128)(2,1)}, f32[128,1024]{1,0:T(8,128)}, f32[1,64]{1,0:T(1,128)}, f32[64,512]{1,0:T(8,128)}, f32[64,256]{1,0:T(8,128)}, /*in...) custom-call(bf16[128,1024]{1,0:T(8,128)(2,1)} %bitcast.22, ...), custom_call_target="tpu_custom_call" | custom-call | tf_op jit(solution)/shard_map/finish/pallas_call | solution.py:1399
